TPU v7x, 128 devices: a whole 4x4x4 slice. The times are simulated.
128 devices in a mesh: dom: 128 (over x, z, y, core).
Axes of the slice: x: 4, y: 4, z: 4, core: 2. Of those that a mesh axis runs over, the one named last changes fastest.
Arguments:
- modal_dofs: float32 [35, 9, 32768], P(None, None, 'dom'), may hold values from -6 to 6
- jacobian: float32 [3, 32768], P(None, 'dom'), may hold values from 0.2 to 0.8
- face_area: float32 [4, 32768], P(None, 'dom'), may hold values from 0.1 to 0.4
- cluster_id: int32 [32768], P('dom'), may hold values from 0 to 1
- target_slot: int32 [32768], P('dom'), may hold values from 0 to 383, as said below
- ghost_slots: int32 [128, 8, 6], P('dom'), may hold values from 0 to 383
- face_neighbours: int32 [4, 49152], P(None, 'dom'), may hold values from 0 to 431, as said below
- stiffness: float32 [3, 35, 35], replicated, may hold values from -1 to 1
- star_matrix: float32 [3, 9, 9], replicated, may hold values from -2 to 2
- face_minus: float32 [4, 35, 35], replicated, may hold values from -1 to 1
- face_plus: float32 [4, 35, 35], replicated, may hold values from -1 to 1
- solver_minus: float32 [4, 9, 9], replicated, may hold values from -2 to 2
- solver_plus: float32 [4, 9, 9], replicated, may hold values from -2 to 2
Outputs:
- updated: float32 [35, 9, 32768], P(None, None, 'dom')
Inputs may be any that keep to these rules, and one draw needn't show every extreme that they name: `target_slot`: within the 256 elements of one block the values are distinct. One owner, the same for every block, receives 3 elements from every block. `face_neighbours`: values from 384 on address the ghost table of 48 entries.
All inputs are finite; a program needn't handle non-finite values.
Results may differ from a plain program's by a relative error of at most 0.0003.
Values sent between devices are 32-bit elements; how exact they have to be, the bound alone decides.
No kernel may reach another device: no remote copies, remote signals or barrier semaphores. Data moves between devices by JAX's collectives and lax.ppermute only.
A program may use at most 64 MiB of HBM per device.

v0:
```python
import math

import jax
import jax.numpy as jnp
from jax import lax
from jax.experimental import pallas as pl
from jax.experimental.pallas import tpu as pltpu
from jax.sharding import PartitionSpec as P

ORDER = 5
MODES = 35
QUANT = 9
FEAT = MODES * QUANT
ROWS = 320
BLOCK = 256
DEVS = 128
CAP = 3
SLOTS = 384
STRIDE = 336
CHUNK = 1024
GHOSTS = 6
NEIGH = 8
STEPS = (1, -1, 2, -2, 3, -3, 4, -4)
F32 = jnp.float32
BF16 = jnp.bfloat16
FULL = 67043328


def weights_of(lower, upper):
    return [(upper ** (k + 1) - lower ** (k + 1)) / math.factorial(k + 1) for k in range(ORDER)]


def dot(a, b):
    return jnp.dot(a, b, preferred_element_type=F32)


def split2(x):
    high = x.astype(BF16)
    return high, (x - high.astype(F32)).astype(BF16)


def split3(x):
    high = x.astype(BF16)
    rest = x - high.astype(F32)
    mid = rest.astype(BF16)
    return high, mid, (rest - mid.astype(F32)).astype(BF16)


def dot3(a, b, dims=None):
    total = None
    for part in split3(a):
        if dims is None:
            term = dot(part, b)
        else:
            term = lax.dot_general(part, b, (dims, ((), ())), preferred_element_type=F32)
        total = term if total is None else total + term
    return total


def product(a_high, a_low, b_high, b_low):
    return dot(a_high, b_high) + dot(a_low, b_high) + dot(a_high, b_low)


def iota(shape, dim):
    return lax.broadcasted_iota(jnp.int32, shape, dim)


def onehot(condition):
    return jnp.where(condition, 1.0, 0.0).astype(BF16)


def pack_rows(stage, out_ref):
    for k in range(8):
        out_ref[pl.ds(k, DEVS, stride=8), :] = stage[128 * k : 128 * k + 128, :].T


def unpack_rows(recv_ref, stage):
    for k in range(8):
        stage[128 * k : 128 * k + 128, :] = recv_ref[pl.ds(k, DEVS, stride=8), :].T


def scatter_kernel(modal, jac, area, cluster, target, out, cells, values, stage, kinds, places, done):
    copies = [
        pltpu.make_async_copy(modal, cells, done.at[0]),
        pltpu.make_async_copy(jac, values.at[0:3, :], done.at[1]),
        pltpu.make_async_copy(area, values.at[3:7, :], done.at[2]),
        pltpu.make_async_copy(cluster, kinds, done.at[3]),
        pltpu.make_async_copy(target, places, done.at[4]),
    ]
    for copy in copies:
        copy.start()
    for copy in copies:
        copy.wait()
    values[7:8, :] = 1.0 + kinds[...].astype(F32)
    values[320:328, :] = jnp.zeros((8, BLOCK), F32)
    for q in range(QUANT):
        values[8 + MODES * q : 8 + MODES * (q + 1), :] = cells[q]
    slot = iota((DEVS, BLOCK), 0) * CAP
    wanted = places[...]
    stage[CAP * STRIDE :, :] = jnp.zeros((CHUNK - CAP * STRIDE, DEVS), F32)
    parts = split3(values[...])
    for t in range(CAP):
        hot = onehot(slot + t == wanted)
        total = None
        for part in parts:
            term = lax.dot_general(part, hot, (((1,), (1,)), ((), ())), preferred_element_type=F32)
            total = term if total is None else total + term
        stage[STRIDE * t : STRIDE * t + 328, :] = total
        stage[STRIDE * t + 328 : STRIDE * (t + 1), :] = jnp.zeros((8, DEVS), F32)
    pack_rows(stage, out)


def gather_kernel(recv, target, out, stage):
    unpack_rows(recv, stage)
    wanted = target[...]
    slot = iota((DEVS, BLOCK), 0) * CAP
    total = None
    for t in range(CAP):
        part = stage[STRIDE * t + 8 : STRIDE * t + 8 + ROWS, :]
        term = dot3(part, onehot(slot + t == wanted))
        total = term if total is None else total + term
    for q in range(QUANT):
        out[q] = total[MODES * q : MODES * (q + 1), :]


def expand_family(mode_in, flux_in, first, count, sign, high, low, at, stage):
    width = count * ROWS
    col = iota((8, width), 1)
    op = jnp.zeros_like(col)
    for c in range(1, count):
        op = op + jnp.where(col >= c * ROWS, 1, 0)
    inner = col - op * ROWS
    quant = (inner * 1873) >> 16
    mode = inner - quant * MODES
    valid = inner < FEAT
    mode_code = jnp.where(valid, op * 128 + mode, -1)[0:1]
    quant_code = jnp.where(valid, op * 128 + quant, -1)[0:1]
    row = iota((count * 128, width), 0)
    modes = jnp.concatenate([mode_in[first + c] for c in range(count)], axis=1)
    fluxes = jnp.concatenate([flux_in[first + c] for c in range(count)], axis=1)
    spread = dot3(modes, onehot(row == mode_code)) * sign
    scale = dot3(fluxes, onehot(row == quant_code))
    for p in range(QUANT):
        stage[MODES * p : MODES * (p + 1), 0:width] = spread[0:MODES, :] * scale[p : p + 1, :]
    stage[FEAT:ROWS, 0:width] = jnp.zeros((ROWS - FEAT, width), F32)
    a_high, a_low = split2(stage[:, 0:width])
    high[:, at : at + width] = a_high
    low[:, at : at + width] = a_low


def operator_kernel(mode_in, flux_in, faces, d_high, d_low, c_high, c_low, b_high, b_low, order,
    stage, dh, dl, bh, bl, ch, cl, moved, done,
):
    expand_family(mode_in, flux_in, 0, 3, -1.0, dh, dl, 0, stage)
    copies = fetch([(dh, d_high), (dl, d_low)], done)
    expand_family(mode_in, flux_in, 10, 4, -1.0, bh, bl, 0, stage)
    copies += fetch([(bh, b_high), (bl, b_low)], done, 2)
    expand_family(mode_in, flux_in, 3, 3, 1.0, ch, cl, 0, stage)
    expand_family(mode_in, flux_in, 6, 4, -1.0, ch, cl, 3 * ROWS, stage)
    copies += fetch([(ch, c_high), (cl, c_low)], done, 4)
    value = faces[...]
    digits = jnp.concatenate([value >> 4, value & 15], axis=0).astype(F32).astype(BF16)
    row = iota((SLOTS, SLOTS), 0)
    col = iota((SLOTS, SLOTS), 1)
    swapped = dot(digits, onehot(row == (col & 127) * CAP + (col >> 7))).astype(jnp.int32)
    moved[...] = swapped[0:4, :] * 16 + swapped[4:8, :]
    copies += fetch([(moved, order)], done, 6)
    for copy in copies:
        copy.wait()


def taylor(start, extras, d_high, d_low, x_high, x_low, factor_sets):
    sums = [start * factors[0] for factors in factor_sets]
    current = start
    for k in range(1, ORDER):
        for c in range(3):
            high, low = split2(current * extras[c : c + 1, :])
            x_high[ROWS * c : ROWS * (c + 1), :] = high
            x_low[ROWS * c : ROWS * (c + 1), :] = low
        current = product(d_high[...], d_low[...], x_high[...], x_low[...])
        sums = [s + current * factors[k] for s, factors in zip(sums, factor_sets)]
    return sums


def send_ghosts(value, picks, owner, out):
    out[...] = jnp.zeros(out.shape, F32)
    slot = iota((SLOTS, 128), 0)
    slot = (slot & 127) * CAP + (slot >> 7)
    base = onehot(slot == picks[0:1, :])
    rest = jnp.concatenate([onehot(slot == picks[k : k + 1, :]) for k in range(1, 5)], axis=1)
    main = dot3(value[0:256, :], base)
    tail = dot3(value[256:320, :], rest)
    first = (main[0:128, :] + jnp.concatenate([tail[:, 0:128], tail[:, 128:256]], axis=0)).T
    second = (main[128:256, :] + jnp.concatenate([tail[:, 256:384], tail[:, 384:512]], axis=0)).T
    spot = owner & 7
    for b, step in enumerate(STEPS):
        goal = spot + step
        outside = jnp.where((goal < 0) | (goal > 7), 16, 0)
        place = ((goal + 8) & 7) * 32 + outside
        out[pl.ds(pl.multiple_of(place, 16), 8), :] = first[8 * b : 8 * b + 8, :]
        out[pl.ds(pl.multiple_of(place + 8, 8), 8), :] = second[8 * b : 8 * b + 8, :]


def read_ghosts(near, above, below, owner):
    firsts, seconds = [], []
    spot = owner & 7
    for step in STEPS:
        origin = spot - step
        inside = (origin >= 0) & (origin <= 7)
        place = pl.multiple_of(((origin + 8) & 7) * 32, 32)
        far = pl.multiple_of((origin & 3) * 16, 16)
        other = above if step > 0 else below
        firsts.append(jnp.where(inside, near[pl.ds(place, 8), :], other[pl.ds(far, 8), :]))
        seconds.append(jnp.where(inside, near[pl.ds(place + 8, 8), :], other[pl.ds(far + 8, 8), :]))
    blank = jnp.zeros((64, 128), F32)
    first = jnp.concatenate(firsts + [blank], axis=0).T
    second = jnp.concatenate(seconds + [blank], axis=0).T
    row = iota((128, 128), 0)
    col = iota((128, 128), 1)
    part = col & 7
    group = col - part
    halves = [first[0:64, :], first[64:128, :], second[0:64, :], second[64:128, :]]
    places = [((0, 6), (2, 7)), ((1, 6), (3, 7)), ((4, 6),), ((5, 6),)]
    tail = None
    for half, moves in zip(halves, places):
        hit = None
        for ghost, spot in moves:
            one = (part == ghost) & (row == group + spot)
            hit = one if hit is None else hit | one
        term = dot3(half, onehot(hit))
        tail = term if tail is None else tail + term
    return jnp.concatenate([first, second, tail], axis=0)


def remote_flux(value, ghosts, extras, faces, b_high, b_low, y_high, y_low, copies):
    high, low = split2(jnp.concatenate([value, ghosts], axis=1))
    row = iota((512, 128), 0)
    beyond = row - SLOTS
    local = (row & 127) * CAP + (row >> 7)
    spot = beyond & 7
    ghost = jnp.where((spot < GHOSTS) & (beyond < 64), SLOTS + (beyond >> 3) * GHOSTS + spot, -1)
    code = jnp.where(row < SLOTS, local, ghost)
    for f in range(4):
        hot = jnp.concatenate(
            [onehot(code == faces[f : f + 1, 128 * k : 128 * (k + 1)]) for k in range(3)], axis=1
        )
        picked = (dot(high, hot) + dot(low, hot)) * extras[3 + f : 4 + f, :]
        p_high, p_low = split2(picked)
        y_high[ROWS * f : ROWS * (f + 1), :] = p_high
        y_low[ROWS * f : ROWS * (f + 1), :] = p_low
    for copy in copies:
        copy.wait()
    return product(b_high[...], b_low[...], y_high[...], y_low[...])


def fetch(pairs, done, base=0):
    copies = [pltpu.make_async_copy(src, dst, done.at[base + k]) for k, (src, dst) in enumerate(pairs)]
    for copy in copies:
        copy.start()
    return copies


def occupied(extras):
    return jnp.where(extras[7:8, :] > 0.5, 1.0, 0.0)


def start_kernel(owner, recv, picks, d_high, d_low, state, extras, first, later, ghosts, stage, dh, dl, x_high, x_low, done):
    copies = fetch([(d_high, dh), (d_low, dl)], done)
    unpack_rows(recv, stage)
    for t in range(CAP):
        extras[:, 128 * t : 128 * (t + 1)] = stage[STRIDE * t : STRIDE * t + 8, :]
        state[:, 128 * t : 128 * (t + 1)] = stage[STRIDE * t + 8 : STRIDE * t + 8 + ROWS, :]
    for copy in copies:
        copy.wait()
    one, two = taylor(
        state[...], extras, dh, dl, x_high, x_low, [weights_of(0.0, 1.0), weights_of(1.0, 2.0)]
    )
    first[...] = one
    later[...] = two
    send_ghosts(first, picks, owner[0], ghosts)


def local_kernel(state, value, extras, c_high, c_low, out, z_high, z_low):
    for k in range(7):
        high, low = split2(value[...] * extras[k : k + 1, :])
        z_high[ROWS * k : ROWS * (k + 1), :] = high
        z_low[ROWS * k : ROWS * (k + 1), :] = low
    change = product(c_high[...], c_low[...], z_high[...], z_low[...])
    out[...] = state[...] + occupied(extras) * change


def middle_kernel(
    owner, near, above, below, partial, first, later, extras, faces, picks, d_high, d_low, b_high, b_low,
    middle, second, ghosts, dh, dl, bh, bl, x_high, x_low, y_high, y_low, done,
):
    copies = fetch([(b_high, bh), (b_low, bl), (d_high, dh), (d_low, dl)], done)
    table = read_ghosts(near, above, below, owner[0])
    flux = remote_flux(first[...], table, extras, faces, bh, bl, y_high, y_low, copies[0:2])
    for copy in copies[2:4]:
        copy.wait()
    middle[...] = partial[...] + occupied(extras) * flux
    (fresh,) = taylor(middle[...], extras, dh, dl, x_high, x_low, [weights_of(0.0, 1.0)])
    second[...] = jnp.where(extras[7:8, :] > 1.5, later[...], fresh)
    send_ghosts(second, picks, owner[0], ghosts)


def final_kernel(
    owner, near, above, below, partial, second, extras, faces, b_high, b_low, out, stage, bh, bl, y_high, y_low, done
):
    copies = fetch([(b_high, bh), (b_low, bl)], done)
    table = read_ghosts(near, above, below, owner[0])
    flux = remote_flux(second[...], table, extras, faces, bh, bl, y_high, y_low, copies)
    final = partial[...] + occupied(extras) * flux
    stage[...] = jnp.zeros((CHUNK, DEVS), F32)
    for t in range(CAP):
        stage[STRIDE * t + 8 : STRIDE * t + 8 + ROWS, :] = final[:, 128 * t : 128 * (t + 1)]
    pack_rows(stage, out)


def shape(*dims, dtype=F32):
    return jax.ShapeDtypeStruct(dims, dtype)


def call(kernel, name, outs, scratch, flops, operands, spaces="", out_spaces="", limit=16 * 1024 * 1024):
    kinds = {"s": pltpu.SMEM, "v": pltpu.VMEM, "h": pltpu.HBM}
    spaces = spaces.ljust(len(operands), "v")
    flat = jax.tree.leaves(outs)
    out_specs = [pl.BlockSpec(memory_space=kinds[k]) for k in out_spaces.ljust(len(flat), "v")]
    moved = sum(math.prod(o.shape) * 4 for o in operands)
    return pl.pallas_call(
        kernel,
        name=name,
        out_shape=outs,
        in_specs=[pl.BlockSpec(memory_space=kinds[k]) for k in spaces],
        out_specs=out_specs if isinstance(outs, list) else out_specs[0],
        scratch_shapes=scratch,
        cost_estimate=pl.CostEstimate(flops=flops, bytes_accessed=moved, transcendentals=0),
        compiler_params=pltpu.CompilerParams(vmem_limit_bytes=limit),
    )(*operands)


def vmem(*dims, dtype=F32):
    return pltpu.VMEM(dims, dtype)


def exchange(rows, per):
    cube = rows.reshape(DEVS, per, 128)
    return lax.all_to_all(cube, "dom", split_axis=0, concat_axis=0, tiled=True).reshape(DEVS * per, 128)


def swap_ghosts(rows):
    groups = [list(range(8 * k, 8 * k + 8)) for k in range(DEVS // 8)]
    cube = rows.reshape(8, 32, 128)
    near = lax.all_to_all(cube, "dom", split_axis=0, concat_axis=0, axis_index_groups=groups, tiled=True)
    up = [(i, (i + 8) % DEVS) for i in range(DEVS)]
    down = [((i + 8) % DEVS, i) for i in range(DEVS)]
    above = lax.ppermute(near[4:8, 16:32].reshape(64, 128), "dom", up)
    below = lax.ppermute(near[0:4, 16:32].reshape(64, 128), "dom", down)
    return near.reshape(256, 128), above, below


def local(
    modal_dofs, jacobian, face_area, cluster_id, target_slot, ghost_slots, face_neighbours,
    stiffness, star_matrix, face_minus, face_plus, solver_minus, solver_plus,
):
    owner = lax.axis_index("dom").astype(jnp.int32).reshape(1)
    target = target_slot.reshape(1, BLOCK)
    sent = call(
        scatter_kernel, "scatter", shape(CHUNK, DEVS),
        [
            vmem(QUANT, MODES, BLOCK), vmem(328, BLOCK), vmem(CHUNK, DEVS),
            vmem(1, BLOCK, dtype=jnp.int32), vmem(1, BLOCK, dtype=jnp.int32), pltpu.SemaphoreType.DMA((5,)),
        ],
        10**8,
        (jnp.transpose(modal_dofs, (1, 0, 2)), jacobian, face_area, cluster_id.reshape(1, BLOCK), target),
        "hhhhh", "", FULL,
    )
    received = exchange(sent, 8)

    modes = jnp.concatenate([jnp.transpose(stiffness, (0, 2, 1)), stiffness, face_minus, face_plus], axis=0)
    fluxes = jnp.concatenate([star_matrix, star_matrix, solver_minus, solver_plus], axis=0)
    modes = jnp.pad(modes, ((0, 0), (0, 48 - MODES), (0, 128 - MODES)))
    fluxes = jnp.pad(jnp.transpose(fluxes, (0, 2, 1)), ((0, 0), (0, 16 - QUANT), (0, 128 - QUANT)))
    sizes = [3 * ROWS, 7 * ROWS, 4 * ROWS]
    d_high, d_low, c_high, c_low, b_high, b_low, faces = call(
        operator_kernel, "operators",
        [shape(ROWS, s, dtype=BF16) for s in sizes for _ in range(2)] + [shape(4, SLOTS, dtype=jnp.int32)],
        [vmem(ROWS, 4 * ROWS)]
        + [vmem(ROWS, k * ROWS, dtype=BF16) for k in (3, 3, 4, 4, 7, 7)]
        + [vmem(4, SLOTS, dtype=jnp.int32), pltpu.SemaphoreType.DMA((7,))],
        10**9, (modes, fluxes, face_neighbours), "", "hhhhhhh", FULL,
    )
    wanted = ghost_slots[0]
    none = jnp.full((NEIGH, 1), -1, jnp.int32)
    wide = jnp.full((NEIGH, 6), -1, jnp.int32)

    def lanes(*columns):
        table = jnp.concatenate(columns, axis=1).reshape(1, 64)
        return jnp.concatenate([table, jnp.full((1, 64), -1, jnp.int32)], axis=1)

    picks = jnp.concatenate(
        [
            lanes(wanted, none, none),
            lanes(wide, wanted[:, 0:1], wanted[:, 2:3]),
            lanes(wide, wanted[:, 1:2], wanted[:, 3:4]),
            lanes(wide, wanted[:, 4:5], none),
            lanes(wide, wanted[:, 5:6], none),
            jnp.full((3, 128), -1, jnp.int32),
        ],
        axis=0,
    )
    d_scratch = [vmem(ROWS, 3 * ROWS, dtype=BF16)] * 2
    b_scratch = [vmem(ROWS, 4 * ROWS, dtype=BF16)] * 2
    x_scratch = [vmem(3 * ROWS, SLOTS, dtype=BF16)] * 2
    y_scratch = [vmem(4 * ROWS, SLOTS, dtype=BF16)] * 2
    z_scratch = [vmem(7 * ROWS, SLOTS, dtype=BF16)] * 2
    field = shape(ROWS, SLOTS)
    halo = shape(8 * 32, 128)
    state, extras, first, later, out1 = call(
        start_kernel, "start", [field, shape(8, SLOTS), field, field, halo],
        [vmem(CHUNK, DEVS)] + d_scratch + x_scratch + [pltpu.SemaphoreType.DMA((2,))], 10**9,
        (owner, received, picks, d_high, d_low), "svvhh",
    )
    near, above, below = swap_ghosts(out1)
    first, _ = lax.optimization_barrier((first, near))
    partial1 = call(
        local_kernel, "local1", field, z_scratch, 10**9, (state, first, extras, c_high, c_low)
    )
    middle, second, out2 = call(
        middle_kernel, "middle", [field, field, halo],
        d_scratch + b_scratch + x_scratch + y_scratch + [pltpu.SemaphoreType.DMA((4,))], 2 * 10**9,
        (owner, near, above, below, partial1, first, later, extras, faces, picks, d_high, d_low, b_high, b_low),
        "svvvvvvvvvhhhh",
    )
    near, above, below = swap_ghosts(out2)
    second, _ = lax.optimization_barrier((second, near))
    partial2 = call(
        local_kernel, "local2", field, z_scratch, 10**9, (middle, second, extras, c_high, c_low)
    )
    back = call(
        final_kernel, "final", shape(CHUNK, DEVS),
        [vmem(CHUNK, DEVS)] + b_scratch + y_scratch + [pltpu.SemaphoreType.DMA((2,))], 10**9,
        (owner, near, above, below, partial2, second, extras, faces, b_high, b_low), "svvvvvvvhh",
    )
    returned = exchange(back, 8)
    result = call(
        gather_kernel, "gather", shape(QUANT, MODES, BLOCK), [vmem(CHUNK, DEVS)], 10**8, (returned, target)
    )
    return jnp.transpose(result, (1, 0, 2))


def solution(mesh):
    placed = (
        P(None, None, "dom"), P(None, "dom"), P(None, "dom"), P("dom"), P("dom"), P("dom", None, None),
        P(None, "dom"), P(), P(), P(), P(), P(), P(),
    )
    return jax.shard_map(
        local, mesh=mesh, in_specs=placed, out_specs=P(None, None, "dom"), check_vma=False
    )
```

profile of v0, /device:TPU:1, one launch (start us, length us, event | category | flops | bytes accessed | tf_op | source)
XLA Modules:
  0.0 109.6 jit_solution(772243881282730189)
XLA Ops:
  0.0 2.5 %scatter.1 = f32[1024,128]{1,0:T(8,128)} custom-call(f32[9,35,256]{2,1,0:T(8,128)} %bitcast.31, f32[3,256]{1,0:T(4,128)} %jac.1, f32[4,256]{1,0:T(4,128)} %area.1, s32[1,256]{1,0:T(1,128)} %bitcast.39, s32[1,256]{1,0:T(1,128)} %bitcast.28), custom_call_target="tpu_custom_call" | custom-call | flops 100000000 | bytes 331776 | tf_op jit(solution)/shard_map/scatter/pallas_call | solution.py:330
  2.6 0.0 copy-start.11
  2.6 0.0 copy-start.12
  2.6 0.0 copy-start.10
  2.6 11.9 %all-to-all-start = ((f32[128,8,128]{2,1,0:T(8,128)}), f32[128,8,128]{2,1,0:T(8,128)}, u32[]{:S(2)}, u32[]{:S(2)}) async-start(f32[128,8,128]{2,1,0:T(8,128)} %bitcast.30), calls=%async_computation | async-start | bytes 1048576 | tf_op jit(solution)/shard_map/all_to_all | solution.py:348
  14.6 0.8 copy.14
  15.3 0.1 fusion.2
  15.4 0.1 pad.29.clone
  15.5 0.1 reshape.65
  15.6 0.1 add_add_fusion.1
  15.6 0.1 reshape.69
  15.7 0.1 reshape.68
  15.8 0.1 reshape.67
  15.9 0.1 reshape.66
  16.0 0.8 copy.18
  16.8 0.8 copy.20
  17.7 0.8 copy.21
  18.5 0.9 copy.15
  19.4 0.0 copy-done.11
  19.4 0.0 copy-done.12
  19.5 0.7 pad.15.flux_in
  20.1 0.6 concatenate.49.picks
  20.8 0.0 copy-done.10
  20.8 0.8 select_maximum_fusion.mode_in
  21.5 7.8 %operators.1 = (bf16[320,960]{1,0:T(8,128)(2,1)}, bf16[320,960]{1,0:T(8,128)(2,1)}, bf16[320,2240]{1,0:T(8,128)(2,1)}, bf16[320,2240]{1,0:T(8,128)(2,1)}, bf16[3...) custom-call(f32[14,48,128]{2,1,0:T(8,128)} %select_maximum_fusion.mode_in, ...), custom_call_target="tpu_custom_call" | custom-call | flops 1000000000 | bytes 464896 | tf_op jit(solution)/shard_map/operators/pallas_call | solution.py:330
  29.4 0.0 all-to-all-done
  29.4 0.0 copy-start.2
  29.4 0.7 copy-done.2
  30.1 0.0 copy-start.7
  30.1 1.1 copy-done.7
  31.2 0.0 copy-start.8
  31.2 1.1 copy-done.8
  32.3 0.0 copy-start
  32.3 0.0 copy-start.1
  32.3 7.6 %start.1 = (f32[320,384]{1,0:T(8,128)S(1)}, f32[8,384]{1,0:T(8,128)S(1)}, f32[320,384]{1,0:T(8,128)S(1)}, f32[320,384]{1,0:T(8,128)S(1)}, f32[256,128]{1,0:T(8,128)S(1)}) custom-call(s32[1]{0:T(128)} %bitcast.owner, f32[1024,128]{1,0:T(8,128)} %bitcast.5.recv, s32[8,128]{1,0:T(8,128)S(1)} %copy-done.2, bf16[320,960]{1,0:T(8,128)(2,1)S(1)} %copy-done.7, ...), custom_call_target="tpu_custom_call" | custom-call | flops 1000000000 | bytes 2985988 | tf_op jit(solution)/shard_map/start/pallas_call | solution.py:330
  39.8 9.8 %all_to_all.20 = f32[8,32,128]{2,1,0:T(8,128)S(1)} all-to-all(f32[8,32,128]{2,1,0:T(8,128)S(1)} %bitcast.27), channel_id=1, replica_groups={{0,1,2,3,4,5,6,7},{8,9,10,11,12,13,14,15},{16,17,18,19,20,21,22,23},{24..., dimensions={0} | all-to-all | bytes 262144 | tf_op jit(solution)/shard_map/all_to_all | solution.py:354
  49.7 1.4 %collective-permute-start = (f32[64,128]{1,0:T(8,128)S(1)}, f32[64,128]{1,0:T(8,128)S(1)}, u32[]{:S(2)}, u32[]{:S(2)}) collective-permute-start(f32[64,128]{1,0:T(8,128)S(1)} %bitcast.38), channel_id=1, source_target_pairs={{0,8},{1,9},{2,10},{3,11},{4,12},{5,13},{6,14},{7,15},{8,16},{9,17... | collective-permute-start | bytes 98312 | tf_op jit(solution)/shard_map/ppermute | solution.py:357
  51.1 4.2 %collective-permute-start.1 = (f32[64,128]{1,0:T(8,128)S(1)}, f32[64,128]{1,0:T(8,128)S(1)}, u32[]{:S(2)}, u32[]{:S(2)}) collective-permute-start(f32[64,128]{1,0:T(8,128)S(1)} %bitcast.36), channel_id=1, source_target_pairs={{8,0},{9,1},{10,2},{11,3},{12,4},{13,5},{14,6},{15,7},{16,8},{17,9... | collective-permute-start | bytes 98312 | tf_op jit(solution)/shard_map/ppermute | solution.py:358
  55.3 0.0 copy-done
  55.3 0.0 copy-done.1
  55.3 0.0 copy-start.3
  55.3 0.0 copy-start.5
  55.3 0.0 copy-start.6
  55.3 0.0 copy-start.9
  55.3 2.6 %local1.1.partial = f32[320,384]{1,0:T(8,128)S(1)} custom-call(f32[320,384]{1,0:T(8,128)S(1)} %get-tuple-element.25.state, f32[320,384]{1,0:T(8,128)S(1)} %get-tuple-element.27.value.first, f32[8,384]{1,0:T(8,128)S(1)} %get-tuple-element.28.extras, bf16[320,2240]{1,0:T(8,128)(2,1)S(1)} %copy-done, bf16[320,2240]{1,0:T(8,128)(2,1)S(1)} %copy-done.1), custom_call_target="tpu_custom_call" | custom-call | flops 1000000000 | bytes 6729728 | tf_op jit(solution)/shard_map/local1/pallas_call | solution.py:330
  57.9 0.0 collective-permute-done.above
  57.9 0.0 collective-permute-done.1.below
  57.9 0.0 copy-done.3
  57.9 0.0 copy-done.5
  57.9 0.0 copy-done.6
  57.9 0.0 copy-done.9
  58.0 9.6 %middle.1 = (f32[320,384]{1,0:T(8,128)S(1)}, f32[320,384]{1,0:T(8,128)S(1)}, f32[256,128]{1,0:T(8,128)S(1)}) custom-call(s32[1]{0:T(128)} %bitcast.owner, f32[256,128]{1,0:T(8,128)S(1)} %bitcast.24, f32[64,128]{1,0:T(8,128)S(1)} %collective-permute-done.above, f32[64,128]{1,0:T(8,128)S(1)} %collective-permute-done.1.below, f32[320,384]{1,0:T(8,128)S(1)} %local1.1.partial, ...), custom_call_target="tpu_custom_call" | custom-call | flops 2000000000 | bytes 7428100 | tf_op jit(solution)/shard_map/middle/pallas_call | solution.py:330
  67.6 8.8 %all_to_all.21 = f32[8,32,128]{2,1,0:T(8,128)S(1)} all-to-all(f32[8,32,128]{2,1,0:T(8,128)S(1)} %bitcast.26), channel_id=1, replica_groups={{0,1,2,3,4,5,6,7},{8,9,10,11,12,13,14,15},{16,17,18,19,20,21,22,23},{24..., dimensions={0} | all-to-all | bytes 262144 | tf_op jit(solution)/shard_map/all_to_all | solution.py:354
  76.4 0.0 collective-permute-start.2
  76.4 4.8 %collective-permute-start.3 = (f32[64,128]{1,0:T(8,128)S(1)}, f32[64,128]{1,0:T(8,128)S(1)}, u32[]{:S(2)}, u32[]{:S(2)}) collective-permute-start(f32[64,128]{1,0:T(8,128)S(1)} %bitcast.35), channel_id=1, source_target_pairs={{8,0},{9,1},{10,2},{11,3},{12,4},{13,5},{14,6},{15,7},{16,8},{17,9... | collective-permute-start | bytes 98312 | tf_op jit(solution)/shard_map/ppermute | solution.py:358
  81.2 2.6 %local2.1.partial = f32[320,384]{1,0:T(8,128)S(1)} custom-call(f32[320,384]{1,0:T(8,128)S(1)} %get-tuple-element.36.state, f32[320,384]{1,0:T(8,128)S(1)} %get-tuple-element.38.value.second, f32[8,384]{1,0:T(8,128)S(1)} %get-tuple-element.28.extras, bf16[320,2240]{1,0:T(8,128)(2,1)S(1)} %copy-done, bf16[320,2240]{1,0:T(8,128)(2,1)S(1)} %copy-done.1), custom_call_target="tpu_custom_call" | custom-call | flops 1000000000 | bytes 6729728 | tf_op jit(solution)/shard_map/local2/pallas_call | solution.py:330
  83.7 0.0 copy-start.4
  83.7 0.0 collective-permute-done.2.above
  83.8 0.0 collective-permute-done.3.below
  83.8 3.6 %final.1 = f32[1024,128]{1,0:T(8,128)S(1)} custom-call(s32[1]{0:T(128)} %bitcast.owner, f32[256,128]{1,0:T(8,128)S(1)} %bitcast.25, f32[64,128]{1,0:T(8,128)S(1)} %collective-permute-done.2.above, f32[64,128]{1,0:T(8,128)S(1)} %collective-permute-done.3.below, f32[320,384]{1,0:T(8,128)S(1)} %local2.1.partial, f32[320,384]{1,0:T(8,128)S(1)} %get-tuple-element.38.value.second, ...), custom_call_target="tpu_custom_call" | custom-call | flops 1000000000 | bytes 4474884 | tf_op jit(solution)/shard_map/final/pallas_call | solution.py:330
  87.4 20.8 %all_to_all.22 = f32[128,8,128]{2,1,0:T(8,128)S(1)} all-to-all(f32[128,8,128]{2,1,0:T(8,128)S(1)} %bitcast.23), channel_id=1, replica_groups=mesh['dom'=128] {'dom'}, dimensions={0} | all-to-all | bytes 1048576 | tf_op jit(solution)/shard_map/all_to_all | solution.py:348
  108.2 0.0 copy-done.4
  108.2 1.3 %gather.1 = f32[9,35,256]{2,1,0:T(8,128)} custom-call(f32[1024,128]{1,0:T(8,128)S(1)} %bitcast.22, s32[1,256]{1,0:T(1,128)S(1)} %bitcast.29), custom_call_target="tpu_custom_call" | custom-call | flops 100000000 | bytes 525312 | tf_op jit(solution)/shard_map/gather/pallas_call | solution.py:330
  (14 shorter events, 0.1 us)
Async XLA Ops:
  2.6 16.9 %copy-start.11 = (f32[4,35,35]{2,0,1:T(4,128)S(1)}, f32[4,35,35]{2,0,1:T(4,128)}, u32[]{:S(2)}) copy-start(f32[4,35,35]{2,0,1:T(4,128)} %param.22) | copy-start | bytes 58804
  2.6 16.9 %copy-start.12 = (f32[4,35,35]{2,0,1:T(4,128)S(1)}, f32[4,35,35]{2,0,1:T(4,128)}, u32[]{:S(2)}) copy-start(f32[4,35,35]{2,0,1:T(4,128)} %param.23) | copy-start | bytes 58804
  2.6 18.2 %copy-start.10 = (f32[3,35,35]{2,1,0:T(8,128)S(1)}, f32[3,35,35]{2,1,0:T(8,128)}, u32[]{:S(2)}) copy-start(f32[3,35,35]{2,1,0:T(8,128)} %param.20) | copy-start | bytes 44104
  2.6 26.8 %all-to-all-start = ((f32[128,8,128]{2,1,0:T(8,128)}), f32[128,8,128]{2,1,0:T(8,128)}, u32[]{:S(2)}, u32[]{:S(2)}) async-start(f32[128,8,128]{2,1,0:T(8,128)} %bitcast.30), calls=%async_computation | async-start | bytes 1048576 | tf_op jit(solution)/shard_map/all_to_all | solution.py:348
  29.4 0.7 copy-start.2
  30.1 1.1 copy-start.7
  31.2 1.1 copy-start.8
  32.3 23.0 %copy-start = (bf16[320,2240]{1,0:T(8,128)(2,1)S(1)}, bf16[320,2240]{1,0:T(8,128)(2,1)}, u32[]{:S(2)}) copy-start(bf16[320,2240]{1,0:T(8,128)(2,1)} %get-tuple-element.29.c_high) | copy-start | bytes 4300804
  32.3 23.0 %copy-start.1 = (bf16[320,2240]{1,0:T(8,128)(2,1)S(1)}, bf16[320,2240]{1,0:T(8,128)(2,1)}, u32[]{:S(2)}) copy-start(bf16[320,2240]{1,0:T(8,128)(2,1)} %get-tuple-element.30.c_low) | copy-start | bytes 4300804
  49.7 8.2 %collective-permute-start = (f32[64,128]{1,0:T(8,128)S(1)}, f32[64,128]{1,0:T(8,128)S(1)}, u32[]{:S(2)}, u32[]{:S(2)}) collective-permute-start(f32[64,128]{1,0:T(8,128)S(1)} %bitcast.38), channel_id=1, source_target_pairs={{0,8},{1,9},{2,10},{3,11},{4,12},{5,13},{6,14},{7,15},{8,16},{9,17... | collective-permute-start | bytes 98312 | tf_op jit(solution)/shard_map/ppermute | solution.py:357
  51.1 6.8 %collective-permute-start.1 = (f32[64,128]{1,0:T(8,128)S(1)}, f32[64,128]{1,0:T(8,128)S(1)}, u32[]{:S(2)}, u32[]{:S(2)}) collective-permute-start(f32[64,128]{1,0:T(8,128)S(1)} %bitcast.36), channel_id=1, source_target_pairs={{8,0},{9,1},{10,2},{11,3},{12,4},{13,5},{14,6},{15,7},{16,8},{17,9... | collective-permute-start | bytes 98312 | tf_op jit(solution)/shard_map/ppermute | solution.py:358
  55.3 2.6 %copy-start.3 = (s32[8,128]{1,0:T(8,128)S(1)}, s32[8,128]{1,0:T(8,128)}, u32[]{:S(2)}) copy-start(s32[8,128]{1,0:T(8,128)} %concatenate.49.picks) | copy-start | bytes 12292
  55.3 2.6 %copy-start.5 = (bf16[320,1280]{1,0:T(8,128)(2,1)S(1)}, bf16[320,1280]{1,0:T(8,128)(2,1)}, u32[]{:S(2)}) copy-start(bf16[320,1280]{1,0:T(8,128)(2,1)} %get-tuple-element.33.b_high) | copy-start | bytes 2457604
  55.3 2.6 %copy-start.6 = (bf16[320,1280]{1,0:T(8,128)(2,1)S(1)}, bf16[320,1280]{1,0:T(8,128)(2,1)}, u32[]{:S(2)}) copy-start(bf16[320,1280]{1,0:T(8,128)(2,1)} %get-tuple-element.34.b_low) | copy-start | bytes 2457604
  55.3 2.6 %copy-start.9 = (s32[4,384]{1,0:T(4,128)S(1)}, s32[4,384]{1,0:T(4,128)}, u32[]{:S(2)}) copy-start(s32[4,384]{1,0:T(4,128)} %get-tuple-element.32.faces) | copy-start | bytes 18436
  76.4 7.4 %collective-permute-start.2 = (f32[64,128]{1,0:T(8,128)S(1)}, f32[64,128]{1,0:T(8,128)S(1)}, u32[]{:S(2)}, u32[]{:S(2)}) collective-permute-start(f32[64,128]{1,0:T(8,128)S(1)} %bitcast.37), channel_id=1, source_target_pairs={{0,8},{1,9},{2,10},{3,11},{4,12},{5,13},{6,14},{7,15},{8,16},{9,17... | collective-permute-start | bytes 98312 | tf_op jit(solution)/shard_map/ppermute | solution.py:357
  76.4 7.4 %collective-permute-start.3 = (f32[64,128]{1,0:T(8,128)S(1)}, f32[64,128]{1,0:T(8,128)S(1)}, u32[]{:S(2)}, u32[]{:S(2)}) collective-permute-start(f32[64,128]{1,0:T(8,128)S(1)} %bitcast.35), channel_id=1, source_target_pairs={{8,0},{9,1},{10,2},{11,3},{12,4},{13,5},{14,6},{15,7},{16,8},{17,9... | collective-permute-start | bytes 98312 | tf_op jit(solution)/shard_map/ppermute | solution.py:358
  83.7 24.5 %copy-start.4 = (s32[256]{0:T(256)S(1)}, s32[256]{0:T(256)}, u32[]{:S(2)}) copy-start(s32[256]{0:T(256)} %param.17) | copy-start | bytes 3076
where the time goes:
time: 110 us
  blocking collectives  39.4 us (36%)
  Pallas kernels  37.7 us (34%)
  starting transfers between devices  22.3 us (20%)
  local copies, waits for them, and re-layouts  8.96 us (8%)
    pallas_call x8, Pallas kernels, call(): pl.pallas_call(kernel, name=name, out_shape=outs, in_specs=[pl.BlockSpec(...  37.7 us
    all_to_all x1, blocking collectives, exchange(): lax.all_to_all(cube, 'dom', split_axis=0, concat_axis=0, tiled=True)  20.8 us
    all_to_all x2, blocking collectives, swap_ghosts(): lax.all_to_all(cube, 'dom', split_axis=0, concat_axis=0, axis_index_group...  18.6 us
    all_to_all x1, starting transfers between devices, exchange(): lax.all_to_all(cube, 'dom', split_axis=0, concat_axis=0, tiled=True)  11.9 us
    ppermute x2, starting transfers between devices, swap_ghosts(): below = lax.ppermute(near[0:4, 16:32].reshape(64, 128), 'dom', down)  8.95 us
    unnamed x33, local copies, waits for them, and re-layouts  7.09 us
  transfers between devices with their start and end apart: 5, of which 0 were waited for; matrix products, arithmetic and copies ran while one was open for 6% of the time, Pallas kernels for 12%

commit v1 on v0

v1 whole, which is shorter than its diff:
```python
import math

import jax
import jax.numpy as jnp
from jax import lax
from jax.experimental import pallas as pl
from jax.experimental.pallas import tpu as pltpu
from jax.sharding import PartitionSpec as P

ORDER = 5
MODES = 35
QUANT = 9
FEAT = MODES * QUANT
ROWS = 320
BLOCK = 256
DEVS = 128
CAP = 3
SLOTS = 384
STRIDE = 336
CHUNK = 1024
GHOSTS = 6
NEIGH = 8
STEPS = (1, -1, 2, -2, 3, -3, 4, -4)
F32 = jnp.float32
BF16 = jnp.bfloat16
FULL = 67043328


def weights_of(lower, upper):
    return [(upper ** (k + 1) - lower ** (k + 1)) / math.factorial(k + 1) for k in range(ORDER)]


def dot(a, b):
    return jnp.dot(a, b, preferred_element_type=F32)


def split2(x):
    high = x.astype(BF16)
    return high, (x - high.astype(F32)).astype(BF16)


def split3(x):
    high = x.astype(BF16)
    rest = x - high.astype(F32)
    mid = rest.astype(BF16)
    return high, mid, (rest - mid.astype(F32)).astype(BF16)


def dot3(a, b, dims=None):
    total = None
    for part in split3(a):
        if dims is None:
            term = dot(part, b)
        else:
            term = lax.dot_general(part, b, (dims, ((), ())), preferred_element_type=F32)
        total = term if total is None else total + term
    return total


def product(op, both):
    width = both.shape[1] // 2
    wide = dot(op[0:ROWS, :], both[...])
    return wide[:, 0:width] + wide[:, width:] + dot(op[ROWS:, :], both[:, 0:width])


def put(both, at, value):
    width = both.shape[1] // 2
    high, low = split2(value)
    both[ROWS * at : ROWS * (at + 1), 0:width] = high
    both[ROWS * at : ROWS * (at + 1), width:] = low


def owner_of(device):
    return jnp.where((device & 32) > 0, device ^ 24, device)


def iota(shape, dim):
    return lax.broadcasted_iota(jnp.int32, shape, dim)


def onehot(condition):
    return jnp.where(condition, 1.0, 0.0).astype(BF16)


def pack_rows(stage, out_ref):
    for k in range(8):
        out_ref[pl.ds(k, DEVS, stride=8), :] = stage[128 * k : 128 * k + 128, :].T


def unpack_rows(recv_ref, stage):
    for k in range(8):
        stage[128 * k : 128 * k + 128, :] = recv_ref[pl.ds(k, DEVS, stride=8), :].T


def scatter_kernel(
    modal, jac, area, cluster, target, faces, listed, out, tables, cells, values, stage, kinds, places, lists, done
):
    copies = [
        pltpu.make_async_copy(modal, cells, done.at[0]),
        pltpu.make_async_copy(jac, values.at[0:3, :], done.at[1]),
        pltpu.make_async_copy(area, values.at[3:7, :], done.at[2]),
        pltpu.make_async_copy(cluster, kinds, done.at[3]),
        pltpu.make_async_copy(target, places, done.at[4]),
        pltpu.make_async_copy(faces, tables.at[0:4, :], done.at[5]),
        pltpu.make_async_copy(listed, lists, done.at[6]),
    ]
    for copy in copies:
        copy.start()
    for copy in copies:
        copy.wait()
    tables[8:16, :] = jnp.zeros((8, SLOTS), jnp.int32)
    for i in range(GHOSTS):
        tables[8 + i : 9 + i, 0:NEIGH] = lists[i]
    values[7:8, :] = 1.0 + kinds[...].astype(F32)
    values[320:328, :] = jnp.zeros((8, BLOCK), F32)
    for q in range(QUANT):
        values[8 + MODES * q : 8 + MODES * (q + 1), :] = cells[q]
    slot = owner_of(iota((DEVS, BLOCK), 0)) * CAP
    wanted = places[...]
    stage[CAP * STRIDE :, :] = jnp.zeros((CHUNK - CAP * STRIDE, DEVS), F32)
    parts = split3(values[...])
    for t in range(CAP):
        hot = onehot(slot + t == wanted)
        total = None
        for part in parts:
            term = lax.dot_general(part, hot, (((1,), (1,)), ((), ())), preferred_element_type=F32)
            total = term if total is None else total + term
        stage[STRIDE * t : STRIDE * t + 328, :] = total
        stage[STRIDE * t + 328 : STRIDE * (t + 1), :] = jnp.zeros((8, DEVS), F32)
    pack_rows(stage, out)


def gather_kernel(recv, target, out, stage):
    unpack_rows(recv, stage)
    wanted = target[...]
    slot = owner_of(iota((DEVS, BLOCK), 0)) * CAP
    total = None
    for t in range(CAP):
        part = stage[STRIDE * t + 8 : STRIDE * t + 8 + ROWS, :]
        term = dot3(part, onehot(slot + t == wanted))
        total = term if total is None else total + term
    for q in range(QUANT):
        out[q] = total[MODES * q : MODES * (q + 1), :]


def operator_kernel(
    stiffness, minus, plus, star, solver_minus, solver_plus, d_out, c_out, b_out,
    k_in, m_in, p_in, s_in, sm_in, sp_in, tiles, square, columns, stage, b_op, c_op, loads, done,
):
    copies = fetch(
        [
            (stiffness, k_in), (minus, m_in), (plus, p_in), (star, s_in),
            (solver_minus, sm_in), (solver_plus, sp_in),
        ],
        loads,
    )
    col = iota((8, 2 * ROWS), 1)
    second = jnp.where(col >= ROWS, 1, 0)
    inner = col - second * ROWS
    quant = (inner * 1873) >> 16
    mode = inner - quant * MODES
    valid = inner < FEAT
    mode_code = jnp.where(valid, second * 128 + mode, -1)[0:1]
    quant_code = jnp.where(valid, second * 16 + quant, -512)[0:1]
    row = iota((256, 2 * ROWS), 0)
    mode_hot = onehot(row == mode_code)
    tiles[...] = jnp.zeros(tiles.shape, F32)
    square[...] = jnp.zeros(square.shape, F32)
    columns[...] = jnp.zeros(columns.shape, F32)
    for copy in copies:
        copy.wait()
    for c in range(3):
        square[0:MODES, 0:MODES] = -k_in[c]
        tiles[c] = square[...].T[0:48, :]
        tiles[3 + c, 0:MODES, 0:MODES] = k_in[c]
        columns[16 * c : 16 * c + QUANT, 0:QUANT] = s_in[:, c, :]
        columns[16 * (3 + c) : 16 * (3 + c) + QUANT, 0:QUANT] = s_in[:, c, :]
    for f in range(4):
        tiles[6 + f, 0:MODES, 0:MODES] = -m_in[:, f, :]
        tiles[10 + f, 0:MODES, 0:MODES] = -p_in[:, f, :]
        columns[16 * (6 + f) : 16 * (6 + f) + QUANT, 0:QUANT] = sm_in[:, f, :]
        columns[16 * (10 + f) : 16 * (10 + f) + QUANT, 0:QUANT] = sp_in[:, f, :]
    flux = split2(jnp.concatenate([columns[0:128, :].T[0:16, :], columns[128:256, :].T[0:16, :]], axis=1))

    def family(first, count, out):
        stage[FEAT:ROWS, :] = jnp.zeros((ROWS - FEAT, stage.shape[1]), F32)
        for k in range(0, count, 2):
            width = ROWS * min(2, count - k)
            at = first + k
            after = min(at + 1, 13)
            pair = split2(jnp.concatenate([tiles[at], tiles[after]], axis=1))
            quant_hot = onehot(row == quant_code + 16 * at)
            spread = dot(pair[0], mode_hot) + dot(pair[1], mode_hot)
            scale = dot(flux[0], quant_hot) + dot(flux[1], quant_hot)
            for p in range(QUANT):
                stage[MODES * p : MODES * (p + 1), ROWS * k : ROWS * k + width] = (
                    spread[0:MODES, 0:width] * scale[p : p + 1, 0:width]
                )
        a_high, a_low = split2(stage[:, 0 : ROWS * count])
        out[0:ROWS, :] = a_high
        out[ROWS:, :] = a_low

    family(3, 7, c_op)
    copies = fetch([(c_op, c_out)], done)
    family(10, 4, b_op)
    copies += fetch([(b_op, b_out)], done, 1)
    family(0, 3, d_out)
    for copy in copies:
        copy.wait()


def order_faces(faces):
    digits = jnp.concatenate([faces >> 4, faces & 15], axis=0).astype(F32).astype(BF16)
    from_slot = iota((SLOTS, SLOTS), 0)
    to_slot = iota((SLOTS, SLOTS), 1)
    moved = dot(digits, onehot(from_slot == (to_slot & 127) * CAP + (to_slot >> 7))).astype(jnp.int32)
    return moved[0:4, :] * 16 + moved[4:8, :]


def taylor(start, extras, d_op, pieces, factor_sets):
    cuts = [(0, 256), (256, SLOTS)]
    current = [start[:, lo:hi] for lo, hi in cuts]
    sums = [[value * factors[0] for value in current] for factors in factor_sets]
    for k in range(1, ORDER):
        for i, (lo, hi) in enumerate(cuts):
            for c in range(3):
                put(pieces[i], c, current[i] * extras[c : c + 1, lo:hi])
            current[i] = product(d_op, pieces[i])
            for total, factors in zip(sums, factor_sets):
                total[i] = total[i] + current[i] * factors[k]
    return [jnp.concatenate(total, axis=1) for total in sums]


def order_picks(listed, picks):
    value = listed
    digits = jnp.concatenate([value >> 4, value & 15], axis=0).astype(F32).astype(BF16)
    spread = dot(digits, onehot(iota((128, 128), 0) == (iota((128, 128), 1) >> 3))).astype(jnp.int32)
    spread = spread[0:8, :] * 16 + spread[8:16, :]
    lane = iota((1, 128), 1)
    part = jnp.where(lane < 64, lane & 7, 8)

    def choose(*moves):
        line = jnp.full((1, 128), -1, jnp.int32)
        for ghost, spot in moves:
            line = jnp.where(part == spot, spread[ghost : ghost + 1, :], line)
        return line

    picks[...] = jnp.full(picks.shape, -1, jnp.int32)
    picks[0:1, :] = choose(*[(i, i) for i in range(GHOSTS)])
    picks[1:2, :] = choose((0, 6), (2, 7))
    picks[2:3, :] = choose((1, 6), (3, 7))
    picks[3:4, :] = choose((4, 6))
    picks[4:5, :] = choose((5, 6))


def send_ghosts(value, picks, owner, out):
    out[...] = jnp.zeros(out.shape, F32)
    slot = iota((SLOTS, 128), 0)
    slot = (slot & 127) * CAP + (slot >> 7)
    base = onehot(slot == picks[0:1, :])
    rest = jnp.concatenate([onehot(slot == picks[k : k + 1, :]) for k in range(1, 5)], axis=1)
    main = dot3(value[0:256, :], base)
    tail = dot3(value[256:320, :], rest)
    first = (main[0:128, :] + jnp.concatenate([tail[:, 0:128], tail[:, 128:256]], axis=0)).T
    second = (main[128:256, :] + jnp.concatenate([tail[:, 256:384], tail[:, 384:512]], axis=0)).T
    spot = owner & 7
    for b, step in enumerate(STEPS):
        goal = spot + step
        outside = jnp.where((goal < 0) | (goal > 7), 16, 0)
        place = ((goal + 8) & 7) * 32 + outside
        out[pl.ds(pl.multiple_of(place, 16), 8), :] = first[8 * b : 8 * b + 8, :]
        out[pl.ds(pl.multiple_of(place + 8, 8), 8), :] = second[8 * b : 8 * b + 8, :]


def read_ghosts(near, above, below, owner):
    firsts, seconds = [], []
    spot = owner & 7
    for step in STEPS:
        origin = spot - step
        inside = (origin >= 0) & (origin <= 7)
        place = pl.multiple_of(((origin + 8) & 7) * 32, 32)
        far = pl.multiple_of((origin & 3) * 16, 16)
        other = above if step > 0 else below
        firsts.append(jnp.where(inside, near[pl.ds(place, 8), :], other[pl.ds(far, 8), :]))
        seconds.append(jnp.where(inside, near[pl.ds(place + 8, 8), :], other[pl.ds(far + 8, 8), :]))
    blank = jnp.zeros((64, 128), F32)
    first = jnp.concatenate(firsts + [blank], axis=0).T
    second = jnp.concatenate(seconds + [blank], axis=0).T
    row = iota((128, 128), 0)
    col = iota((128, 128), 1)
    part = col & 7
    group = col - part
    halves = [first[0:64, :], first[64:128, :], second[0:64, :], second[64:128, :]]
    places = [((0, 6), (2, 7)), ((1, 6), (3, 7)), ((4, 6),), ((5, 6),)]
    tail = None
    for half, moves in zip(halves, places):
        hit = None
        for ghost, spot in moves:
            one = (part == ghost) & (row == group + spot)
            hit = one if hit is None else hit | one
        term = dot3(half, onehot(hit))
        tail = term if tail is None else tail + term
    return jnp.concatenate([first, second, tail], axis=0)


def remote_flux(value, ghosts, extras, faces, b_op, both):
    high, low = split2(jnp.concatenate([value, ghosts], axis=1))
    row = iota((512, 128), 0)
    beyond = row - SLOTS
    local = (row & 127) * CAP + (row >> 7)
    spot = beyond & 7
    ghost = jnp.where((spot < GHOSTS) & (beyond < 64), SLOTS + (beyond >> 3) * GHOSTS + spot, -1)
    code = jnp.where(row < SLOTS, local, ghost)
    for f in range(4):
        hot = jnp.concatenate(
            [onehot(code == faces[f : f + 1, 128 * k : 128 * (k + 1)]) for k in range(3)], axis=1
        )
        picked = (dot(high, hot) + dot(low, hot)) * extras[3 + f : 4 + f, :]
        put(both, f, picked)
    return product(b_op, both)


def fetch(pairs, done, base=0):
    copies = [pltpu.make_async_copy(src, dst, done.at[base + k]) for k, (src, dst) in enumerate(pairs)]
    for copy in copies:
        copy.start()
    return copies


def occupied(extras):
    return jnp.where(extras[7:8, :] > 0.5, 1.0, 0.0)


def start_kernel(
    owner, recv, tables, d_op, state, extras, first, later, picks, ghosts, stage, one_piece, other_piece
):
    order_picks(tables[8:16, 0:128], picks)
    unpack_rows(recv, stage)
    for t in range(CAP):
        extras[:, 128 * t : 128 * (t + 1)] = stage[STRIDE * t : STRIDE * t + 8, :]
        state[:, 128 * t : 128 * (t + 1)] = stage[STRIDE * t + 8 : STRIDE * t + 8 + ROWS, :]
    one, two = taylor(
        state[...], extras, d_op, (one_piece, other_piece), [weights_of(0.0, 1.0), weights_of(1.0, 2.0)]
    )
    first[...] = one
    later[...] = two
    send_ghosts(first, picks, owner[0], ghosts)


def local_kernel(state, value, extras, c_op, faces, out, order, both):
    order[...] = order_faces(faces[0:4, :])
    local_terms(state, value, extras, c_op, out, both)


def local_terms(state, value, extras, c_op, out, both):
    for k in range(7):
        put(both, k, value[...] * extras[k : k + 1, :])
    change = product(c_op, both)
    out[...] = state[...] + occupied(extras) * change


def middle_kernel(
    owner, near, above, below, partial, first, later, extras, faces, picks, d_op, b_op,
    middle, second, ghosts, one_piece, other_piece, wide,
):
    table = read_ghosts(near, above, below, owner[0])
    flux = remote_flux(first[...], table, extras, faces, b_op, wide)
    middle[...] = partial[...] + occupied(extras) * flux
    (fresh,) = taylor(middle[...], extras, d_op, (one_piece, other_piece), [weights_of(0.0, 1.0)])
    second[...] = jnp.where(extras[7:8, :] > 1.5, later[...], fresh)
    send_ghosts(second, picks, owner[0], ghosts)


def final_kernel(
    owner, near, above, below, partial, second, extras, faces, b_op, out, stage, wide
):
    table = read_ghosts(near, above, below, owner[0])
    flux = remote_flux(second[...], table, extras, faces, b_op, wide)
    final = partial[...] + occupied(extras) * flux
    stage[...] = jnp.zeros((CHUNK, DEVS), F32)
    for t in range(CAP):
        stage[STRIDE * t + 8 : STRIDE * t + 8 + ROWS, :] = final[:, 128 * t : 128 * (t + 1)]
    pack_rows(stage, out)


def shape(*dims, dtype=F32):
    return jax.ShapeDtypeStruct(dims, dtype)


def call(kernel, name, outs, scratch, flops, operands, spaces="", out_spaces="", limit=16 * 1024 * 1024):
    kinds = {"s": pltpu.SMEM, "v": pltpu.VMEM, "h": pltpu.HBM}
    spaces = spaces.ljust(len(operands), "v")
    flat = jax.tree.leaves(outs)
    out_specs = [pl.BlockSpec(memory_space=kinds[k]) for k in out_spaces.ljust(len(flat), "v")]
    moved = sum(math.prod(o.shape) * 4 for o in operands)
    return pl.pallas_call(
        kernel,
        name=name,
        out_shape=outs,
        in_specs=[pl.BlockSpec(memory_space=kinds[k]) for k in spaces],
        out_specs=out_specs if isinstance(outs, list) else out_specs[0],
        scratch_shapes=scratch,
        cost_estimate=pl.CostEstimate(flops=flops, bytes_accessed=moved, transcendentals=0),
        compiler_params=pltpu.CompilerParams(vmem_limit_bytes=limit),
    )(*operands)


def vmem(*dims, dtype=F32):
    return pltpu.VMEM(dims, dtype)


def exchange(rows, per):
    cube = rows.reshape(DEVS, per, 128)
    return lax.all_to_all(cube, "dom", split_axis=0, concat_axis=0, tiled=True).reshape(DEVS * per, 128)


def device_of(owner):
    return owner ^ 24 if owner & 32 else owner


def swap_ghosts(rows):
    groups = [list(range(8 * k, 8 * k + 8)) for k in range(DEVS // 8)]
    cube = rows.reshape(8, 32, 128)
    near = lax.all_to_all(cube, "dom", split_axis=0, concat_axis=0, axis_index_groups=groups, tiled=True)
    up = [(device_of(i), device_of((i + 8) % DEVS)) for i in range(DEVS)]
    down = [(b, a) for a, b in up]
    above = lax.ppermute(near[4:8, 16:32].reshape(64, 128), "dom", up)
    below = lax.ppermute(near[0:4, 16:32].reshape(64, 128), "dom", down)
    return near.reshape(256, 128), above, below


def local(
    modal_dofs, jacobian, face_area, cluster_id, target_slot, ghost_slots, face_neighbours,
    stiffness, star_matrix, face_minus, face_plus, solver_minus, solver_plus,
):
    owner = lax.axis_index("dom").astype(jnp.int32).reshape(1)
    target = target_slot.reshape(1, BLOCK)
    sent, tables = call(
        scatter_kernel, "scatter", [shape(CHUNK, DEVS), shape(16, SLOTS, dtype=jnp.int32)],
        [
            vmem(QUANT, MODES, BLOCK), vmem(328, BLOCK), vmem(CHUNK, DEVS), vmem(1, BLOCK, dtype=jnp.int32),
            vmem(1, BLOCK, dtype=jnp.int32), vmem(6, 1, NEIGH, dtype=jnp.int32), pltpu.SemaphoreType.DMA((7,)),
        ],
        10**8,
        (
            jnp.transpose(modal_dofs, (1, 0, 2)), jacobian, face_area, cluster_id.reshape(1, BLOCK), target,
            face_neighbours, jnp.transpose(ghost_slots, (2, 0, 1)),
        ),
        "hhhhhhh", "", FULL,
    )
    received = exchange(sent, 8)

    d_op, c_op, b_op = call(
        operator_kernel, "operators",
        [shape(2 * ROWS, k * ROWS, dtype=BF16) for k in (3, 7, 4)],
        [
            vmem(3, MODES, MODES), vmem(MODES, 4, MODES), vmem(MODES, 4, MODES),
            vmem(QUANT, 3, QUANT), vmem(QUANT, 4, QUANT), vmem(QUANT, 4, QUANT),
            vmem(14, 48, 128), vmem(128, 128), vmem(256, 128), vmem(ROWS, 7 * ROWS),
            vmem(2 * ROWS, 4 * ROWS, dtype=BF16), vmem(2 * ROWS, 7 * ROWS, dtype=BF16),
            pltpu.SemaphoreType.DMA((6,)), pltpu.SemaphoreType.DMA((2,)),
        ],
        10**9,
        (stiffness, *[jnp.transpose(a, (1, 0, 2)) for a in (face_minus, face_plus, star_matrix, solver_minus, solver_plus)]),
        "hhhhhh", "vhh", FULL - 1900 * 1024,
    )
    home = [(o, device_of(o)) for o in range(DEVS)]
    tables = lax.ppermute(tables, "dom", home)
    received, tables = lax.optimization_barrier((received, tables))
    x_scratch = [vmem(3 * ROWS, 512, dtype=BF16), vmem(3 * ROWS, 256, dtype=BF16)]
    y_scratch = [vmem(4 * ROWS, 2 * SLOTS, dtype=BF16)]
    z_scratch = [vmem(7 * ROWS, 2 * SLOTS, dtype=BF16)]
    field = shape(ROWS, SLOTS)
    halo = shape(8 * 32, 128)
    state, extras, first, later, picks, out1 = call(
        start_kernel, "start", [field, shape(8, SLOTS), field, field, shape(8, 128, dtype=jnp.int32), halo],
        [vmem(CHUNK, DEVS)] + x_scratch,
        10**9, (owner, received, tables, d_op), "s",
    )
    near, above, below = swap_ghosts(out1)
    first, _ = lax.optimization_barrier((first, near))
    partial1, faces = call(
        local_kernel, "local1", [field, shape(4, SLOTS, dtype=jnp.int32)], z_scratch, 10**9,
        (state, first, extras, c_op, tables),
    )
    middle, second, out2 = call(
        middle_kernel, "middle", [field, field, halo],
        x_scratch + y_scratch, 2 * 10**9,
        (owner, near, above, below, partial1, first, later, extras, faces, picks, d_op, b_op), "s",
    )
    near, above, below = swap_ghosts(out2)
    second, _ = lax.optimization_barrier((second, near))
    partial2 = call(
        local_terms, "local2", field, z_scratch, 10**9, (middle, second, extras, c_op)
    )
    back = call(
        final_kernel, "final", shape(CHUNK, DEVS),
        [vmem(CHUNK, DEVS)] + y_scratch, 10**9,
        (owner, near, above, below, partial2, second, extras, faces, b_op), "s",
    )
    returned = exchange(back, 8)
    result = call(
        gather_kernel, "gather", shape(QUANT, MODES, BLOCK), [vmem(CHUNK, DEVS)], 10**8, (returned, target)
    )
    return jnp.transpose(result, (1, 0, 2))


def solution(mesh):
    placed = (
        P(None, None, "dom"), P(None, "dom"), P(None, "dom"), P("dom"), P("dom"), P("dom", None, None),
        P(None, "dom"), P(), P(), P(), P(), P(), P(),
    )
    return jax.shard_map(
        local, mesh=mesh, in_specs=placed, out_specs=P(None, None, "dom"), check_vma=False
    )
```

time: 110 us -> 94.2 us (0.86)
  local copies, waits for them, and re-layouts: 8.96 us -> 1.34 us
  Pallas kernels: 37.7 us -> 32 us
  waiting for transfers between devices: 0.01 us -> 5.3 us
  starting transfers between devices: 22.3 us -> 18.3 us
  blocking collectives: 39.4 us -> 36.7 us
    unnamed x33 -> x8, local copies, waits for them, and re-layouts: 7.09 us -> 1.33 us
    pallas_call x8, Pallas kernels: 37.7 us -> 32 us  [call(): pl.pallas_call(kernel, name=name, out_shape=outs, in_specs=[pl.BlockSpec(...]
    all_to_all x1, waiting for transfers between devices: 0.01 us -> 5.28 us  [exchange(): lax.all_to_all(cube, 'dom', split_axis=0, concat_axis=0, tiled=True)]
    ppermute x2, starting transfers between devices: 8.95 us -> 4.94 us  [swap_ghosts(): below = lax.ppermute(near[0:4, 16:32].reshape(64, 128), 'dom', down)]
    all_to_all x1, blocking collectives: 20.8 us -> 18.9 us  [exchange(): lax.all_to_all(cube, 'dom', split_axis=0, concat_axis=0, tiled=True)]
    ppermute x0 -> x1, starting transfers between devices: none -> 1.4 us  [local(): tables = lax.ppermute(tables, 'dom', home)]
  transfers between devices with their start and end apart: 5 -> 6, of which waited for: 0 -> 1; matrix products, arithmetic and copies ran while one was open for 6% -> 0% of each run, Pallas kernels for 12% -> 12%
where the time goes in v1:
time: 94.2 us; the launch traced here: 93.8 us
  blocking collectives  36.7 us (39%)
  Pallas kernels  32 us (34%)
  starting transfers between devices  18.3 us (19%)
  waiting for transfers between devices  5.3 us (6%)
  local copies, waits for them, and re-layouts  1.34 us (1%)
    pallas_call x8, Pallas kernels, call(): pl.pallas_call(kernel, name=name, out_shape=outs, in_specs=[pl.BlockSpec(...  32 us
    all_to_all x1, blocking collectives, exchange(): lax.all_to_all(cube, 'dom', split_axis=0, concat_axis=0, tiled=True)  18.9 us
    all_to_all x2, blocking collectives, swap_ghosts(): lax.all_to_all(cube, 'dom', split_axis=0, concat_axis=0, axis_index_group...  17.8 us
    all_to_all x1, starting transfers between devices, exchange(): lax.all_to_all(cube, 'dom', split_axis=0, concat_axis=0, tiled=True)  11.5 us
    all_to_all x1, waiting for transfers between devices, exchange(): lax.all_to_all(cube, 'dom', split_axis=0, concat_axis=0, tiled=True)  5.28 us
    ppermute x2, starting transfers between devices, swap_ghosts(): below = lax.ppermute(near[0:4, 16:32].reshape(64, 128), 'dom', down)  4.94 us
  transfers between devices with their start and end apart: 6, of which 1 were waited for; matrix products, arithmetic and copies ran while one was open for 0% of the time, Pallas kernels for 12%

profile of v1, /device:TPU:1, one launch (start us, length us, event | category | flops | bytes accessed | tf_op | source)
XLA Modules:
  0.0 93.8 jit_solution(12311512886334487307)
XLA Ops:
  0.0 2.6 %scatter.1 = (f32[1024,128]{1,0:T(8,128)}, s32[16,384]{1,0:T(8,128)}) custom-call(f32[9,35,256]{2,1,0:T(8,128)} %bitcast.33, f32[3,256]{1,0:T(4,128)} %jac.1, f32[4,256]{1,0:T(4,128)} %area.1, s32[1,256]{1,0:T(1,128)} %bitcast.39, s32[1,256]{1,0:T(1,128)} %bitcast.30, s32[4,384]{1,0:T(4,128)} %faces.1, s32[6,1,8]{2,1,0:T(1,128)} %bitcast.38), custom_call_target="tpu_custom_call" | custom-call | flops 100000000 | bytes 338112 | tf_op jit(solution)/shard_map/scatter/pallas_call | solution.py:396
  2.6 11.5 %all-to-all-start = ((f32[128,8,128]{2,1,0:T(8,128)}), f32[128,8,128]{2,1,0:T(8,128)S(1)}, u32[]{:S(2)}, u32[]{:S(2)}) async-start(f32[128,8,128]{2,1,0:T(8,128)} %bitcast.32), calls=%async_computation | async-start | bytes 1048576 | tf_op jit(solution)/shard_map/all_to_all | solution.py:414
  14.1 1.4 %collective-permute-start = (s32[16,384]{1,0:T(8,128)}, s32[16,384]{1,0:T(8,128)S(1)}, u32[]{:S(2)}, u32[]{:S(2)}) collective-permute-start(s32[16,384]{1,0:T(8,128)} %get-tuple-element.26), channel_id=1, source_target_pairs={{0,0},{1,1},{2,2},{3,3},{4,4},{5,5},{6,6},{7,7},{8,8},{9,9},{10,10... | collective-permute-start | bytes 73736 | tf_op jit(solution)/shard_map/ppermute | solution.py:468
  15.5 6.8 %operators.1 = (bf16[640,960]{1,0:T(8,128)(2,1)}, bf16[640,2240]{1,0:T(8,128)(2,1)}, bf16[640,1280]{1,0:T(8,128)(2,1)}) custom-call(f32[3,35,35]{2,1,0:T(8,128)} %stiffness.1, f32[35,4,35]{2,1,0:T(4,128)} %bitcast.40, f32[35,4,35]{2,1,0:T(4,128)} %bitcast.41, f32[9,3,9]{2,1,0:T(4,128)} %bitcast.42, f32[9,4,9]{2,1,0:T(4,128)} %bitcast.43, f32[9,4,9]{2,1,0:T(4,128)} %bitcast.44), custom_call_target="tpu_custom_call" | custom-call | flops 1000000000 | bytes 57464 | tf_op jit(solution)/shard_map/operators/pallas_call | solution.py:396
  22.3 0.0 collective-permute-done.tables.faces
  22.3 5.3 %all-to-all-done = f32[128,8,128]{2,1,0:T(8,128)S(1)} async-done(((f32[128,8,128]{2,1,0:T(8,128)}), f32[128,8,128]{2,1,0:T(8,128)S(1)}, u32[]{:S(2)}, u32[]{:S(2)}) %all-to-all-start) | async-done | bytes 524320 | tf_op jit(solution)/shard_map/all_to_all | solution.py:414
  27.6 0.0 copy-start.3
  27.6 1.3 %copy-done.3 = bf16[640,960]{1,0:T(8,128)(2,1)S(1)} copy-done((bf16[640,960]{1,0:T(8,128)(2,1)S(1)}, bf16[640,960]{1,0:T(8,128)(2,1)}, u32[]{:S(2)}) %copy-start.3) | copy-done | bytes 1228824
  28.9 0.0 copy-start
  28.9 5.5 %start.1 = (f32[320,384]{1,0:T(8,128)S(1)}, f32[8,384]{1,0:T(8,128)S(1)}, f32[320,384]{1,0:T(8,128)S(1)}, f32[320,384]{1,0:T(8,128)S(1)}, s32[8,128]{1,0:T(8,128)S(1)}, /*index=5*/f32[256,128]{1,0:T(8,128)S(1)}) custom-call(s32[1]{0:T(128)} %bitcast.owner, f32[1024,128]{1,0:T(8,128)S(1)} %bitcast.24, s32[16,384]{1,0:T(8,128)S(1)} %collective-permute-done.tables.faces, ...), custom_call_target="tpu_custom_call" | custom-call | flops 1000000000 | bytes 3006468 | tf_op jit(solution)/shard_map/start/pallas_call | solution.py:396
  34.4 8.7 %all_to_all.20 = f32[8,32,128]{2,1,0:T(8,128)S(1)} all-to-all(f32[8,32,128]{2,1,0:T(8,128)S(1)} %bitcast.29), channel_id=1, replica_groups={{0,1,2,3,4,5,6,7},{8,9,10,11,12,13,14,15},{16,17,18,19,20,21,22,23},{24..., dimensions={0} | all-to-all | bytes 262144 | tf_op jit(solution)/shard_map/all_to_all | solution.py:424
  43.1 0.5 collective-permute-start.1
  43.6 2.2 %collective-permute-start.2 = (f32[64,128]{1,0:T(8,128)S(1)}, f32[64,128]{1,0:T(8,128)S(1)}, u32[]{:S(2)}, u32[]{:S(2)}) collective-permute-start(f32[64,128]{1,0:T(8,128)S(1)} %bitcast.34), channel_id=1, source_target_pairs={{8,0},{9,1},{10,2},{11,3},{12,4},{13,5},{14,6},{15,7},{16,8},{17,9... | collective-permute-start | bytes 98312 | tf_op jit(solution)/shard_map/ppermute | solution.py:428
  45.8 0.0 copy-done
  45.8 0.0 copy-start.2
  45.8 2.3 %local1.1 = (f32[320,384]{1,0:T(8,128)S(1)}, s32[4,384]{1,0:T(4,128)S(1)}) custom-call(f32[320,384]{1,0:T(8,128)S(1)} %get-tuple-element.31.state, f32[320,384]{1,0:T(8,128)S(1)} %get-tuple-element.33.value.first, f32[8,384]{1,0:T(8,128)S(1)} %get-tuple-element.34.extras, bf16[640,2240]{1,0:T(8,128)(2,1)S(1)} %copy-done, ...), custom_call_target="tpu_custom_call" | custom-call | flops 1000000000 | bytes 6754304 | tf_op jit(solution)/shard_map/local1/pallas_call | solution.py:396
  48.1 0.0 collective-permute-done.1.above
  48.1 0.0 collective-permute-done.2.below
  48.1 0.0 copy-done.2
  48.1 8.2 %middle.1 = (f32[320,384]{1,0:T(8,128)S(1)}, f32[320,384]{1,0:T(8,128)S(1)}, f32[256,128]{1,0:T(8,128)S(1)}) custom-call(s32[1]{0:T(128)} %bitcast.owner, f32[256,128]{1,0:T(8,128)S(1)} %bitcast.26, f32[64,128]{1,0:T(8,128)S(1)} %collective-permute-done.1.above, f32[64,128]{1,0:T(8,128)S(1)} %collective-permute-done.2.below, ...), custom_call_target="tpu_custom_call" | custom-call | flops 2000000000 | bytes 7428100 | tf_op jit(solution)/shard_map/middle/pallas_call | solution.py:396
  56.3 9.0 %all_to_all.21 = f32[8,32,128]{2,1,0:T(8,128)S(1)} all-to-all(f32[8,32,128]{2,1,0:T(8,128)S(1)} %bitcast.28), channel_id=1, replica_groups={{0,1,2,3,4,5,6,7},{8,9,10,11,12,13,14,15},{16,17,18,19,20,21,22,23},{24..., dimensions={0} | all-to-all | bytes 262144 | tf_op jit(solution)/shard_map/all_to_all | solution.py:424
  65.4 0.0 collective-permute-start.3
  65.4 2.8 %collective-permute-start.4 = (f32[64,128]{1,0:T(8,128)S(1)}, f32[64,128]{1,0:T(8,128)S(1)}, u32[]{:S(2)}, u32[]{:S(2)}) collective-permute-start(f32[64,128]{1,0:T(8,128)S(1)} %bitcast.35), channel_id=1, source_target_pairs={{8,0},{9,1},{10,2},{11,3},{12,4},{13,5},{14,6},{15,7},{16,8},{17,9... | collective-permute-start | bytes 98312 | tf_op jit(solution)/shard_map/ppermute | solution.py:428
  68.2 2.3 %local2.1.partial = f32[320,384]{1,0:T(8,128)S(1)} custom-call(f32[320,384]{1,0:T(8,128)S(1)} %get-tuple-element.42.state, f32[320,384]{1,0:T(8,128)S(1)} %get-tuple-element.44.value.second, f32[8,384]{1,0:T(8,128)S(1)} %get-tuple-element.34.extras, bf16[640,2240]{1,0:T(8,128)(2,1)S(1)} %copy-done), custom_call_target="tpu_custom_call" | custom-call | flops 1000000000 | bytes 6729728 | tf_op jit(solution)/shard_map/local2/pallas_call | solution.py:396
  70.4 0.0 copy-start.1
  70.4 0.0 collective-permute-done.3.above
  70.4 0.0 collective-permute-done.4.below
  70.5 3.0 %final.1 = f32[1024,128]{1,0:T(8,128)S(1)} custom-call(s32[1]{0:T(128)} %bitcast.owner, f32[256,128]{1,0:T(8,128)S(1)} %bitcast.27, f32[64,128]{1,0:T(8,128)S(1)} %collective-permute-done.3.above, f32[64,128]{1,0:T(8,128)S(1)} %collective-permute-done.4.below, f32[320,384]{1,0:T(8,128)S(1)} %local2.1.partial, f32[320,384]{1,0:T(8,128)S(1)} %get-tuple-element.44.value.second, ...), custom_call_target="tpu_custom_call" | custom-call | flops 1000000000 | bytes 4474884 | tf_op jit(solution)/shard_map/final/pallas_call | solution.py:396
  73.5 18.9 %all_to_all.22 = f32[128,8,128]{2,1,0:T(8,128)S(1)} all-to-all(f32[128,8,128]{2,1,0:T(8,128)S(1)} %bitcast.25), channel_id=1, replica_groups=mesh['dom'=128] {'dom'}, dimensions={0} | all-to-all | bytes 1048576 | tf_op jit(solution)/shard_map/all_to_all | solution.py:414
  92.4 0.0 copy-done.1
  92.4 1.3 %gather.1 = f32[9,35,256]{2,1,0:T(8,128)} custom-call(f32[1024,128]{1,0:T(8,128)S(1)} %bitcast.23, s32[1,256]{1,0:T(1,128)S(1)} %bitcast.31), custom_call_target="tpu_custom_call" | custom-call | flops 100000000 | bytes 525312 | tf_op jit(solution)/shard_map/gather/pallas_call | solution.py:396
  (2 shorter events, 0.0 us)
Async XLA Ops:
  2.6 25.0 %all-to-all-start = ((f32[128,8,128]{2,1,0:T(8,128)}), f32[128,8,128]{2,1,0:T(8,128)S(1)}, u32[]{:S(2)}, u32[]{:S(2)}) async-start(f32[128,8,128]{2,1,0:T(8,128)} %bitcast.32), calls=%async_computation | async-start | bytes 1048576 | tf_op jit(solution)/shard_map/all_to_all | solution.py:414
  14.1 8.2 %collective-permute-start = (s32[16,384]{1,0:T(8,128)}, s32[16,384]{1,0:T(8,128)S(1)}, u32[]{:S(2)}, u32[]{:S(2)}) collective-permute-start(s32[16,384]{1,0:T(8,128)} %get-tuple-element.26), channel_id=1, source_target_pairs={{0,0},{1,1},{2,2},{3,3},{4,4},{5,5},{6,6},{7,7},{8,8},{9,9},{10,10... | collective-permute-start | bytes 73736 | tf_op jit(solution)/shard_map/ppermute | solution.py:468
  27.6 1.3 %copy-start.3 = (bf16[640,960]{1,0:T(8,128)(2,1)S(1)}, bf16[640,960]{1,0:T(8,128)(2,1)}, u32[]{:S(2)}) copy-start(bf16[640,960]{1,0:T(8,128)(2,1)} %get-tuple-element.29.d_op) | copy-start | bytes 3686404
  28.9 16.9 %copy-start = (bf16[640,2240]{1,0:T(8,128)(2,1)S(1)}, bf16[640,2240]{1,0:T(8,128)(2,1)}, u32[]{:S(2)}) copy-start(bf16[640,2240]{1,0:T(8,128)(2,1)} %get-tuple-element.35.c_op) | copy-start | bytes 8601604
  43.1 5.0 %collective-permute-start.1 = (f32[64,128]{1,0:T(8,128)S(1)}, f32[64,128]{1,0:T(8,128)S(1)}, u32[]{:S(2)}, u32[]{:S(2)}) collective-permute-start(f32[64,128]{1,0:T(8,128)S(1)} %bitcast.36), channel_id=1, source_target_pairs={{0,8},{1,9},{2,10},{3,11},{4,12},{5,13},{6,14},{7,15},{8,16},{9,17... | collective-permute-start | bytes 98312 | tf_op jit(solution)/shard_map/ppermute | solution.py:427
  43.6 4.5 %collective-permute-start.2 = (f32[64,128]{1,0:T(8,128)S(1)}, f32[64,128]{1,0:T(8,128)S(1)}, u32[]{:S(2)}, u32[]{:S(2)}) collective-permute-start(f32[64,128]{1,0:T(8,128)S(1)} %bitcast.34), channel_id=1, source_target_pairs={{8,0},{9,1},{10,2},{11,3},{12,4},{13,5},{14,6},{15,7},{16,8},{17,9... | collective-permute-start | bytes 98312 | tf_op jit(solution)/shard_map/ppermute | solution.py:428
  45.8 2.4 %copy-start.2 = (bf16[640,1280]{1,0:T(8,128)(2,1)S(1)}, bf16[640,1280]{1,0:T(8,128)(2,1)}, u32[]{:S(2)}) copy-start(bf16[640,1280]{1,0:T(8,128)(2,1)} %get-tuple-element.40.b_op) | copy-start | bytes 4915204
  65.4 5.0 %collective-permute-start.3 = (f32[64,128]{1,0:T(8,128)S(1)}, f32[64,128]{1,0:T(8,128)S(1)}, u32[]{:S(2)}, u32[]{:S(2)}) collective-permute-start(f32[64,128]{1,0:T(8,128)S(1)} %bitcast.37), channel_id=1, source_target_pairs={{0,8},{1,9},{2,10},{3,11},{4,12},{5,13},{6,14},{7,15},{8,16},{9,17... | collective-permute-start | bytes 98312 | tf_op jit(solution)/shard_map/ppermute | solution.py:427
  65.4 5.1 %collective-permute-start.4 = (f32[64,128]{1,0:T(8,128)S(1)}, f32[64,128]{1,0:T(8,128)S(1)}, u32[]{:S(2)}, u32[]{:S(2)}) collective-permute-start(f32[64,128]{1,0:T(8,128)S(1)} %bitcast.35), channel_id=1, source_target_pairs={{8,0},{9,1},{10,2},{11,3},{12,4},{13,5},{14,6},{15,7},{16,8},{17,9... | collective-permute-start | bytes 98312 | tf_op jit(solution)/shard_map/ppermute | solution.py:428
  70.4 22.0 %copy-start.1 = (s32[256]{0:T(256)S(1)}, s32[256]{0:T(256)}, u32[]{:S(2)}) copy-start(s32[256]{0:T(256)} %param.17) | copy-start | bytes 3076

commit v2 on v1

--- a/solution.py
+++ b/solution.py
@@ -272,17 +272,16 @@
         out[pl.ds(pl.multiple_of(place + 8, 8), 8), :] = second[8 * b : 8 * b + 8, :]
 
 
-def read_ghosts(near, above, below, owner):
+def read_ghosts(near, far, owner):
     firsts, seconds = [], []
     spot = owner & 7
     for step in STEPS:
         origin = spot - step
         inside = (origin >= 0) & (origin <= 7)
         place = pl.multiple_of(((origin + 8) & 7) * 32, 32)
-        far = pl.multiple_of((origin & 3) * 16, 16)
-        other = above if step > 0 else below
-        firsts.append(jnp.where(inside, near[pl.ds(place, 8), :], other[pl.ds(far, 8), :]))
-        seconds.append(jnp.where(inside, near[pl.ds(place + 8, 8), :], other[pl.ds(far + 8, 8), :]))
+        other = pl.multiple_of((origin & 3) * 16, 16)
+        firsts.append(jnp.where(inside, near[pl.ds(place, 8), :], far[pl.ds(other, 8), :]))
+        seconds.append(jnp.where(inside, near[pl.ds(place + 8, 8), :], far[pl.ds(other + 8, 8), :]))
     blank = jnp.zeros((64, 128), F32)
     first = jnp.concatenate(firsts + [blank], axis=0).T
     second = jnp.concatenate(seconds + [blank], axis=0).T
@@ -331,14 +330,15 @@
     return jnp.where(extras[7:8, :] > 0.5, 1.0, 0.0)
 
 
-def start_kernel(
-    owner, recv, tables, d_op, state, extras, first, later, picks, ghosts, stage, one_piece, other_piece
-):
+def unpack_kernel(recv, tables, state, extras, picks, stage):
     order_picks(tables[8:16, 0:128], picks)
     unpack_rows(recv, stage)
     for t in range(CAP):
         extras[:, 128 * t : 128 * (t + 1)] = stage[STRIDE * t : STRIDE * t + 8, :]
         state[:, 128 * t : 128 * (t + 1)] = stage[STRIDE * t + 8 : STRIDE * t + 8 + ROWS, :]
+
+
+def start_kernel(owner, state, extras, picks, d_op, first, later, ghosts, one_piece, other_piece):
     one, two = taylor(
         state[...], extras, d_op, (one_piece, other_piece), [weights_of(0.0, 1.0), weights_of(1.0, 2.0)]
     )
@@ -360,10 +360,10 @@
 
 
 def middle_kernel(
-    owner, near, above, below, partial, first, later, extras, faces, picks, d_op, b_op,
+    owner, near, far, partial, first, later, extras, faces, picks, d_op, b_op,
     middle, second, ghosts, one_piece, other_piece, wide,
 ):
-    table = read_ghosts(near, above, below, owner[0])
+    table = read_ghosts(near, far, owner[0])
     flux = remote_flux(first[...], table, extras, faces, b_op, wide)
     middle[...] = partial[...] + occupied(extras) * flux
     (fresh,) = taylor(middle[...], extras, d_op, (one_piece, other_piece), [weights_of(0.0, 1.0)])
@@ -372,9 +372,9 @@
 
 
 def final_kernel(
-    owner, near, above, below, partial, second, extras, faces, b_op, out, stage, wide
+    owner, near, far, partial, second, extras, faces, b_op, out, stage, wide
 ):
-    table = read_ghosts(near, above, below, owner[0])
+    table = read_ghosts(near, far, owner[0])
     flux = remote_flux(second[...], table, extras, faces, b_op, wide)
     final = partial[...] + occupied(extras) * flux
     stage[...] = jnp.zeros((CHUNK, DEVS), F32)
@@ -420,13 +420,13 @@
 
 def swap_ghosts(rows):
     groups = [list(range(8 * k, 8 * k + 8)) for k in range(DEVS // 8)]
+    first = jnp.where((lax.axis_index("dom") & 4) == 0, 4, 0).astype(jnp.uint32)
+    rows, first = lax.optimization_barrier((rows, first))
     cube = rows.reshape(8, 32, 128)
     near = lax.all_to_all(cube, "dom", split_axis=0, concat_axis=0, axis_index_groups=groups, tiled=True)
-    up = [(device_of(i), device_of((i + 8) % DEVS)) for i in range(DEVS)]
-    down = [(b, a) for a, b in up]
-    above = lax.ppermute(near[4:8, 16:32].reshape(64, 128), "dom", up)
-    below = lax.ppermute(near[0:4, 16:32].reshape(64, 128), "dom", down)
-    return near.reshape(256, 128), above, below
+    relay = lax.dynamic_slice(near, (first, jnp.uint32(16), jnp.uint32(0)), (4, 16, 128)).reshape(64, 128)
+    pairs = [(device_of(o), device_of((o + (8 if o & 4 == 0 else -8)) % DEVS)) for o in range(DEVS)]
+    return near.reshape(256, 128), lax.ppermute(relay, "dom", pairs)
 
 
 def local(
@@ -472,12 +472,14 @@
     z_scratch = [vmem(7 * ROWS, 2 * SLOTS, dtype=BF16)]
     field = shape(ROWS, SLOTS)
     halo = shape(8 * 32, 128)
-    state, extras, first, later, picks, out1 = call(
-        start_kernel, "start", [field, shape(8, SLOTS), field, field, shape(8, 128, dtype=jnp.int32), halo],
-        [vmem(CHUNK, DEVS)] + x_scratch,
-        10**9, (owner, received, tables, d_op), "s",
-    )
-    near, above, below = swap_ghosts(out1)
+    state, extras, picks = call(
+        unpack_kernel, "unpack", [field, shape(8, SLOTS), shape(8, 128, dtype=jnp.int32)],
+        [vmem(CHUNK, DEVS)], 10**8, (received, tables),
+    )
+    first, later, out1 = call(
+        start_kernel, "start", [field, field, halo], x_scratch, 10**9, (owner, state, extras, picks, d_op), "s",
+    )
+    near, far = swap_ghosts(out1)
     first, _ = lax.optimization_barrier((first, near))
     partial1, faces = call(
         local_kernel, "local1", [field, shape(4, SLOTS, dtype=jnp.int32)], z_scratch, 10**9,
@@ -486,9 +488,9 @@
     middle, second, out2 = call(
         middle_kernel, "middle", [field, field, halo],
         x_scratch + y_scratch, 2 * 10**9,
-        (owner, near, above, below, partial1, first, later, extras, faces, picks, d_op, b_op), "s",
-    )
-    near, above, below = swap_ghosts(out2)
+        (owner, near, far, partial1, first, later, extras, faces, picks, d_op, b_op), "s",
+    )
+    near, far = swap_ghosts(out2)
     second, _ = lax.optimization_barrier((second, near))
     partial2 = call(
         local_terms, "local2", field, z_scratch, 10**9, (middle, second, extras, c_op)
@@ -496,7 +498,7 @@
     back = call(
         final_kernel, "final", shape(CHUNK, DEVS),
         [vmem(CHUNK, DEVS)] + y_scratch, 10**9,
-        (owner, near, above, below, partial2, second, extras, faces, b_op), "s",
+        (owner, near, far, partial2, second, extras, faces, b_op), "s",
     )
     returned = exchange(back, 8)
     result = call(

time: 94.2 us -> 92.9 us (0.986)
  starting transfers between devices: 18.3 us -> 13.4 us
  waiting for transfers between devices: 5.3 us -> 8.1 us
    ppermute x4 -> x2, starting transfers between devices: 5.44 us -> 0.52 us  [swap_ghosts(): return (near.reshape(256, 128), lax.ppermute(relay, 'dom', pairs))]
    ppermute x4 -> x2, waiting for transfers between devices: 0.01 us -> 2.83 us  [swap_ghosts(): return (near.reshape(256, 128), lax.ppermute(relay, 'dom', pairs))]
    pallas_call x8 -> x9, Pallas kernels: 32 us -> 31.9 us  [call(): pl.pallas_call(kernel, name=name, out_shape=outs, in_specs=[pl.BlockSpec(...]
  transfers between devices with their start and end apart: 6 -> 4, of which waited for: 1 -> 3; matrix products, arithmetic and copies ran while one was open for 0% -> 0% of each run, Pallas kernels for 12% -> 12%
where the time goes in v2:
time: 92.9 us; the launch traced here: 92.4 us
  blocking collectives  37.6 us (40%)
  Pallas kernels  31.9 us (34%)
  starting transfers between devices  13.4 us (14%)
  waiting for transfers between devices  8.1 us (9%)
  local copies, waits for them, and re-layouts  1.34 us (1%)
    pallas_call x9, Pallas kernels, call(): pl.pallas_call(kernel, name=name, out_shape=outs, in_specs=[pl.BlockSpec(...  31.9 us
    all_to_all x1, blocking collectives, exchange(): lax.all_to_all(cube, 'dom', split_axis=0, concat_axis=0, tiled=True)  19.2 us
    all_to_all x2, blocking collectives, swap_ghosts(): lax.all_to_all(cube, 'dom', split_axis=0, concat_axis=0, axis_index_group...  18.4 us
    all_to_all x1, starting transfers between devices, exchange(): lax.all_to_all(cube, 'dom', split_axis=0, concat_axis=0, tiled=True)  11.5 us
    all_to_all x1, waiting for transfers between devices, exchange(): lax.all_to_all(cube, 'dom', split_axis=0, concat_axis=0, tiled=True)  5.27 us
    ppermute x2, waiting for transfers between devices, swap_ghosts(): return (near.reshape(256, 128), lax.ppermute(relay, 'dom', pairs))  2.83 us
  transfers between devices with their start and end apart: 4, of which 3 were waited for; matrix products, arithmetic and copies ran while one was open for 0% of the time, Pallas kernels for 12%

profile of v2, /device:TPU:1, one launch (start us, length us, event | category | flops | bytes accessed | tf_op | source)
XLA Modules:
  0.0 92.4 jit_solution(1236510567255941042)
XLA Ops:
  0.0 2.6 %scatter.1 = (f32[1024,128]{1,0:T(8,128)}, s32[16,384]{1,0:T(8,128)}) custom-call(f32[9,35,256]{2,1,0:T(8,128)} %bitcast.31, f32[3,256]{1,0:T(4,128)} %jac.1, f32[4,256]{1,0:T(4,128)} %area.1, s32[1,256]{1,0:T(1,128)} %bitcast.35, s32[1,256]{1,0:T(1,128)} %bitcast.28, s32[4,384]{1,0:T(4,128)} %faces.1, s32[6,1,8]{2,1,0:T(1,128)} %bitcast.34), custom_call_target="tpu_custom_call" | custom-call | flops 100000000 | bytes 338112 | tf_op jit(solution)/shard_map/scatter/pallas_call | solution.py:396
  2.6 11.5 %all-to-all-start = ((f32[128,8,128]{2,1,0:T(8,128)}), f32[128,8,128]{2,1,0:T(8,128)S(1)}, u32[]{:S(2)}, u32[]{:S(2)}) async-start(f32[128,8,128]{2,1,0:T(8,128)} %bitcast.30), calls=%async_computation | async-start | bytes 1048576 | tf_op jit(solution)/shard_map/all_to_all | solution.py:414
  14.1 1.4 %collective-permute-start = (s32[16,384]{1,0:T(8,128)}, s32[16,384]{1,0:T(8,128)S(1)}, u32[]{:S(2)}, u32[]{:S(2)}) collective-permute-start(s32[16,384]{1,0:T(8,128)} %get-tuple-element.30), channel_id=1, source_target_pairs={{0,0},{1,1},{2,2},{3,3},{4,4},{5,5},{6,6},{7,7},{8,8},{9,9},{10,10... | collective-permute-start | bytes 73736 | tf_op jit(solution)/shard_map/ppermute | solution.py:468
  15.5 6.8 %operators.1 = (bf16[640,960]{1,0:T(8,128)(2,1)}, bf16[640,2240]{1,0:T(8,128)(2,1)}, bf16[640,1280]{1,0:T(8,128)(2,1)}) custom-call(f32[3,35,35]{2,1,0:T(8,128)} %stiffness.1, f32[35,4,35]{2,1,0:T(4,128)} %bitcast.36, f32[35,4,35]{2,1,0:T(4,128)} %bitcast.37, f32[9,3,9]{2,1,0:T(4,128)} %bitcast.38, f32[9,4,9]{2,1,0:T(4,128)} %bitcast.39, f32[9,4,9]{2,1,0:T(4,128)} %bitcast.40), custom_call_target="tpu_custom_call" | custom-call | flops 1000000000 | bytes 57464 | tf_op jit(solution)/shard_map/operators/pallas_call | solution.py:396
  22.3 0.0 collective-permute-done.tables.faces
  22.3 5.3 %all-to-all-done = f32[128,8,128]{2,1,0:T(8,128)S(1)} async-done(((f32[128,8,128]{2,1,0:T(8,128)}), f32[128,8,128]{2,1,0:T(8,128)S(1)}, u32[]{:S(2)}, u32[]{:S(2)}) %all-to-all-start) | async-done | bytes 524320 | tf_op jit(solution)/shard_map/all_to_all | solution.py:414
  27.6 0.2 unpack.1
  27.8 0.0 copy-start.3
  27.8 1.3 %copy-done.3 = bf16[640,960]{1,0:T(8,128)(2,1)S(1)} copy-done((bf16[640,960]{1,0:T(8,128)(2,1)S(1)}, bf16[640,960]{1,0:T(8,128)(2,1)}, u32[]{:S(2)}) %copy-start.3) | copy-done | bytes 1228824
  29.1 0.0 copy-start
  29.1 5.2 %start.1 = (f32[320,384]{1,0:T(8,128)S(1)}, f32[320,384]{1,0:T(8,128)S(1)}, f32[256,128]{1,0:T(8,128)S(1)}) custom-call(s32[1]{0:T(128)} %bitcast.owner, f32[320,384]{1,0:T(8,128)S(1)} %get-tuple-element.33.state, f32[8,384]{1,0:T(8,128)S(1)} %get-tuple-element.34.extras, s32[8,128]{1,0:T(8,128)S(1)} %get-tuple-element.35.picks, bf16[640,960]{1,0:T(8,128)(2,1)S(1)} %copy-done.3), custom_call_target="tpu_custom_call" | custom-call | flops 1000000000 | bytes 2965508 | tf_op jit(solution)/shard_map/start/pallas_call | solution.py:396
  34.3 8.7 %all_to_all.20 = f32[8,32,128]{2,1,0:T(8,128)S(1)} all-to-all(f32[8,32,128]{2,1,0:T(8,128)S(1)} %bitcast.27), channel_id=1, replica_groups={{0,1,2,3,4,5,6,7},{8,9,10,11,12,13,14,15},{16,17,18,19,20,21,22,23},{24..., dimensions={0} | all-to-all | bytes 262144 | tf_op jit(solution)/shard_map/all_to_all | solution.py:426
  43.1 0.5 collective-permute-start.1
  43.6 0.0 copy-done
  43.6 0.0 copy-start.2
  43.6 0.0 copy-start.4
  43.6 2.3 %local1.1 = (f32[320,384]{1,0:T(8,128)S(1)}, s32[4,384]{1,0:T(4,128)S(1)}) custom-call(f32[320,384]{1,0:T(8,128)S(1)} %get-tuple-element.33.state, f32[320,384]{1,0:T(8,128)S(1)} %get-tuple-element.41.value.first, f32[8,384]{1,0:T(8,128)S(1)} %get-tuple-element.34.extras, bf16[640,2240]{1,0:T(8,128)(2,1)S(1)} %copy-done, ...), custom_call_target="tpu_custom_call" | custom-call | flops 1000000000 | bytes 6754304 | tf_op jit(solution)/shard_map/local1/pallas_call | solution.py:396
  45.9 1.1 %collective-permute-done.1.far = f32[64,128]{1,0:T(8,128)S(1)} collective-permute-done((f32[64,128]{1,0:T(8,128)S(1)}, f32[64,128]{1,0:T(8,128)S(1)}, u32[]{:S(2)}, u32[]{:S(2)}) %collective-permute-start.1) | collective-permute-done | bytes 32800 | tf_op jit(solution)/shard_map/ppermute | solution.py:429
  47.1 0.0 copy-done.2
  47.1 0.0 copy-done.4
  47.1 8.2 %middle.1 = (f32[320,384]{1,0:T(8,128)S(1)}, f32[320,384]{1,0:T(8,128)S(1)}, f32[256,128]{1,0:T(8,128)S(1)}) custom-call(s32[1]{0:T(128)} %bitcast.owner, f32[256,128]{1,0:T(8,128)S(1)} %bitcast.24, f32[64,128]{1,0:T(8,128)S(1)} %collective-permute-done.1.far, f32[320,384]{1,0:T(8,128)S(1)} %get-tuple-element.43.partial, ...), custom_call_target="tpu_custom_call" | custom-call | flops 2000000000 | bytes 7395332 | tf_op jit(solution)/shard_map/middle/pallas_call | solution.py:396
  55.2 9.6 %all_to_all.21 = f32[8,32,128]{2,1,0:T(8,128)S(1)} all-to-all(f32[8,32,128]{2,1,0:T(8,128)S(1)} %bitcast.26), channel_id=1, replica_groups={{0,1,2,3,4,5,6,7},{8,9,10,11,12,13,14,15},{16,17,18,19,20,21,22,23},{24..., dimensions={0} | all-to-all | bytes 262144 | tf_op jit(solution)/shard_map/all_to_all | solution.py:426
  64.9 0.0 collective-permute-start.2
  64.9 2.3 %local2.1.partial = f32[320,384]{1,0:T(8,128)S(1)} custom-call(f32[320,384]{1,0:T(8,128)S(1)} %get-tuple-element.50.state, f32[320,384]{1,0:T(8,128)S(1)} %get-tuple-element.52.value.second, f32[8,384]{1,0:T(8,128)S(1)} %get-tuple-element.34.extras, bf16[640,2240]{1,0:T(8,128)(2,1)S(1)} %copy-done), custom_call_target="tpu_custom_call" | custom-call | flops 1000000000 | bytes 6729728 | tf_op jit(solution)/shard_map/local2/pallas_call | solution.py:396
  67.2 0.0 copy-start.1
  67.2 1.7 %collective-permute-done.2.far = f32[64,128]{1,0:T(8,128)S(1)} collective-permute-done((f32[64,128]{1,0:T(8,128)S(1)}, f32[64,128]{1,0:T(8,128)S(1)}, u32[]{:S(2)}, u32[]{:S(2)}) %collective-permute-start.2) | collective-permute-done | bytes 32800 | tf_op jit(solution)/shard_map/ppermute | solution.py:429
  68.9 3.0 %final.1 = f32[1024,128]{1,0:T(8,128)S(1)} custom-call(s32[1]{0:T(128)} %bitcast.owner, f32[256,128]{1,0:T(8,128)S(1)} %bitcast.25, f32[64,128]{1,0:T(8,128)S(1)} %collective-permute-done.2.far, f32[320,384]{1,0:T(8,128)S(1)} %local2.1.partial, f32[320,384]{1,0:T(8,128)S(1)} %get-tuple-element.52.value.second, f32[8,384]{1,0:T(8,128)S(1)} %get-tuple-element.34.extras, ...), custom_call_target="tpu_custom_call" | custom-call | flops 1000000000 | bytes 4442116 | tf_op jit(solution)/shard_map/final/pallas_call | solution.py:396
  71.9 19.2 %all_to_all.22 = f32[128,8,128]{2,1,0:T(8,128)S(1)} all-to-all(f32[128,8,128]{2,1,0:T(8,128)S(1)} %bitcast.23), channel_id=1, replica_groups=mesh['dom'=128] {'dom'}, dimensions={0} | all-to-all | bytes 1048576 | tf_op jit(solution)/shard_map/all_to_all | solution.py:414
  91.1 0.0 copy-done.1
  91.1 1.3 %gather.1 = f32[9,35,256]{2,1,0:T(8,128)} custom-call(f32[1024,128]{1,0:T(8,128)S(1)} %bitcast.22, s32[1,256]{1,0:T(1,128)S(1)} %bitcast.29), custom_call_target="tpu_custom_call" | custom-call | flops 100000000 | bytes 525312 | tf_op jit(solution)/shard_map/gather/pallas_call | solution.py:396
  (2 shorter events, 0.0 us)
Async XLA Ops:
  2.6 25.0 %all-to-all-start = ((f32[128,8,128]{2,1,0:T(8,128)}), f32[128,8,128]{2,1,0:T(8,128)S(1)}, u32[]{:S(2)}, u32[]{:S(2)}) async-start(f32[128,8,128]{2,1,0:T(8,128)} %bitcast.30), calls=%async_computation | async-start | bytes 1048576 | tf_op jit(solution)/shard_map/all_to_all | solution.py:414
  14.1 8.2 %collective-permute-start = (s32[16,384]{1,0:T(8,128)}, s32[16,384]{1,0:T(8,128)S(1)}, u32[]{:S(2)}, u32[]{:S(2)}) collective-permute-start(s32[16,384]{1,0:T(8,128)} %get-tuple-element.30), channel_id=1, source_target_pairs={{0,0},{1,1},{2,2},{3,3},{4,4},{5,5},{6,6},{7,7},{8,8},{9,9},{10,10... | collective-permute-start | bytes 73736 | tf_op jit(solution)/shard_map/ppermute | solution.py:468
  27.8 1.3 %copy-start.3 = (bf16[640,960]{1,0:T(8,128)(2,1)S(1)}, bf16[640,960]{1,0:T(8,128)(2,1)}, u32[]{:S(2)}) copy-start(bf16[640,960]{1,0:T(8,128)(2,1)} %get-tuple-element.36.d_op) | copy-start | bytes 3686404
  29.1 14.5 %copy-start = (bf16[640,2240]{1,0:T(8,128)(2,1)S(1)}, bf16[640,2240]{1,0:T(8,128)(2,1)}, u32[]{:S(2)}) copy-start(bf16[640,2240]{1,0:T(8,128)(2,1)} %get-tuple-element.42.c_op) | copy-start | bytes 8601604
  43.1 4.0 %collective-permute-start.1 = (f32[64,128]{1,0:T(8,128)S(1)}, f32[64,128]{1,0:T(8,128)S(1)}, u32[]{:S(2)}, u32[]{:S(2)}) collective-permute-start(f32[64,128]{1,0:T(8,128)S(1)} %bitcast.32), channel_id=1, source_target_pairs={{0,8},{1,9},{2,10},{3,11},{4,100},{5,101},{6,102},{7,103},{8,16},{... | collective-permute-start | bytes 98312 | tf_op jit(solution)/shard_map/ppermute | solution.py:429
  43.6 3.5 %copy-start.2 = (bf16[640,1280]{1,0:T(8,128)(2,1)S(1)}, bf16[640,1280]{1,0:T(8,128)(2,1)}, u32[]{:S(2)}) copy-start(bf16[640,1280]{1,0:T(8,128)(2,1)} %get-tuple-element.46.b_op) | copy-start | bytes 4915204
  43.6 3.5 %copy-start.4 = (bf16[640,960]{1,0:T(8,128)(2,1)S(1)}, bf16[640,960]{1,0:T(8,128)(2,1)}, u32[]{:S(2)}) copy-start(bf16[640,960]{1,0:T(8,128)(2,1)} %get-tuple-element.36.d_op) | copy-start | bytes 3686404
  64.9 4.0 %collective-permute-start.2 = (f32[64,128]{1,0:T(8,128)S(1)}, f32[64,128]{1,0:T(8,128)S(1)}, u32[]{:S(2)}, u32[]{:S(2)}) collective-permute-start(f32[64,128]{1,0:T(8,128)S(1)} %bitcast.33), channel_id=1, source_target_pairs={{0,8},{1,9},{2,10},{3,11},{4,100},{5,101},{6,102},{7,103},{8,16},{... | collective-permute-start | bytes 98312 | tf_op jit(solution)/shard_map/ppermute | solution.py:429
  67.2 23.9 %copy-start.1 = (s32[256]{0:T(256)S(1)}, s32[256]{0:T(256)}, u32[]{:S(2)}) copy-start(s32[256]{0:T(256)} %param.17) | copy-start | bytes 3076

commit v3 on v2

--- a/solution.py
+++ b/solution.py
@@ -58,9 +58,9 @@
 
 
 def product(op, both):
-    width = both.shape[1] // 2
-    wide = dot(op[0:ROWS, :], both[...])
-    return wide[:, 0:width] + wide[:, width:] + dot(op[ROWS:, :], both[:, 0:width])
+    depth, width = both.shape[0], both.shape[1] // 2
+    wide = dot(op[0:ROWS, 0:depth], both[...])
+    return wide[:, 0:width] + wide[:, width:] + dot(op[ROWS:, 0:depth], both[:, 0:width])
 
 
 def put(both, at, value):
@@ -70,8 +70,19 @@
     both[ROWS * at : ROWS * (at + 1), width:] = low
 
 
+PATH = (0, 1, 2, 3, 7, 11, 15, 14, 10, 6, 5, 9, 13, 12, 8, 4)
+
+
 def owner_of(device):
-    return jnp.where((device & 32) > 0, device ^ 24, device)
+    group = device >> 3
+    place = jnp.zeros_like(group)
+    for k, g in enumerate(PATH):
+        place = jnp.where(group == g, k, place)
+    return place * 8 + (device & 7)
+
+
+def device_of(owner):
+    return PATH[owner // 8] * 8 + owner % 8
 
 
 def iota(shape, dim):
@@ -115,7 +126,8 @@
     values[320:328, :] = jnp.zeros((8, BLOCK), F32)
     for q in range(QUANT):
         values[8 + MODES * q : 8 + MODES * (q + 1), :] = cells[q]
-    slot = owner_of(iota((DEVS, BLOCK), 0)) * CAP
+    half = owner_of(iota((DEVS, DEVS), 0)) * CAP
+    slot = jnp.concatenate([half, half], axis=1)
     wanted = places[...]
     stage[CAP * STRIDE :, :] = jnp.zeros((CHUNK - CAP * STRIDE, DEVS), F32)
     parts = split3(values[...])
@@ -133,7 +145,8 @@
 def gather_kernel(recv, target, out, stage):
     unpack_rows(recv, stage)
     wanted = target[...]
-    slot = owner_of(iota((DEVS, BLOCK), 0)) * CAP
+    half = owner_of(iota((DEVS, DEVS), 0)) * CAP
+    slot = jnp.concatenate([half, half], axis=1)
     total = None
     for t in range(CAP):
         part = stage[STRIDE * t + 8 : STRIDE * t + 8 + ROWS, :]
@@ -143,17 +156,7 @@
         out[q] = total[MODES * q : MODES * (q + 1), :]
 
 
-def operator_kernel(
-    stiffness, minus, plus, star, solver_minus, solver_plus, d_out, c_out, b_out,
-    k_in, m_in, p_in, s_in, sm_in, sp_in, tiles, square, columns, stage, b_op, c_op, loads, done,
-):
-    copies = fetch(
-        [
-            (stiffness, k_in), (minus, m_in), (plus, p_in), (star, s_in),
-            (solver_minus, sm_in), (solver_plus, sp_in),
-        ],
-        loads,
-    )
+def pair_codes():
     col = iota((8, 2 * ROWS), 1)
     second = jnp.where(col >= ROWS, 1, 0)
     inner = col - second * ROWS
@@ -163,49 +166,72 @@
     mode_code = jnp.where(valid, second * 128 + mode, -1)[0:1]
     quant_code = jnp.where(valid, second * 16 + quant, -512)[0:1]
     row = iota((256, 2 * ROWS), 0)
-    mode_hot = onehot(row == mode_code)
+    return row, onehot(row == mode_code), quant_code
+
+
+def expand_pairs(first, last, count, tiles, columns, codes, stage, op, ready):
+    row, mode_hot, quant_code = codes
+    flux = split2(jnp.concatenate([columns[0:128, :].T[0:16, :], columns[128:256, :].T[0:16, :]], axis=1))
+    for k in range(0, count, 2):
+        width = ROWS * min(2, count - k)
+        at = first + k
+        pair = split2(jnp.concatenate([tiles[at], tiles[min(at + 1, last)]], axis=1))
+        quant_hot = onehot(row == quant_code + 16 * at)
+        spread = dot(pair[0], mode_hot) + dot(pair[1], mode_hot)
+        scale = dot(flux[0], quant_hot) + dot(flux[1], quant_hot)
+        for p in range(QUANT):
+            stage[MODES * p : MODES * (p + 1), 0:width] = spread[0:MODES, 0:width] * scale[p : p + 1, 0:width]
+        high, low = split2(stage[:, 0:width])
+        op[0:ROWS, ROWS * k : ROWS * k + width] = high
+        op[ROWS:, ROWS * k : ROWS * k + width] = low
+        ready(slice(ROWS * k, ROWS * k + -(-width // 128) * 128))
+
+
+def taylor_operator_kernel(stiffness, star, op, tiles, square, columns, stage):
     tiles[...] = jnp.zeros(tiles.shape, F32)
     square[...] = jnp.zeros(square.shape, F32)
     columns[...] = jnp.zeros(columns.shape, F32)
+    stage[FEAT:ROWS, :] = jnp.zeros((ROWS - FEAT, stage.shape[1]), F32)
+    for c in range(3):
+        square[0:MODES, 0:MODES] = -stiffness[c]
+        tiles[c] = square[...].T[0:48, :]
+        columns[16 * c : 16 * c + QUANT, 0:QUANT] = star[:, c, :]
+    expand_pairs(0, 2, 3, tiles, columns, pair_codes(), stage, op, lambda lanes: None)
+
+
+def operator_kernel(
+    stiffness, minus, plus, star, solver_minus, solver_plus, c_out, b_out,
+    k_in, m_in, p_in, s_in, sm_in, sp_in, tiles, columns, stage, c_op, b_op, loads, done,
+):
+    copies = fetch(
+        [
+            (stiffness, k_in), (minus, m_in), (plus, p_in), (star, s_in),
+            (solver_minus, sm_in), (solver_plus, sp_in),
+        ],
+        loads,
+    )
+    codes = pair_codes()
+    tiles[...] = jnp.zeros(tiles.shape, F32)
+    columns[...] = jnp.zeros(columns.shape, F32)
+    stage[FEAT:ROWS, :] = jnp.zeros((ROWS - FEAT, stage.shape[1]), F32)
     for copy in copies:
         copy.wait()
     for c in range(3):
-        square[0:MODES, 0:MODES] = -k_in[c]
-        tiles[c] = square[...].T[0:48, :]
-        tiles[3 + c, 0:MODES, 0:MODES] = k_in[c]
+        tiles[c, 0:MODES, 0:MODES] = k_in[c]
         columns[16 * c : 16 * c + QUANT, 0:QUANT] = s_in[:, c, :]
-        columns[16 * (3 + c) : 16 * (3 + c) + QUANT, 0:QUANT] = s_in[:, c, :]
     for f in range(4):
-        tiles[6 + f, 0:MODES, 0:MODES] = -m_in[:, f, :]
-        tiles[10 + f, 0:MODES, 0:MODES] = -p_in[:, f, :]
-        columns[16 * (6 + f) : 16 * (6 + f) + QUANT, 0:QUANT] = sm_in[:, f, :]
-        columns[16 * (10 + f) : 16 * (10 + f) + QUANT, 0:QUANT] = sp_in[:, f, :]
-    flux = split2(jnp.concatenate([columns[0:128, :].T[0:16, :], columns[128:256, :].T[0:16, :]], axis=1))
-
-    def family(first, count, out):
-        stage[FEAT:ROWS, :] = jnp.zeros((ROWS - FEAT, stage.shape[1]), F32)
-        for k in range(0, count, 2):
-            width = ROWS * min(2, count - k)
-            at = first + k
-            after = min(at + 1, 13)
-            pair = split2(jnp.concatenate([tiles[at], tiles[after]], axis=1))
-            quant_hot = onehot(row == quant_code + 16 * at)
-            spread = dot(pair[0], mode_hot) + dot(pair[1], mode_hot)
-            scale = dot(flux[0], quant_hot) + dot(flux[1], quant_hot)
-            for p in range(QUANT):
-                stage[MODES * p : MODES * (p + 1), ROWS * k : ROWS * k + width] = (
-                    spread[0:MODES, 0:width] * scale[p : p + 1, 0:width]
-                )
-        a_high, a_low = split2(stage[:, 0 : ROWS * count])
-        out[0:ROWS, :] = a_high
-        out[ROWS:, :] = a_low
-
-    family(3, 7, c_op)
-    copies = fetch([(c_op, c_out)], done)
-    family(10, 4, b_op)
-    copies += fetch([(b_op, b_out)], done, 1)
-    family(0, 3, d_out)
-    for copy in copies:
+        tiles[3 + f, 0:MODES, 0:MODES] = -m_in[:, f, :]
+        tiles[7 + f, 0:MODES, 0:MODES] = -p_in[:, f, :]
+        columns[16 * (3 + f) : 16 * (3 + f) + QUANT, 0:QUANT] = sm_in[:, f, :]
+        columns[16 * (7 + f) : 16 * (7 + f) + QUANT, 0:QUANT] = sp_in[:, f, :]
+    sent = []
+
+    def leave(op, out):
+        return lambda lanes: sent.extend(fetch([(op.at[:, lanes], out.at[:, lanes])], done, len(sent)))
+
+    expand_pairs(0, 10, 7, tiles, columns, codes, stage, c_op, leave(c_op, c_out))
+    expand_pairs(7, 10, 4, tiles, columns, codes, stage, b_op, leave(b_op, b_out))
+    for copy in sent:
         copy.wait()
 
 
@@ -414,10 +440,6 @@
     return lax.all_to_all(cube, "dom", split_axis=0, concat_axis=0, tiled=True).reshape(DEVS * per, 128)
 
 
-def device_of(owner):
-    return owner ^ 24 if owner & 32 else owner
-
-
 def swap_ghosts(rows):
     groups = [list(range(8 * k, 8 * k + 8)) for k in range(DEVS // 8)]
     first = jnp.where((lax.axis_index("dom") & 4) == 0, 4, 0).astype(jnp.uint32)
@@ -450,19 +472,25 @@
     )
     received = exchange(sent, 8)
 
-    d_op, c_op, b_op = call(
+    star, minus, plus, solve_minus, solve_plus = [
+        jnp.transpose(a, (1, 0, 2)) for a in (star_matrix, face_minus, face_plus, solver_minus, solver_plus)
+    ]
+    c_op, b_op = call(
         operator_kernel, "operators",
-        [shape(2 * ROWS, k * ROWS, dtype=BF16) for k in (3, 7, 4)],
+        [shape(2 * ROWS, w, dtype=BF16) for w in (2304, 1280)],
         [
             vmem(3, MODES, MODES), vmem(MODES, 4, MODES), vmem(MODES, 4, MODES),
             vmem(QUANT, 3, QUANT), vmem(QUANT, 4, QUANT), vmem(QUANT, 4, QUANT),
-            vmem(14, 48, 128), vmem(128, 128), vmem(256, 128), vmem(ROWS, 7 * ROWS),
-            vmem(2 * ROWS, 4 * ROWS, dtype=BF16), vmem(2 * ROWS, 7 * ROWS, dtype=BF16),
-            pltpu.SemaphoreType.DMA((6,)), pltpu.SemaphoreType.DMA((2,)),
+            vmem(11, 48, 128), vmem(256, 128), vmem(ROWS, 2 * ROWS), vmem(2 * ROWS, 2304, dtype=BF16),
+            vmem(2 * ROWS, 1280, dtype=BF16), pltpu.SemaphoreType.DMA((6,)), pltpu.SemaphoreType.DMA((6,)),
         ],
-        10**9,
-        (stiffness, *[jnp.transpose(a, (1, 0, 2)) for a in (face_minus, face_plus, star_matrix, solver_minus, solver_plus)]),
-        "hhhhhh", "vhh", FULL - 1900 * 1024,
+        10**9, (stiffness, minus, plus, star, solve_minus, solve_plus), "hhhhhh", "hh", FULL - 1900 * 1024,
+    )
+    stiffness, star, _ = lax.optimization_barrier((stiffness, star, b_op))
+    d_op = call(
+        taylor_operator_kernel, "taylor_operators", shape(2 * ROWS, 960, dtype=BF16),
+        [vmem(3, 48, 128), vmem(128, 128), vmem(256, 128), vmem(ROWS, 2 * ROWS)],
+        10**9, (stiffness, star),
     )
     home = [(o, device_of(o)) for o in range(DEVS)]
     tables = lax.ppermute(tables, "dom", home)

time: 92.9 us -> 89.8 us (0.967)
  waiting for transfers between devices: 8.1 us -> 6.39 us
  local copies, waits for them, and re-layouts: 1.34 us -> 0.03 us
  Pallas kernels: 31.9 us -> 30.7 us
    ppermute x2, waiting for transfers between devices: 2.83 us -> 0.04 us  [swap_ghosts(): return (near.reshape(256, 128), lax.ppermute(relay, 'dom', pairs))]
    unnamed x10, local copies, waits for them, and re-layouts: 1.33 us -> 0.02 us
    pallas_call x9 -> x10, Pallas kernels: 31.9 us -> 30.7 us  [call(): pl.pallas_call(kernel, name=name, out_shape=outs, in_specs=[pl.BlockSpec(...]
    all_to_all x1, waiting for transfers between devices: 5.27 us -> 6.35 us  [exchange(): lax.all_to_all(cube, 'dom', split_axis=0, concat_axis=0, tiled=True)]
  transfers between devices with their start and end apart: 4 -> 4, of which waited for: 3 -> 1; matrix products, arithmetic and copies ran while one was open for 0% -> 0% of each run, Pallas kernels for 12% -> 11%
where the time goes in v3:
time: 89.8 us; the launch traced here: 89.4 us
  blocking collectives  38.3 us (43%)
  Pallas kernels  30.7 us (34%)
  starting transfers between devices  13.9 us (15%)
  waiting for transfers between devices  6.39 us (7%)
    pallas_call x10, Pallas kernels, call(): pl.pallas_call(kernel, name=name, out_shape=outs, in_specs=[pl.BlockSpec(...  30.7 us
    all_to_all x1, blocking collectives, exchange(): lax.all_to_all(cube, 'dom', split_axis=0, concat_axis=0, tiled=True)  19.9 us
    all_to_all x2, blocking collectives, swap_ghosts(): lax.all_to_all(cube, 'dom', split_axis=0, concat_axis=0, axis_index_group...  18.3 us
    all_to_all x1, starting transfers between devices, exchange(): lax.all_to_all(cube, 'dom', split_axis=0, concat_axis=0, tiled=True)  11.5 us
    all_to_all x1, waiting for transfers between devices, exchange(): lax.all_to_all(cube, 'dom', split_axis=0, concat_axis=0, tiled=True)  6.35 us
  transfers between devices with their start and end apart: 4, of which 1 were waited for; matrix products, arithmetic and copies ran while one was open for 0% of the time, Pallas kernels for 11%

profile of v3, /device:TPU:1, one launch (start us, length us, event | category | flops | bytes accessed | tf_op | source)
XLA Modules:
  0.0 89.4 jit_solution(16560472198493590781)
XLA Ops:
  0.0 2.6 %scatter.1 = (f32[1024,128]{1,0:T(8,128)}, s32[16,384]{1,0:T(8,128)}) custom-call(f32[9,35,256]{2,1,0:T(8,128)} %bitcast.33, f32[3,256]{1,0:T(4,128)} %jac.1, f32[4,256]{1,0:T(4,128)} %area.1, s32[1,256]{1,0:T(1,128)} %bitcast.37, s32[1,256]{1,0:T(1,128)} %bitcast.28, s32[4,384]{1,0:T(4,128)} %faces.1, s32[6,1,8]{2,1,0:T(1,128)} %bitcast.36), custom_call_target="tpu_custom_call" | custom-call | flops 100000000 | bytes 338112 | tf_op jit(solution)/shard_map/scatter/pallas_call | solution.py:422
  2.6 11.5 %all-to-all-start = ((f32[128,8,128]{2,1,0:T(8,128)}), f32[128,8,128]{2,1,0:T(8,128)S(1)}, u32[]{:S(2)}, u32[]{:S(2)}) async-start(f32[128,8,128]{2,1,0:T(8,128)} %bitcast.32), calls=%async_computation | async-start | bytes 1048576 | tf_op jit(solution)/shard_map/all_to_all | solution.py:440
  14.1 1.4 %collective-permute-start = (s32[16,384]{1,0:T(8,128)}, s32[16,384]{1,0:T(8,128)S(1)}, u32[]{:S(2)}, u32[]{:S(2)}) collective-permute-start(s32[16,384]{1,0:T(8,128)} %get-tuple-element.31), channel_id=1, source_target_pairs={{0,0},{1,1},{2,2},{3,3},{4,4},{5,5},{6,6},{7,7},{8,8},{9,9},{10,10... | collective-permute-start | bytes 73736 | tf_op jit(solution)/shard_map/ppermute | solution.py:496
  15.5 0.0 copy-start.2
  15.5 0.0 copy-start.3
  15.5 4.7 %operators.1 = (bf16[640,2304]{1,0:T(8,128)(2,1)}, bf16[640,1280]{1,0:T(8,128)(2,1)}) custom-call(f32[3,35,35]{2,1,0:T(8,128)} %stiffness.2, f32[35,4,35]{2,1,0:T(4,128)} %bitcast.38, f32[35,4,35]{2,1,0:T(4,128)} %bitcast.39, f32[9,3,9]{2,1,0:T(4,128)} %bitcast.30, f32[9,4,9]{2,1,0:T(4,128)} %bitcast.40, f32[9,4,9]{2,1,0:T(4,128)} %bitcast.41), custom_call_target="tpu_custom_call" | custom-call | flops 1000000000 | bytes 57464 | tf_op jit(solution)/shard_map/operators/pallas_call | solution.py:422
  20.3 0.0 copy-done.2
  20.3 0.0 copy-done.3
  20.3 1.0 %taylor_operators.1.d_op = bf16[640,960]{1,0:T(8,128)(2,1)S(1)} custom-call(f32[3,35,35]{2,1,0:T(8,128)S(1)} %copy-done.2, f32[9,3,9]{2,1,0:T(4,128)S(1)} %bitcast.31), custom_call_target="tpu_custom_call" | custom-call | flops 1000000000 | bytes 15672 | tf_op jit(solution)/shard_map/taylor_operators/pallas_call | solution.py:422
  21.2 0.0 collective-permute-done.tables.faces
  21.3 6.4 %all-to-all-done = f32[128,8,128]{2,1,0:T(8,128)S(1)} async-done(((f32[128,8,128]{2,1,0:T(8,128)}), f32[128,8,128]{2,1,0:T(8,128)S(1)}, u32[]{:S(2)}, u32[]{:S(2)}) %all-to-all-start) | async-done | bytes 524320 | tf_op jit(solution)/shard_map/all_to_all | solution.py:440
  27.6 0.2 unpack.1
  27.8 0.0 copy-start
  27.8 5.2 %start.1 = (f32[320,384]{1,0:T(8,128)S(1)}, f32[320,384]{1,0:T(8,128)S(1)}, f32[256,128]{1,0:T(8,128)S(1)}) custom-call(s32[1]{0:T(128)} %bitcast.owner, f32[320,384]{1,0:T(8,128)S(1)} %get-tuple-element.34.state, f32[8,384]{1,0:T(8,128)S(1)} %get-tuple-element.35.extras, s32[8,128]{1,0:T(8,128)S(1)} %get-tuple-element.36.picks, ...), custom_call_target="tpu_custom_call" | custom-call | flops 1000000000 | bytes 2965508 | tf_op jit(solution)/shard_map/start/pallas_call | solution.py:422
  33.0 8.7 %all_to_all.20 = f32[8,32,128]{2,1,0:T(8,128)S(1)} all-to-all(f32[8,32,128]{2,1,0:T(8,128)S(1)} %bitcast.27), channel_id=1, replica_groups={{0,1,2,3,4,5,6,7},{8,9,10,11,12,13,14,15},{16,17,18,19,20,21,22,23},{24..., dimensions={0} | all-to-all | bytes 262144 | tf_op jit(solution)/shard_map/all_to_all | solution.py:448
  41.8 0.5 collective-permute-start.1
  42.3 0.0 copy-done
  42.3 0.0 copy-start.4
  42.3 2.3 %local1.1 = (f32[320,384]{1,0:T(8,128)S(1)}, s32[4,384]{1,0:T(4,128)S(1)}) custom-call(f32[320,384]{1,0:T(8,128)S(1)} %get-tuple-element.34.state, f32[320,384]{1,0:T(8,128)S(1)} %get-tuple-element.44.value.first, f32[8,384]{1,0:T(8,128)S(1)} %get-tuple-element.35.extras, bf16[640,2304]{1,0:T(8,128)(2,1)S(1)} %copy-done, ...), custom_call_target="tpu_custom_call" | custom-call | flops 1000000000 | bytes 6918144 | tf_op jit(solution)/shard_map/local1/pallas_call | solution.py:422
  44.6 0.0 collective-permute-done.1.far
  44.6 0.0 copy-done.4
  44.6 8.1 %middle.1 = (f32[320,384]{1,0:T(8,128)S(1)}, f32[320,384]{1,0:T(8,128)S(1)}, f32[256,128]{1,0:T(8,128)S(1)}) custom-call(s32[1]{0:T(128)} %bitcast.owner, f32[256,128]{1,0:T(8,128)S(1)} %bitcast.24, f32[64,128]{1,0:T(8,128)S(1)} %collective-permute-done.1.far, f32[320,384]{1,0:T(8,128)S(1)} %get-tuple-element.46.partial, ...), custom_call_target="tpu_custom_call" | custom-call | flops 2000000000 | bytes 7395332 | tf_op jit(solution)/shard_map/middle/pallas_call | solution.py:422
  52.7 9.6 %all_to_all.21 = f32[8,32,128]{2,1,0:T(8,128)S(1)} all-to-all(f32[8,32,128]{2,1,0:T(8,128)S(1)} %bitcast.26), channel_id=1, replica_groups={{0,1,2,3,4,5,6,7},{8,9,10,11,12,13,14,15},{16,17,18,19,20,21,22,23},{24..., dimensions={0} | all-to-all | bytes 262144 | tf_op jit(solution)/shard_map/all_to_all | solution.py:448
  62.3 0.5 collective-permute-start.2
  62.8 2.2 %local2.1.partial = f32[320,384]{1,0:T(8,128)S(1)} custom-call(f32[320,384]{1,0:T(8,128)S(1)} %get-tuple-element.52.state, f32[320,384]{1,0:T(8,128)S(1)} %get-tuple-element.54.value.second, f32[8,384]{1,0:T(8,128)S(1)} %get-tuple-element.35.extras, bf16[640,2304]{1,0:T(8,128)(2,1)S(1)} %copy-done), custom_call_target="tpu_custom_call" | custom-call | flops 1000000000 | bytes 6893568 | tf_op jit(solution)/shard_map/local2/pallas_call | solution.py:422
  65.0 0.0 copy-start.1
  65.0 0.0 collective-permute-done.2.far
  65.0 3.0 %final.1 = f32[1024,128]{1,0:T(8,128)S(1)} custom-call(s32[1]{0:T(128)} %bitcast.owner, f32[256,128]{1,0:T(8,128)S(1)} %bitcast.25, f32[64,128]{1,0:T(8,128)S(1)} %collective-permute-done.2.far, f32[320,384]{1,0:T(8,128)S(1)} %local2.1.partial, f32[320,384]{1,0:T(8,128)S(1)} %get-tuple-element.54.value.second, f32[8,384]{1,0:T(8,128)S(1)} %get-tuple-element.35.extras, ...), custom_call_target="tpu_custom_call" | custom-call | flops 1000000000 | bytes 4442116 | tf_op jit(solution)/shard_map/final/pallas_call | solution.py:422
  68.1 19.9 %all_to_all.22 = f32[128,8,128]{2,1,0:T(8,128)S(1)} all-to-all(f32[128,8,128]{2,1,0:T(8,128)S(1)} %bitcast.23), channel_id=1, replica_groups=mesh['dom'=128] {'dom'}, dimensions={0} | all-to-all | bytes 1048576 | tf_op jit(solution)/shard_map/all_to_all | solution.py:440
  88.0 0.0 copy-done.1
  88.0 1.4 %gather.1 = f32[9,35,256]{2,1,0:T(8,128)} custom-call(f32[1024,128]{1,0:T(8,128)S(1)} %bitcast.22, s32[1,256]{1,0:T(1,128)S(1)} %bitcast.29), custom_call_target="tpu_custom_call" | custom-call | flops 100000000 | bytes 525312 | tf_op jit(solution)/shard_map/gather/pallas_call | solution.py:422
  (2 shorter events, 0.0 us)
Async XLA Ops:
  2.6 25.0 %all-to-all-start = ((f32[128,8,128]{2,1,0:T(8,128)}), f32[128,8,128]{2,1,0:T(8,128)S(1)}, u32[]{:S(2)}, u32[]{:S(2)}) async-start(f32[128,8,128]{2,1,0:T(8,128)} %bitcast.32), calls=%async_computation | async-start | bytes 1048576 | tf_op jit(solution)/shard_map/all_to_all | solution.py:440
  14.1 7.1 %collective-permute-start = (s32[16,384]{1,0:T(8,128)}, s32[16,384]{1,0:T(8,128)S(1)}, u32[]{:S(2)}, u32[]{:S(2)}) collective-permute-start(s32[16,384]{1,0:T(8,128)} %get-tuple-element.31), channel_id=1, source_target_pairs={{0,0},{1,1},{2,2},{3,3},{4,4},{5,5},{6,6},{7,7},{8,8},{9,9},{10,10... | collective-permute-start | bytes 73736 | tf_op jit(solution)/shard_map/ppermute | solution.py:496
  15.5 4.7 %copy-start.2 = (f32[3,35,35]{2,1,0:T(8,128)S(1)}, f32[3,35,35]{2,1,0:T(8,128)}, u32[]{:S(2)}) copy-start(f32[3,35,35]{2,1,0:T(8,128)} %stiffness.2) | copy-start | bytes 44104
  15.5 4.7 %copy-start.3 = (f32[3,9,9]{2,0,1:T(4,128)S(1)}, f32[3,9,9]{2,0,1:T(4,128)}, u32[]{:S(2)}) copy-start(f32[3,9,9]{2,0,1:T(4,128)} %param.21) | copy-start | bytes 2920
  27.8 14.5 %copy-start = (bf16[640,2304]{1,0:T(8,128)(2,1)S(1)}, bf16[640,2304]{1,0:T(8,128)(2,1)}, u32[]{:S(2)}) copy-start(bf16[640,2304]{1,0:T(8,128)(2,1)} %get-tuple-element.45.c_op) | copy-start | bytes 8847364
  41.8 2.8 %collective-permute-start.1 = (f32[64,128]{1,0:T(8,128)S(1)}, f32[64,128]{1,0:T(8,128)S(1)}, u32[]{:S(2)}, u32[]{:S(2)}) collective-permute-start(f32[64,128]{1,0:T(8,128)S(1)} %bitcast.34), channel_id=1, source_target_pairs={{0,8},{1,9},{2,10},{3,11},{4,36},{5,37},{6,38},{7,39},{8,16},{9,17... | collective-permute-start | bytes 98312 | tf_op jit(solution)/shard_map/ppermute | solution.py:451
  42.3 2.3 %copy-start.4 = (bf16[640,1280]{1,0:T(8,128)(2,1)S(1)}, bf16[640,1280]{1,0:T(8,128)(2,1)}, u32[]{:S(2)}) copy-start(bf16[640,1280]{1,0:T(8,128)(2,1)} %get-tuple-element.37.b_op) | copy-start | bytes 4915204
  62.3 2.8 %collective-permute-start.2 = (f32[64,128]{1,0:T(8,128)S(1)}, f32[64,128]{1,0:T(8,128)S(1)}, u32[]{:S(2)}, u32[]{:S(2)}) collective-permute-start(f32[64,128]{1,0:T(8,128)S(1)} %bitcast.35), channel_id=1, source_target_pairs={{0,8},{1,9},{2,10},{3,11},{4,36},{5,37},{6,38},{7,39},{8,16},{9,17... | collective-permute-start | bytes 98312 | tf_op jit(solution)/shard_map/ppermute | solution.py:451
  65.0 23.0 %copy-start.1 = (s32[256]{0:T(256)S(1)}, s32[256]{0:T(256)}, u32[]{:S(2)}) copy-start(s32[256]{0:T(256)} %param.17) | copy-start | bytes 3076

commit v4 on v3

--- a/solution.py
+++ b/solution.py
@@ -21,6 +21,7 @@
 GHOSTS = 6
 NEIGH = 8
 STEPS = (1, -1, 2, -2, 3, -3, 4, -4)
+SENT = (1, -1, 3, -3, 2, -2, 4, -4)
 F32 = jnp.float32
 BF16 = jnp.bfloat16
 FULL = 67043328
@@ -78,11 +79,13 @@
     place = jnp.zeros_like(group)
     for k, g in enumerate(PATH):
         place = jnp.where(group == g, k, place)
-    return place * 8 + (device & 7)
+    inner = device & 7
+    return place * 8 + jnp.where((place & 1) > 0, inner ^ 6, inner)
 
 
 def device_of(owner):
-    return PATH[owner // 8] * 8 + owner % 8
+    group = owner // 8
+    return PATH[group] * 8 + (owner % 8 ^ (6 if group % 2 else 0))
 
 
 def iota(shape, dim):
@@ -104,7 +107,7 @@
 
 
 def scatter_kernel(
-    modal, jac, area, cluster, target, faces, listed, out, tables, cells, values, stage, kinds, places, lists, done
+    core, modal, jac, area, cluster, target, faces, listed, out, tables, cells, values, stage, kinds, places, lists, done
 ):
     copies = [
         pltpu.make_async_copy(modal, cells, done.at[0]),
@@ -119,6 +122,7 @@
         copy.start()
     for copy in copies:
         copy.wait()
+    tables[4:8, :] = jnp.full((4, SLOTS), core[0], jnp.int32)
     tables[8:16, :] = jnp.zeros((8, SLOTS), jnp.int32)
     for i in range(GHOSTS):
         tables[8 + i : 9 + i, 0:NEIGH] = lists[i]
@@ -279,8 +283,7 @@
     picks[4:5, :] = choose((5, 6))
 
 
-def send_ghosts(value, picks, owner, out):
-    out[...] = jnp.zeros(out.shape, F32)
+def send_ghosts(value, picks, odd, even):
     slot = iota((SLOTS, 128), 0)
     slot = (slot & 127) * CAP + (slot >> 7)
     base = onehot(slot == picks[0:1, :])
@@ -289,25 +292,38 @@
     tail = dot3(value[256:320, :], rest)
     first = (main[0:128, :] + jnp.concatenate([tail[:, 0:128], tail[:, 128:256]], axis=0)).T
     second = (main[128:256, :] + jnp.concatenate([tail[:, 256:384], tail[:, 384:512]], axis=0)).T
-    spot = owner & 7
     for b, step in enumerate(STEPS):
-        goal = spot + step
-        outside = jnp.where((goal < 0) | (goal > 7), 16, 0)
-        place = ((goal + 8) & 7) * 32 + outside
-        out[pl.ds(pl.multiple_of(place, 16), 8), :] = first[8 * b : 8 * b + 8, :]
-        out[pl.ds(pl.multiple_of(place + 8, 8), 8), :] = second[8 * b : 8 * b + 8, :]
-
-
-def read_ghosts(near, far, owner):
+        out = odd if step % 2 else even
+        place = 16 * (SENT.index(step) % 4)
+        out[place : place + 8, :] = first[8 * b : 8 * b + 8, :]
+        out[place + 8 : place + 16, :] = second[8 * b : 8 * b + 8, :]
+
+
+def relay_kernel(even, twin, up, down, far_up, far_down):
+    def piece(rows, step):
+        place = 16 * (SENT.index(step) % 4)
+        return rows[place : place + 16, :]
+
+    for out, sign in ((up, 1), (down, -1)):
+        out[0:16, :] = piece(even, 2 * sign)
+        out[16:32, :] = piece(twin, sign)
+        out[32:48, :] = piece(twin, 3 * sign)
+    for out, sign in ((far_up, 1), (far_down, -1)):
+        out[0:16, :] = piece(even, 4 * sign)
+        out[16:32, :] = piece(twin, 3 * sign)
+
+
+def read_ghosts(twin, up, down, far_up, far_down, core):
+    even = core == 0
+    places = {
+        2: (up, 0, up, 0), -2: (down, 0, down, 0), 4: (far_up, 0, far_up, 0), -4: (far_down, 0, far_down, 0),
+        1: (up, 16, twin, 0), -1: (twin, 16, down, 16), 3: (far_up, 16, up, 32), -3: (down, 32, far_down, 16),
+    }
     firsts, seconds = [], []
-    spot = owner & 7
     for step in STEPS:
-        origin = spot - step
-        inside = (origin >= 0) & (origin <= 7)
-        place = pl.multiple_of(((origin + 8) & 7) * 32, 32)
-        other = pl.multiple_of((origin & 3) * 16, 16)
-        firsts.append(jnp.where(inside, near[pl.ds(place, 8), :], far[pl.ds(other, 8), :]))
-        seconds.append(jnp.where(inside, near[pl.ds(place + 8, 8), :], far[pl.ds(other + 8, 8), :]))
+        a, i, b, j = places[step]
+        firsts.append(jnp.where(even, a[i : i + 8, :], b[j : j + 8, :]))
+        seconds.append(jnp.where(even, a[i + 8 : i + 16, :], b[j + 8 : j + 16, :]))
     blank = jnp.zeros((64, 128), F32)
     first = jnp.concatenate(firsts + [blank], axis=0).T
     second = jnp.concatenate(seconds + [blank], axis=0).T
@@ -364,13 +380,13 @@
         state[:, 128 * t : 128 * (t + 1)] = stage[STRIDE * t + 8 : STRIDE * t + 8 + ROWS, :]
 
 
-def start_kernel(owner, state, extras, picks, d_op, first, later, ghosts, one_piece, other_piece):
+def start_kernel(state, extras, picks, d_op, first, later, odd, even, one_piece, other_piece):
     one, two = taylor(
         state[...], extras, d_op, (one_piece, other_piece), [weights_of(0.0, 1.0), weights_of(1.0, 2.0)]
     )
     first[...] = one
     later[...] = two
-    send_ghosts(first, picks, owner[0], ghosts)
+    send_ghosts(first, picks, odd, even)
 
 
 def local_kernel(state, value, extras, c_op, faces, out, order, both):
@@ -386,21 +402,21 @@
 
 
 def middle_kernel(
-    owner, near, far, partial, first, later, extras, faces, picks, d_op, b_op,
-    middle, second, ghosts, one_piece, other_piece, wide,
+    core, twin, up, down, far_up, far_down, partial, first, later, extras, faces, picks, d_op, b_op,
+    middle, second, odd, even, one_piece, other_piece, wide,
 ):
-    table = read_ghosts(near, far, owner[0])
+    table = read_ghosts(twin, up, down, far_up, far_down, core[0])
     flux = remote_flux(first[...], table, extras, faces, b_op, wide)
     middle[...] = partial[...] + occupied(extras) * flux
     (fresh,) = taylor(middle[...], extras, d_op, (one_piece, other_piece), [weights_of(0.0, 1.0)])
     second[...] = jnp.where(extras[7:8, :] > 1.5, later[...], fresh)
-    send_ghosts(second, picks, owner[0], ghosts)
+    send_ghosts(second, picks, odd, even)
 
 
 def final_kernel(
-    owner, near, far, partial, second, extras, faces, b_op, out, stage, wide
+    core, twin, up, down, far_up, far_down, partial, second, extras, faces, b_op, out, stage, wide
 ):
-    table = read_ghosts(near, far, owner[0])
+    table = read_ghosts(twin, up, down, far_up, far_down, core[0])
     flux = remote_flux(second[...], table, extras, faces, b_op, wide)
     final = partial[...] + occupied(extras) * flux
     stage[...] = jnp.zeros((CHUNK, DEVS), F32)
@@ -440,22 +456,25 @@
     return lax.all_to_all(cube, "dom", split_axis=0, concat_axis=0, tiled=True).reshape(DEVS * per, 128)
 
 
-def swap_ghosts(rows):
-    groups = [list(range(8 * k, 8 * k + 8)) for k in range(DEVS // 8)]
-    first = jnp.where((lax.axis_index("dom") & 4) == 0, 4, 0).astype(jnp.uint32)
-    rows, first = lax.optimization_barrier((rows, first))
-    cube = rows.reshape(8, 32, 128)
-    near = lax.all_to_all(cube, "dom", split_axis=0, concat_axis=0, axis_index_groups=groups, tiled=True)
-    relay = lax.dynamic_slice(near, (first, jnp.uint32(16), jnp.uint32(0)), (4, 16, 128)).reshape(64, 128)
-    pairs = [(device_of(o), device_of((o + (8 if o & 4 == 0 else -8)) % DEVS)) for o in range(DEVS)]
-    return near.reshape(256, 128), lax.ppermute(relay, "dom", pairs)
+def swap_ghosts(odd, even, value):
+    def move(part, shift):
+        pairs = [(device_of(o), device_of((o + shift) % DEVS)) for o in range(DEVS)]
+        return lax.ppermute(part, "dom", pairs)
+
+    twins = [(device_of(o), device_of(o ^ 1)) for o in range(DEVS)]
+    twin = lax.ppermute(odd, "dom", twins)
+    parts = call(
+        relay_kernel, "relay", [shape(48, 128), shape(48, 128), shape(32, 128), shape(32, 128)], [], 10**6, (even, twin)
+    )
+    value, parts = lax.optimization_barrier((value, parts))
+    return (twin, *[move(part, shift) for part, shift in zip(parts, (2, -2, 4, -4))]), value
 
 
 def local(
     modal_dofs, jacobian, face_area, cluster_id, target_slot, ghost_slots, face_neighbours,
     stiffness, star_matrix, face_minus, face_plus, solver_minus, solver_plus,
 ):
-    owner = lax.axis_index("dom").astype(jnp.int32).reshape(1)
+    core = (lax.axis_index("dom").astype(jnp.int32) & 1).reshape(1)
     target = target_slot.reshape(1, BLOCK)
     sent, tables = call(
         scatter_kernel, "scatter", [shape(CHUNK, DEVS), shape(16, SLOTS, dtype=jnp.int32)],
@@ -465,10 +484,10 @@
         ],
         10**8,
         (
-            jnp.transpose(modal_dofs, (1, 0, 2)), jacobian, face_area, cluster_id.reshape(1, BLOCK), target,
+            core, jnp.transpose(modal_dofs, (1, 0, 2)), jacobian, face_area, cluster_id.reshape(1, BLOCK), target,
             face_neighbours, jnp.transpose(ghost_slots, (2, 0, 1)),
         ),
-        "hhhhhhh", "", FULL,
+        "shhhhhhh", "", FULL,
     )
     received = exchange(sent, 8)
 
@@ -499,34 +518,32 @@
     y_scratch = [vmem(4 * ROWS, 2 * SLOTS, dtype=BF16)]
     z_scratch = [vmem(7 * ROWS, 2 * SLOTS, dtype=BF16)]
     field = shape(ROWS, SLOTS)
-    halo = shape(8 * 32, 128)
+    halo = [shape(64, 128)] * 2
     state, extras, picks = call(
         unpack_kernel, "unpack", [field, shape(8, SLOTS), shape(8, 128, dtype=jnp.int32)],
         [vmem(CHUNK, DEVS)], 10**8, (received, tables),
     )
-    first, later, out1 = call(
-        start_kernel, "start", [field, field, halo], x_scratch, 10**9, (owner, state, extras, picks, d_op), "s",
-    )
-    near, far = swap_ghosts(out1)
-    first, _ = lax.optimization_barrier((first, near))
+    first, later, odd, even = call(
+        start_kernel, "start", [field, field, *halo], x_scratch, 10**9, (state, extras, picks, d_op),
+    )
+    ghosts, first = swap_ghosts(odd, even, first)
     partial1, faces = call(
         local_kernel, "local1", [field, shape(4, SLOTS, dtype=jnp.int32)], z_scratch, 10**9,
         (state, first, extras, c_op, tables),
     )
-    middle, second, out2 = call(
-        middle_kernel, "middle", [field, field, halo],
+    middle, second, odd, even = call(
+        middle_kernel, "middle", [field, field, *halo],
         x_scratch + y_scratch, 2 * 10**9,
-        (owner, near, far, partial1, first, later, extras, faces, picks, d_op, b_op), "s",
-    )
-    near, far = swap_ghosts(out2)
-    second, _ = lax.optimization_barrier((second, near))
+        (core, *ghosts, partial1, first, later, extras, faces, picks, d_op, b_op), "s",
+    )
+    ghosts, second = swap_ghosts(odd, even, second)
     partial2 = call(
         local_terms, "local2", field, z_scratch, 10**9, (middle, second, extras, c_op)
     )
     back = call(
         final_kernel, "final", shape(CHUNK, DEVS),
         [vmem(CHUNK, DEVS)] + y_scratch, 10**9,
-        (owner, near, far, partial2, second, extras, faces, b_op), "s",
+        (core, *ghosts, partial2, second, extras, faces, b_op), "s",
     )
     returned = exchange(back, 8)
     result = call(

time: 89.8 us -> 84.6 us (0.942)
  blocking collectives: 38.3 us -> 21.4 us
  starting transfers between devices: 13.9 us -> 23.9 us
  waiting for transfers between devices: 6.39 us -> 8.12 us
    all_to_all x2 -> x0, blocking collectives: 18.3 us -> none  [swap_ghosts(): lax.all_to_all(cube, 'dom', split_axis=0, concat_axis=0, axis_index_group...]
    ppermute x2 -> x10, starting transfers between devices: 1.01 us -> 11 us  [the longest x8 8.24 us: move(): return lax.ppermute(part, 'dom', pairs)]
    ppermute x2 -> x10, waiting for transfers between devices: 0.04 us -> 1.74 us  [the longest x2 1.72 us: swap_ghosts(): twin = lax.ppermute(odd, 'dom', twins)]
    all_to_all x1, blocking collectives: 19.9 us -> 21.4 us  [exchange(): lax.all_to_all(cube, 'dom', split_axis=0, concat_axis=0, tiled=True)]
    pallas_call x10 -> x12, Pallas kernels: 30.7 us -> 30.7 us  [call(): pl.pallas_call(kernel, name=name, out_shape=outs, in_specs=[pl.BlockSpec(...]
  transfers between devices with their start and end apart: 4 -> 12, of which waited for: 1 -> 3; matrix products, arithmetic and copies ran while one was open for 0% -> 0% of each run, Pallas kernels for 11% -> 12%
where the time goes in v4:
time: 84.6 us; the launch traced here: 84.3 us
  Pallas kernels  30.7 us (36%)
  starting transfers between devices  23.9 us (28%)
  blocking collectives  21.4 us (25%)
  waiting for transfers between devices  8.12 us (10%)
    pallas_call x12, Pallas kernels, call(): pl.pallas_call(kernel, name=name, out_shape=outs, in_specs=[pl.BlockSpec(...  30.7 us
    all_to_all x1, blocking collectives, exchange(): lax.all_to_all(cube, 'dom', split_axis=0, concat_axis=0, tiled=True)  21.4 us
    all_to_all x1, starting transfers between devices, exchange(): lax.all_to_all(cube, 'dom', split_axis=0, concat_axis=0, tiled=True)  11.5 us
    ppermute x8, starting transfers between devices, move(): return lax.ppermute(part, 'dom', pairs)  8.24 us
    all_to_all x1, waiting for transfers between devices, exchange(): lax.all_to_all(cube, 'dom', split_axis=0, concat_axis=0, tiled=True)  6.38 us
    ppermute x2, starting transfers between devices, swap_ghosts(): twin = lax.ppermute(odd, 'dom', twins)  2.72 us
    ppermute x2, waiting for transfers between devices, swap_ghosts(): twin = lax.ppermute(odd, 'dom', twins)  1.72 us
  transfers between devices with their start and end apart: 12, of which 3 were waited for; matrix products, arithmetic and copies ran while one was open for 0% of the time, Pallas kernels for 12%

profile of v4, /device:TPU:1, one launch (start us, length us, event | category | flops | bytes accessed | tf_op | source)
XLA Modules:
  0.0 84.3 jit_solution(11150113984984423453)
XLA Ops:
  0.0 2.6 %scatter.1 = (f32[1024,128]{1,0:T(8,128)}, s32[16,384]{1,0:T(8,128)}) custom-call(s32[1]{0:T(128)} %bitcast.core, f32[9,35,256]{2,1,0:T(8,128)} %bitcast.23, f32[3,256]{1,0:T(4,128)} %jac.1, f32[4,256]{1,0:T(4,128)} %area.1, s32[1,256]{1,0:T(1,128)} %bitcast.25, s32[1,256]{1,0:T(1,128)} %bitcast.18, s32[4,384]{1,0:T(4,128)} %faces.1, s32[6,1,8]{2,1,0:T(1,128)} %bitcast.24), custom_call_target="tpu_custom_call" | custom-call | flops 100000000 | bytes 338116 | tf_op jit(solution)/shard_map/scatter/pallas_call | solution.py:438
  2.7 11.5 %all-to-all-start = ((f32[128,8,128]{2,1,0:T(8,128)}), f32[128,8,128]{2,1,0:T(8,128)S(1)}, u32[]{:S(2)}, u32[]{:S(2)}) async-start(f32[128,8,128]{2,1,0:T(8,128)} %bitcast.22), calls=%async_computation | async-start | bytes 1048576 | tf_op jit(solution)/shard_map/all_to_all | solution.py:456
  14.2 1.4 %collective-permute-start = (s32[16,384]{1,0:T(8,128)}, s32[16,384]{1,0:T(8,128)S(1)}, u32[]{:S(2)}, u32[]{:S(2)}) collective-permute-start(s32[16,384]{1,0:T(8,128)} %get-tuple-element.45), channel_id=1, source_target_pairs={{0,0},{1,1},{2,2},{3,3},{4,4},{5,5},{6,6},{7,7},{8,14},{9,15},{10,... | collective-permute-start | bytes 73736 | tf_op jit(solution)/shard_map/ppermute | solution.py:515
  15.6 0.0 copy-start.2
  15.6 0.0 copy-start.3
  15.6 4.7 %operators.1 = (bf16[640,2304]{1,0:T(8,128)(2,1)}, bf16[640,1280]{1,0:T(8,128)(2,1)}) custom-call(f32[3,35,35]{2,1,0:T(8,128)} %stiffness.2, f32[35,4,35]{2,1,0:T(4,128)} %bitcast.26, f32[35,4,35]{2,1,0:T(4,128)} %bitcast.27, f32[9,3,9]{2,1,0:T(4,128)} %bitcast.20, f32[9,4,9]{2,1,0:T(4,128)} %bitcast.28, f32[9,4,9]{2,1,0:T(4,128)} %bitcast.29), custom_call_target="tpu_custom_call" | custom-call | flops 1000000000 | bytes 57464 | tf_op jit(solution)/shard_map/operators/pallas_call | solution.py:438
  20.3 0.0 copy-done.2
  20.3 0.0 copy-done.3
  20.3 1.0 %taylor_operators.1.d_op = bf16[640,960]{1,0:T(8,128)(2,1)S(1)} custom-call(f32[3,35,35]{2,1,0:T(8,128)S(1)} %copy-done.2, f32[9,3,9]{2,1,0:T(4,128)S(1)} %bitcast.21), custom_call_target="tpu_custom_call" | custom-call | flops 1000000000 | bytes 15672 | tf_op jit(solution)/shard_map/taylor_operators/pallas_call | solution.py:438
  21.3 0.0 collective-permute-done.tables.faces
  21.3 6.4 %all-to-all-done = f32[128,8,128]{2,1,0:T(8,128)S(1)} async-done(((f32[128,8,128]{2,1,0:T(8,128)}), f32[128,8,128]{2,1,0:T(8,128)S(1)}, u32[]{:S(2)}, u32[]{:S(2)}) %all-to-all-start) | async-done | bytes 524320 | tf_op jit(solution)/shard_map/all_to_all | solution.py:456
  27.6 0.2 unpack.1
  27.8 0.0 copy-start
  27.8 5.2 %start.1 = (f32[320,384]{1,0:T(8,128)S(1)}, f32[320,384]{1,0:T(8,128)S(1)}, f32[64,128]{1,0:T(8,128)S(1)}, f32[64,128]{1,0:T(8,128)S(1)}) custom-call(f32[320,384]{1,0:T(8,128)S(1)} %get-tuple-element.48.state, f32[8,384]{1,0:T(8,128)S(1)} %get-tuple-element.49.extras, s32[8,128]{1,0:T(8,128)S(1)} %get-tuple-element.50.picks, ...), custom_call_target="tpu_custom_call" | custom-call | flops 1000000000 | bytes 2965504 | tf_op jit(solution)/shard_map/start/pallas_call | solution.py:438
  33.1 1.2 %collective-permute-start.1 = (f32[64,128]{1,0:T(8,128)S(1)}, f32[64,128]{1,0:T(8,128)S(1)}, u32[]{:S(2)}, u32[]{:S(2)}) collective-permute-start(f32[64,128]{1,0:T(8,128)S(1)} %get-tuple-element.54), channel_id=1, source_target_pairs={{0,1},{1,0},{2,3},{3,2},{4,5},{5,4},{6,7},{7,6},{14,15},{15,14},{1... | collective-permute-start | bytes 98312 | tf_op jit(solution)/shard_map/ppermute | solution.py:465
  34.2 0.9 %collective-permute-done.1.twin = f32[64,128]{1,0:T(8,128)S(1)} collective-permute-done((f32[64,128]{1,0:T(8,128)S(1)}, f32[64,128]{1,0:T(8,128)S(1)}, u32[]{:S(2)}, u32[]{:S(2)}) %collective-permute-start.1) | collective-permute-done | bytes 32800 | tf_op jit(solution)/shard_map/ppermute | solution.py:465
  35.1 0.4 collective-permute-start.4
  35.5 1.9 %collective-permute-start.5 = (f32[32,128]{1,0:T(8,128)S(1)}, f32[32,128]{1,0:T(8,128)S(1)}, u32[]{:S(2)}, u32[]{:S(2)}) collective-permute-start(f32[32,128]{1,0:T(8,128)S(1)} %get-tuple-element.64), channel_id=1, source_target_pairs={{0,34},{1,35},{2,32},{3,33},{4,0},{5,1},{6,2},{7,3},{14,4},{15,5},... | collective-permute-start | bytes 49160 | tf_op jit(solution)/shard_map/ppermute | solution.py:462
  37.5 0.1 collective-permute-start.2
  37.6 1.4 %collective-permute-start.3 = (f32[48,128]{1,0:T(8,128)S(1)}, f32[48,128]{1,0:T(8,128)S(1)}, u32[]{:S(2)}, u32[]{:S(2)}) collective-permute-start(f32[48,128]{1,0:T(8,128)S(1)} %get-tuple-element.62), channel_id=1, source_target_pairs={{0,32},{1,33},{2,0},{3,1},{4,2},{5,3},{6,4},{7,5},{14,6},{15,7},{1... | collective-permute-start | bytes 73736 | tf_op jit(solution)/shard_map/ppermute | solution.py:462
  39.0 0.0 copy-done
  39.0 0.0 copy-start.4
  39.0 2.3 %local1.1 = (f32[320,384]{1,0:T(8,128)S(1)}, s32[4,384]{1,0:T(4,128)S(1)}) custom-call(f32[320,384]{1,0:T(8,128)S(1)} %get-tuple-element.48.state, f32[320,384]{1,0:T(8,128)S(1)} %get-tuple-element.65.value.first, f32[8,384]{1,0:T(8,128)S(1)} %get-tuple-element.49.extras, bf16[640,2304]{1,0:T(8,128)(2,1)S(1)} %copy-done, ...), custom_call_target="tpu_custom_call" | custom-call | flops 1000000000 | bytes 6918144 | tf_op jit(solution)/shard_map/local1/pallas_call | solution.py:438
  41.2 0.0 collective-permute-done.4.far_up
  41.2 0.0 collective-permute-done.5.far_down
  41.2 0.0 collective-permute-done.2.up
  41.3 0.0 collective-permute-done.3.down
  41.3 0.0 copy-done.4
  41.3 8.0 %middle.1 = (f32[320,384]{1,0:T(8,128)S(1)}, f32[320,384]{1,0:T(8,128)S(1)}, f32[64,128]{1,0:T(8,128)S(1)}, f32[64,128]{1,0:T(8,128)S(1)}) custom-call(s32[1]{0:T(128)} %bitcast.core, f32[64,128]{1,0:T(8,128)S(1)} %collective-permute-done.1.twin, f32[48,128]{1,0:T(8,128)S(1)} %collective-permute-done.2.up, f32[48,128]{1,0:T(8,128)S(1)} %collective-permute-done.3.down, ...), custom_call_target="tpu_custom_call" | custom-call | flops 2000000000 | bytes 7346180 | tf_op jit(solution)/shard_map/middle/pallas_call | solution.py:438
  49.3 1.5 %collective-permute-start.6 = (f32[64,128]{1,0:T(8,128)S(1)}, f32[64,128]{1,0:T(8,128)S(1)}, u32[]{:S(2)}, u32[]{:S(2)}) collective-permute-start(f32[64,128]{1,0:T(8,128)S(1)} %get-tuple-element.70), channel_id=1, source_target_pairs={{0,1},{1,0},{2,3},{3,2},{4,5},{5,4},{6,7},{7,6},{14,15},{15,14},{1... | collective-permute-start | bytes 98312 | tf_op jit(solution)/shard_map/ppermute | solution.py:465
  50.9 0.9 %collective-permute-done.6.twin = f32[64,128]{1,0:T(8,128)S(1)} collective-permute-done((f32[64,128]{1,0:T(8,128)S(1)}, f32[64,128]{1,0:T(8,128)S(1)}, u32[]{:S(2)}, u32[]{:S(2)}) %collective-permute-start.6) | collective-permute-done | bytes 32800 | tf_op jit(solution)/shard_map/ppermute | solution.py:465
  51.7 2.0 %collective-permute-start.9 = (f32[32,128]{1,0:T(8,128)S(1)}, f32[32,128]{1,0:T(8,128)S(1)}, u32[]{:S(2)}, u32[]{:S(2)}) collective-permute-start(f32[32,128]{1,0:T(8,128)S(1)} %get-tuple-element.79), channel_id=1, source_target_pairs={{0,4},{1,5},{2,6},{3,7},{4,14},{5,15},{6,12},{7,13},{14,10},{15,11... | collective-permute-start | bytes 49160 | tf_op jit(solution)/shard_map/ppermute | solution.py:462
  53.7 0.5 collective-permute-start.10
  54.2 0.4 collective-permute-start.7
  54.5 1.6 %collective-permute-start.8 = (f32[48,128]{1,0:T(8,128)S(1)}, f32[48,128]{1,0:T(8,128)S(1)}, u32[]{:S(2)}, u32[]{:S(2)}) collective-permute-start(f32[48,128]{1,0:T(8,128)S(1)} %get-tuple-element.78), channel_id=1, source_target_pairs={{0,32},{1,33},{2,0},{3,1},{4,2},{5,3},{6,4},{7,5},{14,6},{15,7},{1... | collective-permute-start | bytes 73736 | tf_op jit(solution)/shard_map/ppermute | solution.py:462
  56.1 2.2 %local2.1.partial = f32[320,384]{1,0:T(8,128)S(1)} custom-call(f32[320,384]{1,0:T(8,128)S(1)} %get-tuple-element.81.state, f32[320,384]{1,0:T(8,128)S(1)} %get-tuple-element.82.value.second, f32[8,384]{1,0:T(8,128)S(1)} %get-tuple-element.49.extras, bf16[640,2304]{1,0:T(8,128)(2,1)S(1)} %copy-done), custom_call_target="tpu_custom_call" | custom-call | flops 1000000000 | bytes 6893568 | tf_op jit(solution)/shard_map/local2/pallas_call | solution.py:438
  58.3 0.0 copy-start.1
  58.3 0.0 collective-permute-done.9.far_up
  58.4 0.0 collective-permute-done.10.far_down
  58.4 0.0 collective-permute-done.7.up
  58.4 0.0 collective-permute-done.8.down
  58.4 3.0 %final.1 = f32[1024,128]{1,0:T(8,128)S(1)} custom-call(s32[1]{0:T(128)} %bitcast.core, f32[64,128]{1,0:T(8,128)S(1)} %collective-permute-done.6.twin, f32[48,128]{1,0:T(8,128)S(1)} %collective-permute-done.7.up, f32[48,128]{1,0:T(8,128)S(1)} %collective-permute-done.8.down, f32[32,128]{1,0:T(8,128)S(1)} %collective-permute-done.9.far_up, ...), custom_call_target="tpu_custom_call" | custom-call | flops 1000000000 | bytes 4392964 | tf_op jit(solution)/shard_map/final/pallas_call | solution.py:438
  61.4 21.4 %all_to_all.10 = f32[128,8,128]{2,1,0:T(8,128)S(1)} all-to-all(f32[128,8,128]{2,1,0:T(8,128)S(1)} %bitcast.17), channel_id=1, replica_groups=mesh['dom'=128] {'dom'}, dimensions={0} | all-to-all | bytes 1048576 | tf_op jit(solution)/shard_map/all_to_all | solution.py:456
  82.9 0.0 copy-done.1
  82.9 1.4 %gather.1 = f32[9,35,256]{2,1,0:T(8,128)} custom-call(f32[1024,128]{1,0:T(8,128)S(1)} %bitcast.16, s32[1,256]{1,0:T(1,128)S(1)} %bitcast.19), custom_call_target="tpu_custom_call" | custom-call | flops 100000000 | bytes 525312 | tf_op jit(solution)/shard_map/gather/pallas_call | solution.py:438
  (2 shorter events, 0.0 us)
Async XLA Ops:
  2.7 25.0 %all-to-all-start = ((f32[128,8,128]{2,1,0:T(8,128)}), f32[128,8,128]{2,1,0:T(8,128)S(1)}, u32[]{:S(2)}, u32[]{:S(2)}) async-start(f32[128,8,128]{2,1,0:T(8,128)} %bitcast.22), calls=%async_computation | async-start | bytes 1048576 | tf_op jit(solution)/shard_map/all_to_all | solution.py:456
  14.2 7.1 %collective-permute-start = (s32[16,384]{1,0:T(8,128)}, s32[16,384]{1,0:T(8,128)S(1)}, u32[]{:S(2)}, u32[]{:S(2)}) collective-permute-start(s32[16,384]{1,0:T(8,128)} %get-tuple-element.45), channel_id=1, source_target_pairs={{0,0},{1,1},{2,2},{3,3},{4,4},{5,5},{6,6},{7,7},{8,14},{9,15},{10,... | collective-permute-start | bytes 73736 | tf_op jit(solution)/shard_map/ppermute | solution.py:515
  15.6 4.7 %copy-start.2 = (f32[3,35,35]{2,1,0:T(8,128)S(1)}, f32[3,35,35]{2,1,0:T(8,128)}, u32[]{:S(2)}) copy-start(f32[3,35,35]{2,1,0:T(8,128)} %stiffness.2) | copy-start | bytes 44104
  15.6 4.7 %copy-start.3 = (f32[3,9,9]{2,0,1:T(4,128)S(1)}, f32[3,9,9]{2,0,1:T(4,128)}, u32[]{:S(2)}) copy-start(f32[3,9,9]{2,0,1:T(4,128)} %param.21) | copy-start | bytes 2920
  27.8 11.1 %copy-start = (bf16[640,2304]{1,0:T(8,128)(2,1)S(1)}, bf16[640,2304]{1,0:T(8,128)(2,1)}, u32[]{:S(2)}) copy-start(bf16[640,2304]{1,0:T(8,128)(2,1)} %get-tuple-element.66.c_op) | copy-start | bytes 8847364
  33.1 2.1 %collective-permute-start.1 = (f32[64,128]{1,0:T(8,128)S(1)}, f32[64,128]{1,0:T(8,128)S(1)}, u32[]{:S(2)}, u32[]{:S(2)}) collective-permute-start(f32[64,128]{1,0:T(8,128)S(1)} %get-tuple-element.54), channel_id=1, source_target_pairs={{0,1},{1,0},{2,3},{3,2},{4,5},{5,4},{6,7},{7,6},{14,15},{15,14},{1... | collective-permute-start | bytes 98312 | tf_op jit(solution)/shard_map/ppermute | solution.py:465
  35.1 6.1 %collective-permute-start.4 = (f32[32,128]{1,0:T(8,128)S(1)}, f32[32,128]{1,0:T(8,128)S(1)}, u32[]{:S(2)}, u32[]{:S(2)}) collective-permute-start(f32[32,128]{1,0:T(8,128)S(1)} %get-tuple-element.63), channel_id=1, source_target_pairs={{0,4},{1,5},{2,6},{3,7},{4,14},{5,15},{6,12},{7,13},{14,10},{15,11... | collective-permute-start | bytes 49160 | tf_op jit(solution)/shard_map/ppermute | solution.py:462
  35.5 5.7 %collective-permute-start.5 = (f32[32,128]{1,0:T(8,128)S(1)}, f32[32,128]{1,0:T(8,128)S(1)}, u32[]{:S(2)}, u32[]{:S(2)}) collective-permute-start(f32[32,128]{1,0:T(8,128)S(1)} %get-tuple-element.64), channel_id=1, source_target_pairs={{0,34},{1,35},{2,32},{3,33},{4,0},{5,1},{6,2},{7,3},{14,4},{15,5},... | collective-permute-start | bytes 49160 | tf_op jit(solution)/shard_map/ppermute | solution.py:462
  37.5 3.8 %collective-permute-start.2 = (f32[48,128]{1,0:T(8,128)S(1)}, f32[48,128]{1,0:T(8,128)S(1)}, u32[]{:S(2)}, u32[]{:S(2)}) collective-permute-start(f32[48,128]{1,0:T(8,128)S(1)} %get-tuple-element.61), channel_id=1, source_target_pairs={{0,2},{1,3},{2,4},{3,5},{4,6},{5,7},{6,14},{7,15},{14,12},{15,13},... | collective-permute-start | bytes 73736 | tf_op jit(solution)/shard_map/ppermute | solution.py:462
  37.6 3.7 %collective-permute-start.3 = (f32[48,128]{1,0:T(8,128)S(1)}, f32[48,128]{1,0:T(8,128)S(1)}, u32[]{:S(2)}, u32[]{:S(2)}) collective-permute-start(f32[48,128]{1,0:T(8,128)S(1)} %get-tuple-element.62), channel_id=1, source_target_pairs={{0,32},{1,33},{2,0},{3,1},{4,2},{5,3},{6,4},{7,5},{14,6},{15,7},{1... | collective-permute-start | bytes 73736 | tf_op jit(solution)/shard_map/ppermute | solution.py:462
  39.0 2.3 %copy-start.4 = (bf16[640,1280]{1,0:T(8,128)(2,1)S(1)}, bf16[640,1280]{1,0:T(8,128)(2,1)}, u32[]{:S(2)}) copy-start(bf16[640,1280]{1,0:T(8,128)(2,1)} %get-tuple-element.51.b_op) | copy-start | bytes 4915204
  49.3 2.4 %collective-permute-start.6 = (f32[64,128]{1,0:T(8,128)S(1)}, f32[64,128]{1,0:T(8,128)S(1)}, u32[]{:S(2)}, u32[]{:S(2)}) collective-permute-start(f32[64,128]{1,0:T(8,128)S(1)} %get-tuple-element.70), channel_id=1, source_target_pairs={{0,1},{1,0},{2,3},{3,2},{4,5},{5,4},{6,7},{7,6},{14,15},{15,14},{1... | collective-permute-start | bytes 98312 | tf_op jit(solution)/shard_map/ppermute | solution.py:465
  51.7 6.6 %collective-permute-start.9 = (f32[32,128]{1,0:T(8,128)S(1)}, f32[32,128]{1,0:T(8,128)S(1)}, u32[]{:S(2)}, u32[]{:S(2)}) collective-permute-start(f32[32,128]{1,0:T(8,128)S(1)} %get-tuple-element.79), channel_id=1, source_target_pairs={{0,4},{1,5},{2,6},{3,7},{4,14},{5,15},{6,12},{7,13},{14,10},{15,11... | collective-permute-start | bytes 49160 | tf_op jit(solution)/shard_map/ppermute | solution.py:462
  53.7 4.7 %collective-permute-start.10 = (f32[32,128]{1,0:T(8,128)S(1)}, f32[32,128]{1,0:T(8,128)S(1)}, u32[]{:S(2)}, u32[]{:S(2)}) collective-permute-start(f32[32,128]{1,0:T(8,128)S(1)} %get-tuple-element.80), channel_id=1, source_target_pairs={{0,34},{1,35},{2,32},{3,33},{4,0},{5,1},{6,2},{7,3},{14,4},{15,5},... | collective-permute-start | bytes 49160 | tf_op jit(solution)/shard_map/ppermute | solution.py:462
  54.2 4.2 %collective-permute-start.7 = (f32[48,128]{1,0:T(8,128)S(1)}, f32[48,128]{1,0:T(8,128)S(1)}, u32[]{:S(2)}, u32[]{:S(2)}) collective-permute-start(f32[48,128]{1,0:T(8,128)S(1)} %get-tuple-element.77), channel_id=1, source_target_pairs={{0,2},{1,3},{2,4},{3,5},{4,6},{5,7},{6,14},{7,15},{14,12},{15,13},... | collective-permute-start | bytes 73736 | tf_op jit(solution)/shard_map/ppermute | solution.py:462
  54.5 3.8 %collective-permute-start.8 = (f32[48,128]{1,0:T(8,128)S(1)}, f32[48,128]{1,0:T(8,128)S(1)}, u32[]{:S(2)}, u32[]{:S(2)}) collective-permute-start(f32[48,128]{1,0:T(8,128)S(1)} %get-tuple-element.78), channel_id=1, source_target_pairs={{0,32},{1,33},{2,0},{3,1},{4,2},{5,3},{6,4},{7,5},{14,6},{15,7},{1... | collective-permute-start | bytes 73736 | tf_op jit(solution)/shard_map/ppermute | solution.py:462
  58.3 24.5 %copy-start.1 = (s32[256]{0:T(256)S(1)}, s32[256]{0:T(256)}, u32[]{:S(2)}) copy-start(s32[256]{0:T(256)} %param.17) | copy-start | bytes 3076

commit v5 on v4

--- a/solution.py
+++ b/solution.py
@@ -58,6 +58,11 @@
     return total
 
 
+def dot2(a, b):
+    high, low = split2(a)
+    return dot(high, b) + dot(low, b)
+
+
 def product(op, both):
     depth, width = both.shape[0], both.shape[1] // 2
     wide = dot(op[0:ROWS, 0:depth], both[...])
@@ -120,29 +125,31 @@
     ]
     for copy in copies:
         copy.start()
-    for copy in copies:
-        copy.wait()
+    copies[4].wait()
+    half = owner_of(iota((DEVS, DEVS), 0)) * CAP
+    slot = jnp.concatenate([half, half], axis=1)
+    wanted = places[...]
+    hots = [onehot(slot + t == wanted) for t in range(CAP)]
+    tables[8:16, :] = jnp.zeros((8, SLOTS), jnp.int32)
+    values[320:328, :] = jnp.zeros((8, BLOCK), F32)
+    stage[CAP * STRIDE :, :] = jnp.zeros((CHUNK - CAP * STRIDE, DEVS), F32)
+    for t in range(CAP):
+        stage[STRIDE * t + 328 : STRIDE * (t + 1), :] = jnp.zeros((8, DEVS), F32)
+    for k in (0, 1, 2, 3, 5, 6):
+        copies[k].wait()
     tables[4:8, :] = jnp.full((4, SLOTS), core[0], jnp.int32)
-    tables[8:16, :] = jnp.zeros((8, SLOTS), jnp.int32)
     for i in range(GHOSTS):
         tables[8 + i : 9 + i, 0:NEIGH] = lists[i]
     values[7:8, :] = 1.0 + kinds[...].astype(F32)
-    values[320:328, :] = jnp.zeros((8, BLOCK), F32)
     for q in range(QUANT):
         values[8 + MODES * q : 8 + MODES * (q + 1), :] = cells[q]
-    half = owner_of(iota((DEVS, DEVS), 0)) * CAP
-    slot = jnp.concatenate([half, half], axis=1)
-    wanted = places[...]
-    stage[CAP * STRIDE :, :] = jnp.zeros((CHUNK - CAP * STRIDE, DEVS), F32)
     parts = split3(values[...])
     for t in range(CAP):
-        hot = onehot(slot + t == wanted)
         total = None
         for part in parts:
-            term = lax.dot_general(part, hot, (((1,), (1,)), ((), ())), preferred_element_type=F32)
+            term = lax.dot_general(part, hots[t], (((1,), (1,)), ((), ())), preferred_element_type=F32)
             total = term if total is None else total + term
         stage[STRIDE * t : STRIDE * t + 328, :] = total
-        stage[STRIDE * t + 328 : STRIDE * (t + 1), :] = jnp.zeros((8, DEVS), F32)
     pack_rows(stage, out)
 
 
@@ -288,8 +295,8 @@
     slot = (slot & 127) * CAP + (slot >> 7)
     base = onehot(slot == picks[0:1, :])
     rest = jnp.concatenate([onehot(slot == picks[k : k + 1, :]) for k in range(1, 5)], axis=1)
-    main = dot3(value[0:256, :], base)
-    tail = dot3(value[256:320, :], rest)
+    main = dot2(value[0:256, :], base)
+    tail = dot2(value[256:320, :], rest)
     first = (main[0:128, :] + jnp.concatenate([tail[:, 0:128], tail[:, 128:256]], axis=0)).T
     second = (main[128:256, :] + jnp.concatenate([tail[:, 256:384], tail[:, 384:512]], axis=0)).T
     for b, step in enumerate(STEPS):
@@ -339,7 +346,7 @@
         for ghost, spot in moves:
             one = (part == ghost) & (row == group + spot)
             hit = one if hit is None else hit | one
-        term = dot3(half, onehot(hit))
+        term = dot2(half, onehot(hit))
         tail = term if tail is None else tail + term
     return jnp.concatenate([first, second, tail], axis=0)
 

time: 84.6 us -> 84 us (level)
  no operation moved by 1% of the time
where the time goes in v5:
time: 84 us; the launch traced here: 83.7 us
  Pallas kernels  30.1 us (36%)
  starting transfers between devices  23.8 us (28%)
  blocking collectives  21.4 us (25%)
  waiting for transfers between devices  8.12 us (10%)
    pallas_call x12, Pallas kernels, call(): pl.pallas_call(kernel, name=name, out_shape=outs, in_specs=[pl.BlockSpec(...  30.1 us
    all_to_all x1, blocking collectives, exchange(): lax.all_to_all(cube, 'dom', split_axis=0, concat_axis=0, tiled=True)  21.4 us
    all_to_all x1, starting transfers between devices, exchange(): lax.all_to_all(cube, 'dom', split_axis=0, concat_axis=0, tiled=True)  11.5 us
    ppermute x8, starting transfers between devices, move(): return lax.ppermute(part, 'dom', pairs)  8.24 us
    all_to_all x1, waiting for transfers between devices, exchange(): lax.all_to_all(cube, 'dom', split_axis=0, concat_axis=0, tiled=True)  6.38 us
    ppermute x2, starting transfers between devices, swap_ghosts(): twin = lax.ppermute(odd, 'dom', twins)  2.71 us
    ppermute x2, waiting for transfers between devices, swap_ghosts(): twin = lax.ppermute(odd, 'dom', twins)  1.72 us
  transfers between devices with their start and end apart: 12, of which 3 were waited for; matrix products, arithmetic and copies ran while one was open for 0% of the time, Pallas kernels for 12%

profile of v5, /device:TPU:1, one launch (start us, length us, event | category | flops | bytes accessed | tf_op | source)
XLA Modules:
  0.0 83.7 jit_solution(15195574828694272433)
XLA Ops:
  0.0 2.6 %scatter.1 = (f32[1024,128]{1,0:T(8,128)}, s32[16,384]{1,0:T(8,128)}) custom-call(s32[1]{0:T(128)} %bitcast.core, f32[9,35,256]{2,1,0:T(8,128)} %bitcast.23, f32[3,256]{1,0:T(4,128)} %jac.1, f32[4,256]{1,0:T(4,128)} %area.1, s32[1,256]{1,0:T(1,128)} %bitcast.25, s32[1,256]{1,0:T(1,128)} %bitcast.18, s32[4,384]{1,0:T(4,128)} %faces.1, s32[6,1,8]{2,1,0:T(1,128)} %bitcast.24), custom_call_target="tpu_custom_call" | custom-call | flops 100000000 | bytes 338116 | tf_op jit(solution)/shard_map/scatter/pallas_call | solution.py:445
  2.6 11.5 %all-to-all-start = ((f32[128,8,128]{2,1,0:T(8,128)}), f32[128,8,128]{2,1,0:T(8,128)S(1)}, u32[]{:S(2)}, u32[]{:S(2)}) async-start(f32[128,8,128]{2,1,0:T(8,128)} %bitcast.22), calls=%async_computation | async-start | bytes 1048576 | tf_op jit(solution)/shard_map/all_to_all | solution.py:463
  14.1 1.4 %collective-permute-start = (s32[16,384]{1,0:T(8,128)}, s32[16,384]{1,0:T(8,128)S(1)}, u32[]{:S(2)}, u32[]{:S(2)}) collective-permute-start(s32[16,384]{1,0:T(8,128)} %get-tuple-element.45), channel_id=1, source_target_pairs={{0,0},{1,1},{2,2},{3,3},{4,4},{5,5},{6,6},{7,7},{8,14},{9,15},{10,... | collective-permute-start | bytes 73736 | tf_op jit(solution)/shard_map/ppermute | solution.py:522
  15.5 0.0 copy-start.2
  15.5 0.0 copy-start.3
  15.5 4.7 %operators.1 = (bf16[640,2304]{1,0:T(8,128)(2,1)}, bf16[640,1280]{1,0:T(8,128)(2,1)}) custom-call(f32[3,35,35]{2,1,0:T(8,128)} %stiffness.2, f32[35,4,35]{2,1,0:T(4,128)} %bitcast.26, f32[35,4,35]{2,1,0:T(4,128)} %bitcast.27, f32[9,3,9]{2,1,0:T(4,128)} %bitcast.20, f32[9,4,9]{2,1,0:T(4,128)} %bitcast.28, f32[9,4,9]{2,1,0:T(4,128)} %bitcast.29), custom_call_target="tpu_custom_call" | custom-call | flops 1000000000 | bytes 57464 | tf_op jit(solution)/shard_map/operators/pallas_call | solution.py:445
  20.2 0.0 copy-done.2
  20.2 0.0 copy-done.3
  20.2 1.0 %taylor_operators.1.d_op = bf16[640,960]{1,0:T(8,128)(2,1)S(1)} custom-call(f32[3,35,35]{2,1,0:T(8,128)S(1)} %copy-done.2, f32[9,3,9]{2,1,0:T(4,128)S(1)} %bitcast.21), custom_call_target="tpu_custom_call" | custom-call | flops 1000000000 | bytes 15672 | tf_op jit(solution)/shard_map/taylor_operators/pallas_call | solution.py:445
  21.2 0.0 collective-permute-done.tables.faces
  21.2 6.4 %all-to-all-done = f32[128,8,128]{2,1,0:T(8,128)S(1)} async-done(((f32[128,8,128]{2,1,0:T(8,128)}), f32[128,8,128]{2,1,0:T(8,128)S(1)}, u32[]{:S(2)}, u32[]{:S(2)}) %all-to-all-start) | async-done | bytes 524320 | tf_op jit(solution)/shard_map/all_to_all | solution.py:463
  27.6 0.2 unpack.1
  27.8 0.0 copy-start
  27.8 5.1 %start.1 = (f32[320,384]{1,0:T(8,128)S(1)}, f32[320,384]{1,0:T(8,128)S(1)}, f32[64,128]{1,0:T(8,128)S(1)}, f32[64,128]{1,0:T(8,128)S(1)}) custom-call(f32[320,384]{1,0:T(8,128)S(1)} %get-tuple-element.48.state, f32[8,384]{1,0:T(8,128)S(1)} %get-tuple-element.49.extras, s32[8,128]{1,0:T(8,128)S(1)} %get-tuple-element.50.picks, ...), custom_call_target="tpu_custom_call" | custom-call | flops 1000000000 | bytes 2965504 | tf_op jit(solution)/shard_map/start/pallas_call | solution.py:445
  32.9 1.2 %collective-permute-start.1 = (f32[64,128]{1,0:T(8,128)S(1)}, f32[64,128]{1,0:T(8,128)S(1)}, u32[]{:S(2)}, u32[]{:S(2)}) collective-permute-start(f32[64,128]{1,0:T(8,128)S(1)} %get-tuple-element.54), channel_id=1, source_target_pairs={{0,1},{1,0},{2,3},{3,2},{4,5},{5,4},{6,7},{7,6},{14,15},{15,14},{1... | collective-permute-start | bytes 98312 | tf_op jit(solution)/shard_map/ppermute | solution.py:472
  34.0 0.9 %collective-permute-done.1.twin = f32[64,128]{1,0:T(8,128)S(1)} collective-permute-done((f32[64,128]{1,0:T(8,128)S(1)}, f32[64,128]{1,0:T(8,128)S(1)}, u32[]{:S(2)}, u32[]{:S(2)}) %collective-permute-start.1) | collective-permute-done | bytes 32800 | tf_op jit(solution)/shard_map/ppermute | solution.py:472
  34.9 0.4 collective-permute-start.4
  35.3 1.9 %collective-permute-start.5 = (f32[32,128]{1,0:T(8,128)S(1)}, f32[32,128]{1,0:T(8,128)S(1)}, u32[]{:S(2)}, u32[]{:S(2)}) collective-permute-start(f32[32,128]{1,0:T(8,128)S(1)} %get-tuple-element.64), channel_id=1, source_target_pairs={{0,34},{1,35},{2,32},{3,33},{4,0},{5,1},{6,2},{7,3},{14,4},{15,5},... | collective-permute-start | bytes 49160 | tf_op jit(solution)/shard_map/ppermute | solution.py:469
  37.3 0.1 collective-permute-start.2
  37.4 1.4 %collective-permute-start.3 = (f32[48,128]{1,0:T(8,128)S(1)}, f32[48,128]{1,0:T(8,128)S(1)}, u32[]{:S(2)}, u32[]{:S(2)}) collective-permute-start(f32[48,128]{1,0:T(8,128)S(1)} %get-tuple-element.62), channel_id=1, source_target_pairs={{0,32},{1,33},{2,0},{3,1},{4,2},{5,3},{6,4},{7,5},{14,6},{15,7},{1... | collective-permute-start | bytes 73736 | tf_op jit(solution)/shard_map/ppermute | solution.py:469
  38.7 0.0 copy-done
  38.7 0.0 copy-start.4
  38.7 2.3 %local1.1 = (f32[320,384]{1,0:T(8,128)S(1)}, s32[4,384]{1,0:T(4,128)S(1)}) custom-call(f32[320,384]{1,0:T(8,128)S(1)} %get-tuple-element.48.state, f32[320,384]{1,0:T(8,128)S(1)} %get-tuple-element.65.value.first, f32[8,384]{1,0:T(8,128)S(1)} %get-tuple-element.49.extras, bf16[640,2304]{1,0:T(8,128)(2,1)S(1)} %copy-done, ...), custom_call_target="tpu_custom_call" | custom-call | flops 1000000000 | bytes 6918144 | tf_op jit(solution)/shard_map/local1/pallas_call | solution.py:445
  41.0 0.0 collective-permute-done.4.far_up
  41.0 0.0 collective-permute-done.5.far_down
  41.0 0.0 collective-permute-done.2.up
  41.0 0.0 collective-permute-done.3.down
  41.1 0.0 copy-done.4
  41.1 7.8 %middle.1 = (f32[320,384]{1,0:T(8,128)S(1)}, f32[320,384]{1,0:T(8,128)S(1)}, f32[64,128]{1,0:T(8,128)S(1)}, f32[64,128]{1,0:T(8,128)S(1)}) custom-call(s32[1]{0:T(128)} %bitcast.core, f32[64,128]{1,0:T(8,128)S(1)} %collective-permute-done.1.twin, f32[48,128]{1,0:T(8,128)S(1)} %collective-permute-done.2.up, f32[48,128]{1,0:T(8,128)S(1)} %collective-permute-done.3.down, ...), custom_call_target="tpu_custom_call" | custom-call | flops 2000000000 | bytes 7346180 | tf_op jit(solution)/shard_map/middle/pallas_call | solution.py:445
  48.9 1.5 %collective-permute-start.6 = (f32[64,128]{1,0:T(8,128)S(1)}, f32[64,128]{1,0:T(8,128)S(1)}, u32[]{:S(2)}, u32[]{:S(2)}) collective-permute-start(f32[64,128]{1,0:T(8,128)S(1)} %get-tuple-element.70), channel_id=1, source_target_pairs={{0,1},{1,0},{2,3},{3,2},{4,5},{5,4},{6,7},{7,6},{14,15},{15,14},{1... | collective-permute-start | bytes 98312 | tf_op jit(solution)/shard_map/ppermute | solution.py:472
  50.4 0.9 %collective-permute-done.6.twin = f32[64,128]{1,0:T(8,128)S(1)} collective-permute-done((f32[64,128]{1,0:T(8,128)S(1)}, f32[64,128]{1,0:T(8,128)S(1)}, u32[]{:S(2)}, u32[]{:S(2)}) %collective-permute-start.6) | collective-permute-done | bytes 32800 | tf_op jit(solution)/shard_map/ppermute | solution.py:472
  51.3 2.0 %collective-permute-start.9 = (f32[32,128]{1,0:T(8,128)S(1)}, f32[32,128]{1,0:T(8,128)S(1)}, u32[]{:S(2)}, u32[]{:S(2)}) collective-permute-start(f32[32,128]{1,0:T(8,128)S(1)} %get-tuple-element.79), channel_id=1, source_target_pairs={{0,4},{1,5},{2,6},{3,7},{4,14},{5,15},{6,12},{7,13},{14,10},{15,11... | collective-permute-start | bytes 49160 | tf_op jit(solution)/shard_map/ppermute | solution.py:469
  53.2 0.5 collective-permute-start.10
  53.7 0.4 collective-permute-start.7
  54.1 1.6 %collective-permute-start.8 = (f32[48,128]{1,0:T(8,128)S(1)}, f32[48,128]{1,0:T(8,128)S(1)}, u32[]{:S(2)}, u32[]{:S(2)}) collective-permute-start(f32[48,128]{1,0:T(8,128)S(1)} %get-tuple-element.78), channel_id=1, source_target_pairs={{0,32},{1,33},{2,0},{3,1},{4,2},{5,3},{6,4},{7,5},{14,6},{15,7},{1... | collective-permute-start | bytes 73736 | tf_op jit(solution)/shard_map/ppermute | solution.py:469
  55.7 2.2 %local2.1.partial = f32[320,384]{1,0:T(8,128)S(1)} custom-call(f32[320,384]{1,0:T(8,128)S(1)} %get-tuple-element.81.state, f32[320,384]{1,0:T(8,128)S(1)} %get-tuple-element.82.value.second, f32[8,384]{1,0:T(8,128)S(1)} %get-tuple-element.49.extras, bf16[640,2304]{1,0:T(8,128)(2,1)S(1)} %copy-done), custom_call_target="tpu_custom_call" | custom-call | flops 1000000000 | bytes 6893568 | tf_op jit(solution)/shard_map/local2/pallas_call | solution.py:445
  57.9 0.0 copy-start.1
  57.9 0.0 collective-permute-done.9.far_up
  57.9 0.0 collective-permute-done.10.far_down
  57.9 0.0 collective-permute-done.7.up
  57.9 0.0 collective-permute-done.8.down
  57.9 2.9 %final.1 = f32[1024,128]{1,0:T(8,128)S(1)} custom-call(s32[1]{0:T(128)} %bitcast.core, f32[64,128]{1,0:T(8,128)S(1)} %collective-permute-done.6.twin, f32[48,128]{1,0:T(8,128)S(1)} %collective-permute-done.7.up, f32[48,128]{1,0:T(8,128)S(1)} %collective-permute-done.8.down, f32[32,128]{1,0:T(8,128)S(1)} %collective-permute-done.9.far_up, ...), custom_call_target="tpu_custom_call" | custom-call | flops 1000000000 | bytes 4392964 | tf_op jit(solution)/shard_map/final/pallas_call | solution.py:445
  60.9 21.4 %all_to_all.10 = f32[128,8,128]{2,1,0:T(8,128)S(1)} all-to-all(f32[128,8,128]{2,1,0:T(8,128)S(1)} %bitcast.17), channel_id=1, replica_groups=mesh['dom'=128] {'dom'}, dimensions={0} | all-to-all | bytes 1048576 | tf_op jit(solution)/shard_map/all_to_all | solution.py:463
  82.3 0.0 copy-done.1
  82.3 1.4 %gather.1 = f32[9,35,256]{2,1,0:T(8,128)} custom-call(f32[1024,128]{1,0:T(8,128)S(1)} %bitcast.16, s32[1,256]{1,0:T(1,128)S(1)} %bitcast.19), custom_call_target="tpu_custom_call" | custom-call | flops 100000000 | bytes 525312 | tf_op jit(solution)/shard_map/gather/pallas_call | solution.py:445
  (2 shorter events, 0.0 us)
Async XLA Ops:
  2.6 25.0 %all-to-all-start = ((f32[128,8,128]{2,1,0:T(8,128)}), f32[128,8,128]{2,1,0:T(8,128)S(1)}, u32[]{:S(2)}, u32[]{:S(2)}) async-start(f32[128,8,128]{2,1,0:T(8,128)} %bitcast.22), calls=%async_computation | async-start | bytes 1048576 | tf_op jit(solution)/shard_map/all_to_all | solution.py:463
  14.1 7.1 %collective-permute-start = (s32[16,384]{1,0:T(8,128)}, s32[16,384]{1,0:T(8,128)S(1)}, u32[]{:S(2)}, u32[]{:S(2)}) collective-permute-start(s32[16,384]{1,0:T(8,128)} %get-tuple-element.45), channel_id=1, source_target_pairs={{0,0},{1,1},{2,2},{3,3},{4,4},{5,5},{6,6},{7,7},{8,14},{9,15},{10,... | collective-permute-start | bytes 73736 | tf_op jit(solution)/shard_map/ppermute | solution.py:522
  15.5 4.7 %copy-start.2 = (f32[3,35,35]{2,1,0:T(8,128)S(1)}, f32[3,35,35]{2,1,0:T(8,128)}, u32[]{:S(2)}) copy-start(f32[3,35,35]{2,1,0:T(8,128)} %stiffness.2) | copy-start | bytes 44104
  15.5 4.7 %copy-start.3 = (f32[3,9,9]{2,0,1:T(4,128)S(1)}, f32[3,9,9]{2,0,1:T(4,128)}, u32[]{:S(2)}) copy-start(f32[3,9,9]{2,0,1:T(4,128)} %param.21) | copy-start | bytes 2920
  27.8 11.0 %copy-start = (bf16[640,2304]{1,0:T(8,128)(2,1)S(1)}, bf16[640,2304]{1,0:T(8,128)(2,1)}, u32[]{:S(2)}) copy-start(bf16[640,2304]{1,0:T(8,128)(2,1)} %get-tuple-element.66.c_op) | copy-start | bytes 8847364
  32.9 2.0 %collective-permute-start.1 = (f32[64,128]{1,0:T(8,128)S(1)}, f32[64,128]{1,0:T(8,128)S(1)}, u32[]{:S(2)}, u32[]{:S(2)}) collective-permute-start(f32[64,128]{1,0:T(8,128)S(1)} %get-tuple-element.54), channel_id=1, source_target_pairs={{0,1},{1,0},{2,3},{3,2},{4,5},{5,4},{6,7},{7,6},{14,15},{15,14},{1... | collective-permute-start | bytes 98312 | tf_op jit(solution)/shard_map/ppermute | solution.py:472
  34.9 6.1 %collective-permute-start.4 = (f32[32,128]{1,0:T(8,128)S(1)}, f32[32,128]{1,0:T(8,128)S(1)}, u32[]{:S(2)}, u32[]{:S(2)}) collective-permute-start(f32[32,128]{1,0:T(8,128)S(1)} %get-tuple-element.63), channel_id=1, source_target_pairs={{0,4},{1,5},{2,6},{3,7},{4,14},{5,15},{6,12},{7,13},{14,10},{15,11... | collective-permute-start | bytes 49160 | tf_op jit(solution)/shard_map/ppermute | solution.py:469
  35.3 5.7 %collective-permute-start.5 = (f32[32,128]{1,0:T(8,128)S(1)}, f32[32,128]{1,0:T(8,128)S(1)}, u32[]{:S(2)}, u32[]{:S(2)}) collective-permute-start(f32[32,128]{1,0:T(8,128)S(1)} %get-tuple-element.64), channel_id=1, source_target_pairs={{0,34},{1,35},{2,32},{3,33},{4,0},{5,1},{6,2},{7,3},{14,4},{15,5},... | collective-permute-start | bytes 49160 | tf_op jit(solution)/shard_map/ppermute | solution.py:469
  37.3 3.8 %collective-permute-start.2 = (f32[48,128]{1,0:T(8,128)S(1)}, f32[48,128]{1,0:T(8,128)S(1)}, u32[]{:S(2)}, u32[]{:S(2)}) collective-permute-start(f32[48,128]{1,0:T(8,128)S(1)} %get-tuple-element.61), channel_id=1, source_target_pairs={{0,2},{1,3},{2,4},{3,5},{4,6},{5,7},{6,14},{7,15},{14,12},{15,13},... | collective-permute-start | bytes 73736 | tf_op jit(solution)/shard_map/ppermute | solution.py:469
  37.4 3.7 %collective-permute-start.3 = (f32[48,128]{1,0:T(8,128)S(1)}, f32[48,128]{1,0:T(8,128)S(1)}, u32[]{:S(2)}, u32[]{:S(2)}) collective-permute-start(f32[48,128]{1,0:T(8,128)S(1)} %get-tuple-element.62), channel_id=1, source_target_pairs={{0,32},{1,33},{2,0},{3,1},{4,2},{5,3},{6,4},{7,5},{14,6},{15,7},{1... | collective-permute-start | bytes 73736 | tf_op jit(solution)/shard_map/ppermute | solution.py:469
  38.7 2.3 %copy-start.4 = (bf16[640,1280]{1,0:T(8,128)(2,1)S(1)}, bf16[640,1280]{1,0:T(8,128)(2,1)}, u32[]{:S(2)}) copy-start(bf16[640,1280]{1,0:T(8,128)(2,1)} %get-tuple-element.51.b_op) | copy-start | bytes 4915204
  48.9 2.4 %collective-permute-start.6 = (f32[64,128]{1,0:T(8,128)S(1)}, f32[64,128]{1,0:T(8,128)S(1)}, u32[]{:S(2)}, u32[]{:S(2)}) collective-permute-start(f32[64,128]{1,0:T(8,128)S(1)} %get-tuple-element.70), channel_id=1, source_target_pairs={{0,1},{1,0},{2,3},{3,2},{4,5},{5,4},{6,7},{7,6},{14,15},{15,14},{1... | collective-permute-start | bytes 98312 | tf_op jit(solution)/shard_map/ppermute | solution.py:472
  51.3 6.6 %collective-permute-start.9 = (f32[32,128]{1,0:T(8,128)S(1)}, f32[32,128]{1,0:T(8,128)S(1)}, u32[]{:S(2)}, u32[]{:S(2)}) collective-permute-start(f32[32,128]{1,0:T(8,128)S(1)} %get-tuple-element.79), channel_id=1, source_target_pairs={{0,4},{1,5},{2,6},{3,7},{4,14},{5,15},{6,12},{7,13},{14,10},{15,11... | collective-permute-start | bytes 49160 | tf_op jit(solution)/shard_map/ppermute | solution.py:469
  53.2 4.7 %collective-permute-start.10 = (f32[32,128]{1,0:T(8,128)S(1)}, f32[32,128]{1,0:T(8,128)S(1)}, u32[]{:S(2)}, u32[]{:S(2)}) collective-permute-start(f32[32,128]{1,0:T(8,128)S(1)} %get-tuple-element.80), channel_id=1, source_target_pairs={{0,34},{1,35},{2,32},{3,33},{4,0},{5,1},{6,2},{7,3},{14,4},{15,5},... | collective-permute-start | bytes 49160 | tf_op jit(solution)/shard_map/ppermute | solution.py:469
  53.7 4.2 %collective-permute-start.7 = (f32[48,128]{1,0:T(8,128)S(1)}, f32[48,128]{1,0:T(8,128)S(1)}, u32[]{:S(2)}, u32[]{:S(2)}) collective-permute-start(f32[48,128]{1,0:T(8,128)S(1)} %get-tuple-element.77), channel_id=1, source_target_pairs={{0,2},{1,3},{2,4},{3,5},{4,6},{5,7},{6,14},{7,15},{14,12},{15,13},... | collective-permute-start | bytes 73736 | tf_op jit(solution)/shard_map/ppermute | solution.py:469
  54.1 3.8 %collective-permute-start.8 = (f32[48,128]{1,0:T(8,128)S(1)}, f32[48,128]{1,0:T(8,128)S(1)}, u32[]{:S(2)}, u32[]{:S(2)}) collective-permute-start(f32[48,128]{1,0:T(8,128)S(1)} %get-tuple-element.78), channel_id=1, source_target_pairs={{0,32},{1,33},{2,0},{3,1},{4,2},{5,3},{6,4},{7,5},{14,6},{15,7},{1... | collective-permute-start | bytes 73736 | tf_op jit(solution)/shard_map/ppermute | solution.py:469
  57.9 24.4 %copy-start.1 = (s32[256]{0:T(256)S(1)}, s32[256]{0:T(256)}, u32[]{:S(2)}) copy-start(s32[256]{0:T(256)} %param.17) | copy-start | bytes 3076

commit v6 on v5

--- a/solution.py
+++ b/solution.py
@@ -158,11 +158,8 @@
     wanted = target[...]
     half = owner_of(iota((DEVS, DEVS), 0)) * CAP
     slot = jnp.concatenate([half, half], axis=1)
-    total = None
-    for t in range(CAP):
-        part = stage[STRIDE * t + 8 : STRIDE * t + 8 + ROWS, :]
-        term = dot3(part, onehot(slot + t == wanted))
-        total = term if total is None else total + term
+    held = jnp.concatenate([stage[STRIDE * t + 8 : STRIDE * t + 8 + ROWS, :] for t in range(CAP)], axis=1)
+    total = dot3(held, jnp.concatenate([onehot(slot + t == wanted) for t in range(CAP)], axis=0))
     for q in range(QUANT):
         out[q] = total[MODES * q : MODES * (q + 1), :]
 

time: 84 us -> 83.9 us (level)
  no operation moved by 1% of the time
where the time goes in v6:
time: 83.9 us; the launch traced here: 83.6 us
  Pallas kernels  30.1 us (36%)
  starting transfers between devices  23.8 us (28%)
  blocking collectives  21.4 us (26%)
  waiting for transfers between devices  8.12 us (10%)
    pallas_call x12, Pallas kernels, call(): pl.pallas_call(kernel, name=name, out_shape=outs, in_specs=[pl.BlockSpec(...  30.1 us
    all_to_all x1, blocking collectives, exchange(): lax.all_to_all(cube, 'dom', split_axis=0, concat_axis=0, tiled=True)  21.4 us
    all_to_all x1, starting transfers between devices, exchange(): lax.all_to_all(cube, 'dom', split_axis=0, concat_axis=0, tiled=True)  11.5 us
    ppermute x8, starting transfers between devices, move(): return lax.ppermute(part, 'dom', pairs)  8.24 us
    all_to_all x1, waiting for transfers between devices, exchange(): lax.all_to_all(cube, 'dom', split_axis=0, concat_axis=0, tiled=True)  6.38 us
    ppermute x2, starting transfers between devices, swap_ghosts(): twin = lax.ppermute(odd, 'dom', twins)  2.71 us
    ppermute x2, waiting for transfers between devices, swap_ghosts(): twin = lax.ppermute(odd, 'dom', twins)  1.72 us
  transfers between devices with their start and end apart: 12, of which 3 were waited for; matrix products, arithmetic and copies ran while one was open for 0% of the time, Pallas kernels for 12%

profile of v6, /device:TPU:1, one launch (start us, length us, event | category | flops | bytes accessed | tf_op | source)
XLA Modules:
  0.0 83.6 jit_solution(17390624447764874005)
XLA Ops:
  0.0 2.6 %scatter.1 = (f32[1024,128]{1,0:T(8,128)}, s32[16,384]{1,0:T(8,128)}) custom-call(s32[1]{0:T(128)} %bitcast.core, f32[9,35,256]{2,1,0:T(8,128)} %bitcast.23, f32[3,256]{1,0:T(4,128)} %jac.1, f32[4,256]{1,0:T(4,128)} %area.1, s32[1,256]{1,0:T(1,128)} %bitcast.25, s32[1,256]{1,0:T(1,128)} %bitcast.18, s32[4,384]{1,0:T(4,128)} %faces.1, s32[6,1,8]{2,1,0:T(1,128)} %bitcast.24), custom_call_target="tpu_custom_call" | custom-call | flops 100000000 | bytes 338116 | tf_op jit(solution)/shard_map/scatter/pallas_call | solution.py:442
  2.6 11.5 %all-to-all-start = ((f32[128,8,128]{2,1,0:T(8,128)}), f32[128,8,128]{2,1,0:T(8,128)S(1)}, u32[]{:S(2)}, u32[]{:S(2)}) async-start(f32[128,8,128]{2,1,0:T(8,128)} %bitcast.22), calls=%async_computation | async-start | bytes 1048576 | tf_op jit(solution)/shard_map/all_to_all | solution.py:460
  14.1 1.4 %collective-permute-start = (s32[16,384]{1,0:T(8,128)}, s32[16,384]{1,0:T(8,128)S(1)}, u32[]{:S(2)}, u32[]{:S(2)}) collective-permute-start(s32[16,384]{1,0:T(8,128)} %get-tuple-element.45), channel_id=1, source_target_pairs={{0,0},{1,1},{2,2},{3,3},{4,4},{5,5},{6,6},{7,7},{8,14},{9,15},{10,... | collective-permute-start | bytes 73736 | tf_op jit(solution)/shard_map/ppermute | solution.py:519
  15.5 0.0 copy-start.2
  15.5 0.0 copy-start.3
  15.5 4.7 %operators.1 = (bf16[640,2304]{1,0:T(8,128)(2,1)}, bf16[640,1280]{1,0:T(8,128)(2,1)}) custom-call(f32[3,35,35]{2,1,0:T(8,128)} %stiffness.2, f32[35,4,35]{2,1,0:T(4,128)} %bitcast.26, f32[35,4,35]{2,1,0:T(4,128)} %bitcast.27, f32[9,3,9]{2,1,0:T(4,128)} %bitcast.20, f32[9,4,9]{2,1,0:T(4,128)} %bitcast.28, f32[9,4,9]{2,1,0:T(4,128)} %bitcast.29), custom_call_target="tpu_custom_call" | custom-call | flops 1000000000 | bytes 57464 | tf_op jit(solution)/shard_map/operators/pallas_call | solution.py:442
  20.2 0.0 copy-done.2
  20.2 0.0 copy-done.3
  20.2 1.0 %taylor_operators.1.d_op = bf16[640,960]{1,0:T(8,128)(2,1)S(1)} custom-call(f32[3,35,35]{2,1,0:T(8,128)S(1)} %copy-done.2, f32[9,3,9]{2,1,0:T(4,128)S(1)} %bitcast.21), custom_call_target="tpu_custom_call" | custom-call | flops 1000000000 | bytes 15672 | tf_op jit(solution)/shard_map/taylor_operators/pallas_call | solution.py:442
  21.2 0.0 collective-permute-done.tables.faces
  21.2 6.4 %all-to-all-done = f32[128,8,128]{2,1,0:T(8,128)S(1)} async-done(((f32[128,8,128]{2,1,0:T(8,128)}), f32[128,8,128]{2,1,0:T(8,128)S(1)}, u32[]{:S(2)}, u32[]{:S(2)}) %all-to-all-start) | async-done | bytes 524320 | tf_op jit(solution)/shard_map/all_to_all | solution.py:460
  27.6 0.2 unpack.1
  27.8 0.0 copy-start
  27.8 5.1 %start.1 = (f32[320,384]{1,0:T(8,128)S(1)}, f32[320,384]{1,0:T(8,128)S(1)}, f32[64,128]{1,0:T(8,128)S(1)}, f32[64,128]{1,0:T(8,128)S(1)}) custom-call(f32[320,384]{1,0:T(8,128)S(1)} %get-tuple-element.48.state, f32[8,384]{1,0:T(8,128)S(1)} %get-tuple-element.49.extras, s32[8,128]{1,0:T(8,128)S(1)} %get-tuple-element.50.picks, ...), custom_call_target="tpu_custom_call" | custom-call | flops 1000000000 | bytes 2965504 | tf_op jit(solution)/shard_map/start/pallas_call | solution.py:442
  32.9 1.2 %collective-permute-start.1 = (f32[64,128]{1,0:T(8,128)S(1)}, f32[64,128]{1,0:T(8,128)S(1)}, u32[]{:S(2)}, u32[]{:S(2)}) collective-permute-start(f32[64,128]{1,0:T(8,128)S(1)} %get-tuple-element.54), channel_id=1, source_target_pairs={{0,1},{1,0},{2,3},{3,2},{4,5},{5,4},{6,7},{7,6},{14,15},{15,14},{1... | collective-permute-start | bytes 98312 | tf_op jit(solution)/shard_map/ppermute | solution.py:469
  34.0 0.9 %collective-permute-done.1.twin = f32[64,128]{1,0:T(8,128)S(1)} collective-permute-done((f32[64,128]{1,0:T(8,128)S(1)}, f32[64,128]{1,0:T(8,128)S(1)}, u32[]{:S(2)}, u32[]{:S(2)}) %collective-permute-start.1) | collective-permute-done | bytes 32800 | tf_op jit(solution)/shard_map/ppermute | solution.py:469
  34.9 0.4 collective-permute-start.4
  35.3 1.9 %collective-permute-start.5 = (f32[32,128]{1,0:T(8,128)S(1)}, f32[32,128]{1,0:T(8,128)S(1)}, u32[]{:S(2)}, u32[]{:S(2)}) collective-permute-start(f32[32,128]{1,0:T(8,128)S(1)} %get-tuple-element.64), channel_id=1, source_target_pairs={{0,34},{1,35},{2,32},{3,33},{4,0},{5,1},{6,2},{7,3},{14,4},{15,5},... | collective-permute-start | bytes 49160 | tf_op jit(solution)/shard_map/ppermute | solution.py:466
  37.3 0.1 collective-permute-start.2
  37.4 1.4 %collective-permute-start.3 = (f32[48,128]{1,0:T(8,128)S(1)}, f32[48,128]{1,0:T(8,128)S(1)}, u32[]{:S(2)}, u32[]{:S(2)}) collective-permute-start(f32[48,128]{1,0:T(8,128)S(1)} %get-tuple-element.62), channel_id=1, source_target_pairs={{0,32},{1,33},{2,0},{3,1},{4,2},{5,3},{6,4},{7,5},{14,6},{15,7},{1... | collective-permute-start | bytes 73736 | tf_op jit(solution)/shard_map/ppermute | solution.py:466
  38.7 0.0 copy-done
  38.7 0.0 copy-start.4
  38.7 2.3 %local1.1 = (f32[320,384]{1,0:T(8,128)S(1)}, s32[4,384]{1,0:T(4,128)S(1)}) custom-call(f32[320,384]{1,0:T(8,128)S(1)} %get-tuple-element.48.state, f32[320,384]{1,0:T(8,128)S(1)} %get-tuple-element.65.value.first, f32[8,384]{1,0:T(8,128)S(1)} %get-tuple-element.49.extras, bf16[640,2304]{1,0:T(8,128)(2,1)S(1)} %copy-done, ...), custom_call_target="tpu_custom_call" | custom-call | flops 1000000000 | bytes 6918144 | tf_op jit(solution)/shard_map/local1/pallas_call | solution.py:442
  41.0 0.0 collective-permute-done.4.far_up
  41.0 0.0 collective-permute-done.5.far_down
  41.0 0.0 collective-permute-done.2.up
  41.0 0.0 collective-permute-done.3.down
  41.1 0.0 copy-done.4
  41.1 7.8 %middle.1 = (f32[320,384]{1,0:T(8,128)S(1)}, f32[320,384]{1,0:T(8,128)S(1)}, f32[64,128]{1,0:T(8,128)S(1)}, f32[64,128]{1,0:T(8,128)S(1)}) custom-call(s32[1]{0:T(128)} %bitcast.core, f32[64,128]{1,0:T(8,128)S(1)} %collective-permute-done.1.twin, f32[48,128]{1,0:T(8,128)S(1)} %collective-permute-done.2.up, f32[48,128]{1,0:T(8,128)S(1)} %collective-permute-done.3.down, ...), custom_call_target="tpu_custom_call" | custom-call | flops 2000000000 | bytes 7346180 | tf_op jit(solution)/shard_map/middle/pallas_call | solution.py:442
  48.9 1.5 %collective-permute-start.6 = (f32[64,128]{1,0:T(8,128)S(1)}, f32[64,128]{1,0:T(8,128)S(1)}, u32[]{:S(2)}, u32[]{:S(2)}) collective-permute-start(f32[64,128]{1,0:T(8,128)S(1)} %get-tuple-element.70), channel_id=1, source_target_pairs={{0,1},{1,0},{2,3},{3,2},{4,5},{5,4},{6,7},{7,6},{14,15},{15,14},{1... | collective-permute-start | bytes 98312 | tf_op jit(solution)/shard_map/ppermute | solution.py:469
  50.4 0.9 %collective-permute-done.6.twin = f32[64,128]{1,0:T(8,128)S(1)} collective-permute-done((f32[64,128]{1,0:T(8,128)S(1)}, f32[64,128]{1,0:T(8,128)S(1)}, u32[]{:S(2)}, u32[]{:S(2)}) %collective-permute-start.6) | collective-permute-done | bytes 32800 | tf_op jit(solution)/shard_map/ppermute | solution.py:469
  51.3 2.0 %collective-permute-start.9 = (f32[32,128]{1,0:T(8,128)S(1)}, f32[32,128]{1,0:T(8,128)S(1)}, u32[]{:S(2)}, u32[]{:S(2)}) collective-permute-start(f32[32,128]{1,0:T(8,128)S(1)} %get-tuple-element.79), channel_id=1, source_target_pairs={{0,4},{1,5},{2,6},{3,7},{4,14},{5,15},{6,12},{7,13},{14,10},{15,11... | collective-permute-start | bytes 49160 | tf_op jit(solution)/shard_map/ppermute | solution.py:466
  53.2 0.5 collective-permute-start.10
  53.7 0.4 collective-permute-start.7
  54.1 1.6 %collective-permute-start.8 = (f32[48,128]{1,0:T(8,128)S(1)}, f32[48,128]{1,0:T(8,128)S(1)}, u32[]{:S(2)}, u32[]{:S(2)}) collective-permute-start(f32[48,128]{1,0:T(8,128)S(1)} %get-tuple-element.78), channel_id=1, source_target_pairs={{0,32},{1,33},{2,0},{3,1},{4,2},{5,3},{6,4},{7,5},{14,6},{15,7},{1... | collective-permute-start | bytes 73736 | tf_op jit(solution)/shard_map/ppermute | solution.py:466
  55.7 2.2 %local2.1.partial = f32[320,384]{1,0:T(8,128)S(1)} custom-call(f32[320,384]{1,0:T(8,128)S(1)} %get-tuple-element.81.state, f32[320,384]{1,0:T(8,128)S(1)} %get-tuple-element.82.value.second, f32[8,384]{1,0:T(8,128)S(1)} %get-tuple-element.49.extras, bf16[640,2304]{1,0:T(8,128)(2,1)S(1)} %copy-done), custom_call_target="tpu_custom_call" | custom-call | flops 1000000000 | bytes 6893568 | tf_op jit(solution)/shard_map/local2/pallas_call | solution.py:442
  57.9 0.0 copy-start.1
  57.9 0.0 collective-permute-done.9.far_up
  57.9 0.0 collective-permute-done.10.far_down
  57.9 0.0 collective-permute-done.7.up
  57.9 0.0 collective-permute-done.8.down
  57.9 2.9 %final.1 = f32[1024,128]{1,0:T(8,128)S(1)} custom-call(s32[1]{0:T(128)} %bitcast.core, f32[64,128]{1,0:T(8,128)S(1)} %collective-permute-done.6.twin, f32[48,128]{1,0:T(8,128)S(1)} %collective-permute-done.7.up, f32[48,128]{1,0:T(8,128)S(1)} %collective-permute-done.8.down, f32[32,128]{1,0:T(8,128)S(1)} %collective-permute-done.9.far_up, ...), custom_call_target="tpu_custom_call" | custom-call | flops 1000000000 | bytes 4392964 | tf_op jit(solution)/shard_map/final/pallas_call | solution.py:442
  60.9 21.4 %all_to_all.10 = f32[128,8,128]{2,1,0:T(8,128)S(1)} all-to-all(f32[128,8,128]{2,1,0:T(8,128)S(1)} %bitcast.17), channel_id=1, replica_groups=mesh['dom'=128] {'dom'}, dimensions={0} | all-to-all | bytes 1048576 | tf_op jit(solution)/shard_map/all_to_all | solution.py:460
  82.3 0.0 copy-done.1
  82.3 1.3 %gather.1 = f32[9,35,256]{2,1,0:T(8,128)} custom-call(f32[1024,128]{1,0:T(8,128)S(1)} %bitcast.16, s32[1,256]{1,0:T(1,128)S(1)} %bitcast.19), custom_call_target="tpu_custom_call" | custom-call | flops 100000000 | bytes 525312 | tf_op jit(solution)/shard_map/gather/pallas_call | solution.py:442
  (2 shorter events, 0.0 us)
Async XLA Ops:
  2.6 25.0 %all-to-all-start = ((f32[128,8,128]{2,1,0:T(8,128)}), f32[128,8,128]{2,1,0:T(8,128)S(1)}, u32[]{:S(2)}, u32[]{:S(2)}) async-start(f32[128,8,128]{2,1,0:T(8,128)} %bitcast.22), calls=%async_computation | async-start | bytes 1048576 | tf_op jit(solution)/shard_map/all_to_all | solution.py:460
  14.1 7.1 %collective-permute-start = (s32[16,384]{1,0:T(8,128)}, s32[16,384]{1,0:T(8,128)S(1)}, u32[]{:S(2)}, u32[]{:S(2)}) collective-permute-start(s32[16,384]{1,0:T(8,128)} %get-tuple-element.45), channel_id=1, source_target_pairs={{0,0},{1,1},{2,2},{3,3},{4,4},{5,5},{6,6},{7,7},{8,14},{9,15},{10,... | collective-permute-start | bytes 73736 | tf_op jit(solution)/shard_map/ppermute | solution.py:519
  15.5 4.7 %copy-start.2 = (f32[3,35,35]{2,1,0:T(8,128)S(1)}, f32[3,35,35]{2,1,0:T(8,128)}, u32[]{:S(2)}) copy-start(f32[3,35,35]{2,1,0:T(8,128)} %stiffness.2) | copy-start | bytes 44104
  15.5 4.7 %copy-start.3 = (f32[3,9,9]{2,0,1:T(4,128)S(1)}, f32[3,9,9]{2,0,1:T(4,128)}, u32[]{:S(2)}) copy-start(f32[3,9,9]{2,0,1:T(4,128)} %param.21) | copy-start | bytes 2920
  27.8 11.0 %copy-start = (bf16[640,2304]{1,0:T(8,128)(2,1)S(1)}, bf16[640,2304]{1,0:T(8,128)(2,1)}, u32[]{:S(2)}) copy-start(bf16[640,2304]{1,0:T(8,128)(2,1)} %get-tuple-element.66.c_op) | copy-start | bytes 8847364
  32.9 2.0 %collective-permute-start.1 = (f32[64,128]{1,0:T(8,128)S(1)}, f32[64,128]{1,0:T(8,128)S(1)}, u32[]{:S(2)}, u32[]{:S(2)}) collective-permute-start(f32[64,128]{1,0:T(8,128)S(1)} %get-tuple-element.54), channel_id=1, source_target_pairs={{0,1},{1,0},{2,3},{3,2},{4,5},{5,4},{6,7},{7,6},{14,15},{15,14},{1... | collective-permute-start | bytes 98312 | tf_op jit(solution)/shard_map/ppermute | solution.py:469
  34.9 6.1 %collective-permute-start.4 = (f32[32,128]{1,0:T(8,128)S(1)}, f32[32,128]{1,0:T(8,128)S(1)}, u32[]{:S(2)}, u32[]{:S(2)}) collective-permute-start(f32[32,128]{1,0:T(8,128)S(1)} %get-tuple-element.63), channel_id=1, source_target_pairs={{0,4},{1,5},{2,6},{3,7},{4,14},{5,15},{6,12},{7,13},{14,10},{15,11... | collective-permute-start | bytes 49160 | tf_op jit(solution)/shard_map/ppermute | solution.py:466
  35.3 5.7 %collective-permute-start.5 = (f32[32,128]{1,0:T(8,128)S(1)}, f32[32,128]{1,0:T(8,128)S(1)}, u32[]{:S(2)}, u32[]{:S(2)}) collective-permute-start(f32[32,128]{1,0:T(8,128)S(1)} %get-tuple-element.64), channel_id=1, source_target_pairs={{0,34},{1,35},{2,32},{3,33},{4,0},{5,1},{6,2},{7,3},{14,4},{15,5},... | collective-permute-start | bytes 49160 | tf_op jit(solution)/shard_map/ppermute | solution.py:466
  37.3 3.8 %collective-permute-start.2 = (f32[48,128]{1,0:T(8,128)S(1)}, f32[48,128]{1,0:T(8,128)S(1)}, u32[]{:S(2)}, u32[]{:S(2)}) collective-permute-start(f32[48,128]{1,0:T(8,128)S(1)} %get-tuple-element.61), channel_id=1, source_target_pairs={{0,2},{1,3},{2,4},{3,5},{4,6},{5,7},{6,14},{7,15},{14,12},{15,13},... | collective-permute-start | bytes 73736 | tf_op jit(solution)/shard_map/ppermute | solution.py:466
  37.4 3.7 %collective-permute-start.3 = (f32[48,128]{1,0:T(8,128)S(1)}, f32[48,128]{1,0:T(8,128)S(1)}, u32[]{:S(2)}, u32[]{:S(2)}) collective-permute-start(f32[48,128]{1,0:T(8,128)S(1)} %get-tuple-element.62), channel_id=1, source_target_pairs={{0,32},{1,33},{2,0},{3,1},{4,2},{5,3},{6,4},{7,5},{14,6},{15,7},{1... | collective-permute-start | bytes 73736 | tf_op jit(solution)/shard_map/ppermute | solution.py:466
  38.7 2.3 %copy-start.4 = (bf16[640,1280]{1,0:T(8,128)(2,1)S(1)}, bf16[640,1280]{1,0:T(8,128)(2,1)}, u32[]{:S(2)}) copy-start(bf16[640,1280]{1,0:T(8,128)(2,1)} %get-tuple-element.51.b_op) | copy-start | bytes 4915204
  48.9 2.4 %collective-permute-start.6 = (f32[64,128]{1,0:T(8,128)S(1)}, f32[64,128]{1,0:T(8,128)S(1)}, u32[]{:S(2)}, u32[]{:S(2)}) collective-permute-start(f32[64,128]{1,0:T(8,128)S(1)} %get-tuple-element.70), channel_id=1, source_target_pairs={{0,1},{1,0},{2,3},{3,2},{4,5},{5,4},{6,7},{7,6},{14,15},{15,14},{1... | collective-permute-start | bytes 98312 | tf_op jit(solution)/shard_map/ppermute | solution.py:469
  51.3 6.6 %collective-permute-start.9 = (f32[32,128]{1,0:T(8,128)S(1)}, f32[32,128]{1,0:T(8,128)S(1)}, u32[]{:S(2)}, u32[]{:S(2)}) collective-permute-start(f32[32,128]{1,0:T(8,128)S(1)} %get-tuple-element.79), channel_id=1, source_target_pairs={{0,4},{1,5},{2,6},{3,7},{4,14},{5,15},{6,12},{7,13},{14,10},{15,11... | collective-permute-start | bytes 49160 | tf_op jit(solution)/shard_map/ppermute | solution.py:466
  53.2 4.7 %collective-permute-start.10 = (f32[32,128]{1,0:T(8,128)S(1)}, f32[32,128]{1,0:T(8,128)S(1)}, u32[]{:S(2)}, u32[]{:S(2)}) collective-permute-start(f32[32,128]{1,0:T(8,128)S(1)} %get-tuple-element.80), channel_id=1, source_target_pairs={{0,34},{1,35},{2,32},{3,33},{4,0},{5,1},{6,2},{7,3},{14,4},{15,5},... | collective-permute-start | bytes 49160 | tf_op jit(solution)/shard_map/ppermute | solution.py:466
  53.7 4.2 %collective-permute-start.7 = (f32[48,128]{1,0:T(8,128)S(1)}, f32[48,128]{1,0:T(8,128)S(1)}, u32[]{:S(2)}, u32[]{:S(2)}) collective-permute-start(f32[48,128]{1,0:T(8,128)S(1)} %get-tuple-element.77), channel_id=1, source_target_pairs={{0,2},{1,3},{2,4},{3,5},{4,6},{5,7},{6,14},{7,15},{14,12},{15,13},... | collective-permute-start | bytes 73736 | tf_op jit(solution)/shard_map/ppermute | solution.py:466
  54.1 3.8 %collective-permute-start.8 = (f32[48,128]{1,0:T(8,128)S(1)}, f32[48,128]{1,0:T(8,128)S(1)}, u32[]{:S(2)}, u32[]{:S(2)}) collective-permute-start(f32[48,128]{1,0:T(8,128)S(1)} %get-tuple-element.78), channel_id=1, source_target_pairs={{0,32},{1,33},{2,0},{3,1},{4,2},{5,3},{6,4},{7,5},{14,6},{15,7},{1... | collective-permute-start | bytes 73736 | tf_op jit(solution)/shard_map/ppermute | solution.py:466
  57.9 24.4 %copy-start.1 = (s32[256]{0:T(256)S(1)}, s32[256]{0:T(256)}, u32[]{:S(2)}) copy-start(s32[256]{0:T(256)} %param.17) | copy-start | bytes 3076
